TPU v7x, 32 devices: a whole 2x2x4 slice. The times are simulated.
32 devices in a mesh: group: 2 (over x), feat: 16 (over z, y, core).
Axes of the slice: x: 2, y: 2, z: 4, core: 2. Of those that a mesh axis runs over, the one named last changes fastest.
Arguments:
- store_inputs: bfloat16 [2, 512, 2048], P(None, ('group', 'feat')), parts along dimension 1, may hold values from -6 to 6
- store_targets: bfloat16 [2, 512, 2048], P(None, ('group', 'feat')), parts along dimension 1, may hold values from -6 to 6
- row_ids: int32 [256], P(('group', 'feat')), parts along dimension 0, may hold values from 0 to 15
- enc_weight: bfloat16 [2, 2048, 16384], P(None, None, 'feat'), may hold values from -0.125 to 0.125
- enc_bias: float32 [2, 16384], P(None, 'feat'), may hold values from -3 to 3
- dec_weight: bfloat16 [3, 16384, 2048], P(None, 'feat'), may hold values from -0.046875 to 0.046875
Outputs:
- enc_grad: bfloat16 [4, 2048, 16384], P('group', None, 'feat'), parts along dimension 0
- bias_grad: float32 [4, 16384], P('group', 'feat'), parts along dimension 0
- dec_grad: bfloat16 [6, 16384, 2048], P('group', 'feat'), parts along dimension 0
There are 2 independent parts, one for each index of `group`. A program takes and returns all parts, laid end to end along the dimension named above; an argument that names none is the same for every part. Nothing has to cross between parts.
Inputs may be any that keep to these rules, and one draw needn't show every extreme that they name: row_ids[i] indexes the store rows held with token i, as in the first step.
All inputs are finite; a program needn't handle non-finite values.
Results may differ from a plain program's by a relative error of at most 0.035.
Values may be sent and summed in bfloat16 or wider, within the bound.
No kernel may reach another device: no remote copies, remote signals or barrier semaphores. Data moves between devices by JAX's collectives and lax.ppermute only.
A program may use at most 128 MiB of HBM per device.

v0:
```python
import math

import jax
import jax.numpy as jnp
from jax import lax
from jax.sharding import PartitionSpec as P


def local(store_inputs, store_targets, row_ids, enc_weight, enc_bias, dec_weight):
    layers = enc_weight.shape[0]
    model_width = enc_weight.shape[1]
    tile_width = enc_weight.shape[2]
    local_rows = row_ids.shape[0]
    pair_list = [(source, target) for source in range(layers) for target in range(source, layers)]
    picked_in = (
        jnp.take(store_inputs, row_ids, axis=1)
        .transpose(1, 0, 2)
        .reshape(local_rows, layers * model_width)
    )
    picked_out = (
        jnp.take(store_targets, row_ids, axis=1)
        .transpose(1, 0, 2)
        .reshape(local_rows, layers * model_width)
    )
    inputs_all = lax.all_gather(picked_in, "feat", axis=0, tiled=True)
    tokens = inputs_all.shape[0]
    grad_scale = 1.0 / math.sqrt(tokens)
    layer_inputs = [
        inputs_all[:, index * model_width : (index + 1) * model_width] for index in range(layers)
    ]
    preact = [
        jnp.dot(layer_inputs[index], enc_weight[index], preferred_element_type=jnp.float32)
        + enc_bias[index]
        for index in range(layers)
    ]
    features = [jnp.maximum(value, 0.0).astype(jnp.bfloat16) for value in preact]

    def decoder_terms():
        part_features = [value for value in features]
        outputs = []
        for target in range(layers):
            rebuilt = jnp.zeros((local_rows * lax.axis_size("feat"), model_width), jnp.float32)
            for index, (source, goal) in enumerate(pair_list):
                if goal == target:
                    rebuilt = rebuilt + jnp.dot(
                        part_features[source], dec_weight[index], preferred_element_type=jnp.float32
                    )
            outputs.append(rebuilt)
        return jnp.concatenate(outputs, axis=1)

    def backward_step(block_rows):
        row_count = block_rows.shape[0]
        part_features = [value for value in features]
        part_preact = [value for value in preact]
        part_errors = [
            block_rows[:, index * model_width : (index + 1) * model_width]
            for index in range(layers)
        ]
        feature_grad = [jnp.zeros((row_count, tile_width), jnp.float32) for index in range(layers)]
        updated = []
        for index, (source, target) in enumerate(pair_list):
            product = lax.dot_general(
                part_features[source],
                part_errors[target],
                (((0,), (0,)), ((), ())),
                preferred_element_type=jnp.float32,
            )
            updated.append(product)
            feature_grad[source] = feature_grad[source] + lax.dot_general(
                part_errors[target],
                dec_weight[index],
                (((1,), (1,)), ((), ())),
                preferred_element_type=jnp.float32,
            )
        pre_rows = jnp.stack(
            [
                jnp.where(part_preact[index] > 0, feature_grad[index], 0.0) * grad_scale
                for index in range(layers)
            ]
        )
        return (tuple(updated), pre_rows)

    rebuilt_own = lax.psum_scatter(decoder_terms(), "feat", scatter_dimension=0, tiled=True)
    errors_own = (rebuilt_own - picked_out.astype(jnp.float32)).astype(jnp.bfloat16)
    gradients, pre_buffer = backward_step(lax.all_gather(errors_own, "feat", axis=0, tiled=True))
    dec_grad = jnp.stack([(grad_scale * value).astype(jnp.bfloat16) for value in gradients])
    bias_grad = jnp.sum(pre_buffer, axis=1)
    pre_half = pre_buffer.astype(jnp.bfloat16)
    enc_grad = jnp.stack(
        [
            lax.dot_general(
                layer_inputs[index],
                pre_half[index],
                (((0,), (0,)), ((), ())),
                preferred_element_type=jnp.float32,
            ).astype(jnp.bfloat16)
            for index in range(layers)
        ]
    )
    return (enc_grad, bias_grad, dec_grad)


def solution(mesh):
    in_specs = (
        P(None, ("group", "feat"), None),
        P(None, ("group", "feat"), None),
        P(("group", "feat")),
        P(None, None, "feat"),
        P(None, "feat"),
        P(None, "feat", None),
    )
    out_specs = (P("group", None, "feat"), P("group", "feat"), P("group", "feat", None))
    return jax.shard_map(local, mesh=mesh, in_specs=in_specs, out_specs=out_specs, check_vma=False)
```

profile of v0, /device:TPU:0, one launch (start us, length us, event | category | flops | bytes accessed | tf_op | source)
XLA Modules:
  0.0 205.0 jit_solution(16663511972218497202)
XLA Ops:
  7.2 0.0 copy-start
  7.2 0.0 all-gather.3.cloned.1.call-start
  7.2 0.7 compare_select_fusion
  7.9 0.7 compare_and_fusion
  8.6 0.0 copy-done
  8.6 0.7 gather_fusion
  9.3 1.6 gather_fusion.1
  11.0 0.7 bitcast_convert_fusion
  11.7 0.0 all-gather.3.cloned.1.call-update
  11.7 0.0 reduce-scatter.2.cloned.1.call-start
  11.8 0.8 fusion.71
  12.6 39.9 %all-gather.3.cloned.1.call-done = bf16[128,4096]{1,0:T(8,128)(2,1)} async-done(((bf16[8,4096]{1,0:T(8,128)(2,1)}), bf16[128,4096]{1,0:T(8,128)(2,1)}) %all-gather.3.cloned.1.call-update) | async-done | bytes 1048592 | tf_op jit(solution)/shard_map/all_gather | solution.py:25
  52.5 0.0 copy-start.2
  52.5 0.0 copy-start.3
  52.5 3.2 %fusion.36 = f32[128,1024]{1,0:T(8,128)S(1)} fusion(bf16[2,2048,1024]{2,1,0:T(8,128)(2,1)} %param.11, bf16[128,4096]{1,0:T(8,128)(2,1)} %all-gather.3.cloned.1.call-done, f32[1024]{0:T(1024)S(1)} %bitcast.81), kind=kOutput, calls=%fused_computation.40 | convolution fusion | flops 537001984 | bytes 5246976 | tf_op jit(solution)/shard_map/dot_general | solution.py:32
  55.7 3.7 %fusion.2 = f32[128,2048]{1,0:T(8,128)S(1)} fusion(bf16[3,1024,2048]{2,1,0:T(8,128)(2,1)} %param.13, f32[128,1024]{1,0:T(8,128)S(1)} %fusion.36), kind=kOutput, calls=%fused_computation.9 | convolution fusion | flops 537133056 | bytes 5767168 | tf_op jit(solution)/shard_map/dot_general | solution.py:45
  59.4 0.0 copy-done.2
  59.4 2.9 %maximum_convert_fusion.1 = (bf16[128,1024]{1,0:T(8,128)(2,1)S(1)}, f32[128,1024]{1,0:T(8,128)S(1)}) fusion(f32[1024]{0:T(1024)S(1)} %bitcast.80, bf16[2,2048,1024]{2,1,0:T(8,128)(2,1)} %param.11, bf16[128,4096]{1,0:T(8,128)(2,1)S(1)} %copy-done.2), kind=kOutput, calls=%fused_computation.51 | convolution fusion | flops 537264128 | bytes 5509120 | tf_op jit(solution)/shard_map/dot_general | solution.py:32
  62.3 0.0 copy-done.3
  62.3 0.7 fusion.12
  63.0 0.8 fusion.27
  63.8 1.5 pad_maximum_fusion.2
  65.3 0.0 reduce-scatter.2.cloned.1.call-update
  65.3 0.2 all-gather.5.cloned.1.call-start
  65.5 60.7 %reduce-scatter.2.cloned.1.call-done = f32[8,4096]{1,0:T(8,128)} async-done(((f32[128,4096]{1,0:T(8,128)}), f32[8,4096]{1,0:T(8,128)}) %reduce-scatter.2.cloned.1.call-update) | async-done | bytes 131088 | tf_op jit(solution)/shard_map/reduce_scatter | solution.py:83
  126.2 1.5 subtract_convert_fusion
  127.8 0.0 all-gather.5.cloned.1.call-update
  127.8 38.0 %all-gather.5.cloned.1.call-done = bf16[128,4096]{1,0:T(8,128)(2,1)} async-done(((bf16[8,4096]{1,0:T(8,128)(2,1)}), bf16[128,4096]{1,0:T(8,128)(2,1)}) %all-gather.5.cloned.1.call-update) | async-done | bytes 1048592 | tf_op jit(solution)/shard_map/all_gather | solution.py:85
  165.8 0.0 copy-start.4
  165.8 3.9 %fusion.6 = f32[128,1024]{1,0:T(8,128)S(1)} fusion(bf16[3,1024,2048]{2,1,0:T(8,128)(2,1)} %param.13, bf16[128,4096]{1,0:T(8,128)(2,1)} %all-gather.5.cloned.1.call-done), kind=kOutput, calls=%fused_computation.13 | convolution fusion | flops 536870912 | bytes 5242880 | tf_op jit(solution)/shard_map/dot_general | solution.py:69
  169.8 3.9 %fusion.54 = f32[1,128,1024]{2,1,0:T(8,128)S(1)} fusion(bf16[3,1024,2048]{2,1,0:T(8,128)(2,1)} %param.13, f32[128,1024]{1,0:T(8,128)S(1)} %fusion.36, bf16[128,4096]{1,0:T(8,128)(2,1)} %all-gather.5.cloned.1.call-done), kind=kOutput, calls=%fused_computation.46 | convolution fusion | flops 537264128 | bytes 5767168 | tf_op jit(solution)/shard_map/dot_general | solution.py:69
  173.7 0.0 copy-done.4
  173.7 3.8 %fusion.45 = f32[1,128,1024]{2,1,0:T(8,128)S(1)} fusion(f32[128,1024]{1,0:T(8,128)S(1)} %fusion.6, bf16[3,1024,2048]{2,1,0:T(8,128)(2,1)} %param.13, f32[128,1024]{1,0:T(8,128)S(1)} %get-tuple-element.9, bf16[128,4096]{1,0:T(8,128)(2,1)S(1)} %copy-done.4), kind=kOutput, calls=%fused_computation.43 | convolution fusion | flops 537395200 | bytes 6291456 | tf_op jit(solution)/shard_map/dot_general | solution.py:69
  177.5 0.1 fusion.58
  177.5 0.7 fusion.57
  178.2 1.3 convert_bitcast_fusion.1
  179.5 3.3 %convert_bitcast_fusion = bf16[1,2048,1024]{2,1,0:T(8,128)(2,1)} fusion(bf16[128,4096]{1,0:T(8,128)(2,1)S(1)} %copy-done.2, bf16[2,128,1024]{2,1,0:T(8,128)(2,1)S(1)} %fusion.58), kind=kOutput, calls=%fused_computation.23 | convolution fusion | flops 538968064 | bytes 4980736 | tf_op jit(solution)/shard_map/dot_general | solution.py:91
  182.8 0.0 copy-start.5
  182.8 6.4 %pad_maximum_fusion.1 = bf16[2,2048,1024]{2,1,0:T(8,128)(2,1)} fusion(bf16[1,2048,1024]{2,1,0:T(8,128)(2,1)} %convert_bitcast_fusion, bf16[1,2048,1024]{2,1,0:T(8,128)(2,1)S(1)} %convert_bitcast_fusion.1), kind=kLoop, calls=%fused_computation.3 | loop fusion | flops 4194304 | bytes 16777216 | tf_op jit(solution)/shard_map/stack | solution.py:89
  189.2 0.0 copy-done.5
  189.2 1.3 fusion.24
  190.5 1.3 fusion.25
  191.8 0.0 copy-start.1
  191.8 1.3 fusion.26
  193.1 5.4 %pad_maximum_fusion = bf16[3,1024,2048]{2,1,0:T(8,128)(2,1)} fusion(bf16[1,1024,2048]{2,1,0:T(8,128)(2,1)S(1)} %fusion.26, bf16[1,1024,2048]{2,1,0:T(8,128)(2,1)S(1)} %fusion.25, bf16[1,1024,2048]{2,1,0:T(8,128)(2,1)S(1)} %fusion.24), kind=kLoop, calls=%fused_computation.2 | loop fusion | flops 12582912 | bytes 25165824 | tf_op jit(solution)/shard_map/stack | solution.py:86
  198.4 0.0 copy-done.1
  (1 shorter events, 0.0 us)
Async XLA Ops:
  7.2 1.4 copy-start
  7.2 45.3 %all-gather.3.cloned.1.call-start = ((), (), s32[]{:S(2)}) async-start(), calls=%async_computation.1 | async-start | bytes 1114112 | tf_op jit(solution)/shard_map/all_gather | solution.py:25
  11.7 114.5 %reduce-scatter.2.cloned.1.call-start = ((), (), s32[]{:S(2)}) async-start(), calls=%async_computation.2 | async-start | bytes 2228224 | tf_op jit(solution)/shard_map/reduce_scatter | solution.py:83
  52.5 6.9 %copy-start.2 = (bf16[128,4096]{1,0:T(8,128)(2,1)S(1)}, bf16[128,4096]{1,0:T(8,128)(2,1)}, u32[]{:S(2)}) copy-start(bf16[128,4096]{1,0:T(8,128)(2,1)} %all-gather.3.cloned.1.call-done) | copy-start | bytes 3145732
  52.5 9.8 %copy-start.3 = (bf16[3,1024,2048]{2,1,0:T(8,128)(2,1)S(1)}, bf16[3,1024,2048]{2,1,0:T(8,128)(2,1)}, u32[]{:S(2)}) copy-start(bf16[3,1024,2048]{2,1,0:T(8,128)(2,1)} %param.13) | copy-start | bytes 37748740
  65.3 100.5 %all-gather.5.cloned.1.call-start = ((), (), s32[]{:S(2)}) async-start(), calls=%async_computation.3 | async-start | bytes 1114112 | tf_op jit(solution)/shard_map/all_gather | solution.py:85
  165.8 7.9 %copy-start.4 = (bf16[128,4096]{1,0:T(8,128)(2,1)S(1)}, bf16[128,4096]{1,0:T(8,128)(2,1)}, u32[]{:S(2)}) copy-start(bf16[128,4096]{1,0:T(8,128)(2,1)} %all-gather.5.cloned.1.call-done) | copy-start | bytes 3145732
  182.8 6.4 %copy-start.5 = (bf16[128,4096]{1,0:T(8,128)(2,1)S(1)}, bf16[128,4096]{1,0:T(8,128)(2,1)}, u32[]{:S(2)}) copy-start(bf16[128,4096]{1,0:T(8,128)(2,1)} %all-gather.5.cloned.1.call-done) | copy-start | bytes 3145732
  191.8 6.7 %copy-start.1 = (bf16[2,16,2048]{2,1,0:T(8,128)(2,1)S(1)}, bf16[2,16,2048]{2,1,0:T(8,128)(2,1)}, u32[]{:S(2)}) copy-start(bf16[2,16,2048]{2,1,0:T(8,128)(2,1)} %param.8) | copy-start | bytes 393220
Sparse Core Ops, SparseCore 0:
  11.9 40.5 all-gather.2
  65.4 60.7 reduce-scatter.1
  129.0 36.7 all-gather.4
where the time goes:
time: 205 us
  waiting for transfers between devices  139 us (68%)
  matrix products  31.2 us (15%)
  other arithmetic  17.6 us (9%)
  between operations  13.9 us (7%)
  local copies, waits for them, and re-layouts  3.21 us (2%)
    reduce_scatter x1, waiting for transfers between devices, local(): lax.psum_scatter(decoder_terms(), 'feat', scatter_dimension=0, tiled=True)  60.7 us
    all_gather x1, waiting for transfers between devices, local(): inputs_all = lax.all_gather(picked_in, 'feat', axis=0, tiled=True)  39.9 us
    all_gather x1, waiting for transfers between devices, local(): lax.all_gather(errors_own, 'feat', axis=0, tiled=True)  38 us
    dot_general x3, matrix products, backward_step(): lax.dot_general(part_errors[target], dec_weight[index], (((1,), (1,)), ((...  11.6 us
    another operation x1, other arithmetic, local(): jnp.stack([lax.dot_general(layer_inputs[index], pre_half[index], (((0,),...  6.44 us
    dot_general x2, matrix products, local(): jnp.dot(layer_inputs[index], enc_weight[index], preferred_element_type=jn...  6.12 us
    another operation x1, other arithmetic, local(): jnp.stack([(grad_scale * value).astype(jnp.bfloat16) for value in gradien...  5.38 us
    dot_general x3, matrix products, decoder_terms(): jnp.dot(part_features[source], dec_weight[index], preferred_element_type=...  5.14 us
  transfers between devices with their start and end apart: 3, of which 3 were waited for; matrix products, arithmetic and copies ran while one was open for 0% of the time, Pallas kernels for 0%

commit v1 on v0

v1 whole, which is shorter than its diff:
```python
import math

import jax
import jax.numpy as jnp
from jax import lax
from jax.sharding import PartitionSpec as P


def swap(value, mask, size):
    return lax.ppermute(value, "feat", [(index, index ^ mask) for index in range(size)])


def gather_rows(own, size):
    if size == 1:
        return own
    rows = own.shape[0]
    slots = {0: own}
    far = [4 * step for step in range(1, size // 4)]
    for mask in far[::-1]:
        slots[mask] = swap(own, mask, size)
    if size > 2:
        slots[2] = swap(own, 2, size)
        if far:
            block = swap(jnp.concatenate([slots[mask] for mask in far], axis=0), 2, size)
            for index, mask in enumerate(far):
                slots[mask + 2] = block[index * rows : (index + 1) * rows]
    even = jnp.concatenate([slots[mask] for mask in range(0, size, 2)], axis=0)
    odd = swap(even, 1, size)
    return even, odd


def scatter_sums(parts, size):
    got = swap(parts[:, 1], 1, size)
    pair = (parts[:, 0].astype(jnp.float32) + got.astype(jnp.float32)).astype(jnp.bfloat16)
    total = pair[0].astype(jnp.float32)
    for slot in range(1, size // 2):
        total = total + swap(pair[slot], 2 * slot, size).astype(jnp.float32)
    return total


def local(store_inputs, store_targets, row_ids, enc_weight, enc_bias, dec_weight):
    size = lax.axis_size("feat")
    layers, width, tile = enc_weight.shape
    rows = row_ids.shape[0]
    pairs = [(source, target) for source in range(layers) for target in range(source, layers)]
    tokens = rows * size
    grad_scale = 1.0 / math.sqrt(tokens)

    picked_in = jnp.take(store_inputs, row_ids, axis=1).transpose(1, 0, 2).reshape(rows, layers * width)
    picked_out = jnp.take(store_targets, row_ids, axis=1).transpose(1, 0, 2).reshape(rows, layers * width)

    even, odd = gather_rows(picked_in, size)
    inputs = jnp.concatenate([even, odd], axis=0).reshape(tokens, layers, width).transpose(1, 0, 2)
    preact = [
        jnp.dot(inputs[layer], enc_weight[layer], preferred_element_type=jnp.float32) + enc_bias[layer]
        for layer in range(layers)
    ]
    features = [jnp.maximum(value, 0.0).astype(jnp.bfloat16) for value in preact]
    rebuilt = []
    for target in range(layers):
        total = jnp.zeros((tokens, width), jnp.float32)
        for index, (source, goal) in enumerate(pairs):
            if goal == target:
                total = total + jnp.dot(
                    features[source], dec_weight[index], preferred_element_type=jnp.float32
                )
        rebuilt.append(total.astype(jnp.bfloat16))
    parts = jnp.concatenate(rebuilt, axis=1).reshape(2, size // 2, rows, layers * width)
    own = scatter_sums(parts.transpose(1, 0, 2, 3), size)
    errors_own = (own - picked_out.astype(jnp.float32)).astype(jnp.bfloat16)
    even, odd = gather_rows(errors_own, size)
    errors = jnp.concatenate([even, odd], axis=0).reshape(tokens, layers, width).transpose(1, 0, 2)

    pair_features = jnp.stack([features[source] for source, _ in pairs])
    pair_errors = jnp.stack([errors[target] for _, target in pairs])
    dec_grad = (
        grad_scale
        * jnp.einsum("pbf,pbd->pfd", pair_features, pair_errors, preferred_element_type=jnp.float32)
    ).astype(jnp.bfloat16)
    feature_grad = [jnp.zeros((tokens, tile), jnp.float32) for _ in range(layers)]
    for index, (source, target) in enumerate(pairs):
        feature_grad[source] = feature_grad[source] + lax.dot_general(
            errors[target], dec_weight[index], (((1,), (1,)), ((), ())), preferred_element_type=jnp.float32
        )
    pre_grad = jnp.stack(
        [jnp.where(preact[layer] > 0, feature_grad[layer], 0.0) * grad_scale for layer in range(layers)]
    )
    bias_grad = jnp.sum(pre_grad, axis=1)
    enc_grad = jnp.einsum(
        "lbd,lbf->ldf", inputs, pre_grad.astype(jnp.bfloat16), preferred_element_type=jnp.float32
    ).astype(jnp.bfloat16)
    return (enc_grad, bias_grad, dec_grad)


def solution(mesh):
    in_specs = (
        P(None, ("group", "feat"), None),
        P(None, ("group", "feat"), None),
        P(("group", "feat")),
        P(None, None, "feat"),
        P(None, "feat"),
        P(None, "feat", None),
    )
    out_specs = (P("group", None, "feat"), P("group", "feat"), P("group", "feat", None))
    return jax.shard_map(local, mesh=mesh, in_specs=in_specs, out_specs=out_specs, check_vma=False)
```

time: 205 us -> 123 us (0.60)
  waiting for transfers between devices: 139 us -> 20.8 us
  starting transfers between devices: 0.3 us -> 27.9 us
  local copies, waits for them, and re-layouts: 3.21 us -> 29.7 us
  other arithmetic: 17.6 us -> 3.85 us
  between operations: 13.9 us -> 0.96 us
  matrix products: 31.2 us -> 38.7 us
    all_gather x2 -> x0, waiting for transfers between devices: 77.9 us -> none  [the longest x1 39.9 us: local(): inputs_all = lax.all_gather(picked_in, 'feat', axis=0, tiled=True)]
    reduce_scatter x1 -> x0, waiting for transfers between devices: 60.7 us -> none  [local(): lax.psum_scatter(decoder_terms(), 'feat', scatter_dimension=0, tiled=True)]
    ppermute x0 -> x20, starting transfers between devices: none -> 27.9 us  [swap(): lax.ppermute(value, 'feat', [(index, index ^ mask) for index in range(siz...]
    ppermute x0 -> x20, waiting for transfers between devices: none -> 20.8 us  [swap(): lax.ppermute(value, 'feat', [(index, index ^ mask) for index in range(siz...]
    concatenate x0 -> x5, local copies, waits for them, and re-layouts: none -> 11.1 us  [the longest x3 10.5 us: local(): jnp.concatenate([even, odd], axis=0).reshape(tokens, layers, width)]
    another operation x2 -> x1, other arithmetic: 11.8 us -> 0.77 us  [local(): pair_features = jnp.stack([features[source] for source, _ in pairs])]
    dot_general x13 -> x10, matrix products: 31.2 us -> 38.7 us  [the longest x3 11.4 us: local(): lax.dot_general(errors[target], dec_weight[index], (((1,), (1,)), ((), ()...]
    ppermute x0 -> x5, local copies, waits for them, and re-layouts: none -> 5.79 us  [swap(): lax.ppermute(value, 'feat', [(index, index ^ mask) for index in range(siz...]
  transfers between devices with their start and end apart: 3 -> 20, of which waited for: 3 -> 10; matrix products, arithmetic and copies ran while one was open for 0% -> 10% of each run, Pallas kernels for 0% -> 0%
where the time goes in v1:
time: 123 us; the launch traced here: 122 us
  matrix products  38.7 us (31%)
  local copies, waits for them, and re-layouts  29.7 us (24%)
  starting transfers between devices  27.9 us (23%)
  waiting for transfers between devices  20.8 us (17%)
  other arithmetic  3.85 us (3%)
    ppermute x20, starting transfers between devices, swap(): lax.ppermute(value, 'feat', [(index, index ^ mask) for index in range(siz...  27.9 us
    ppermute x20, waiting for transfers between devices, swap(): lax.ppermute(value, 'feat', [(index, index ^ mask) for index in range(siz...  20.8 us
    dot_general x3, matrix products, local(): lax.dot_general(errors[target], dec_weight[index], (((1,), (1,)), ((), ()...  11.4 us
    concatenate x3, local copies, waits for them, and re-layouts, local(): jnp.concatenate([even, odd], axis=0).reshape(tokens, layers, width)  10.5 us
    dot_general x3, matrix products, local(): jnp.dot(features[source], dec_weight[index], preferred_element_type=jnp.f...  9 us
    dot_general x1, matrix products, local(): jnp.einsum('pbf,pbd->pfd', pair_features, pair_errors, preferred_element_...  6.62 us
    dot_general x2, matrix products, local(): jnp.dot(inputs[layer], enc_weight[layer], preferred_element_type=jnp.floa...  6.05 us
    ppermute x5, local copies, waits for them, and re-layouts, swap(): lax.ppermute(value, 'feat', [(index, index ^ mask) for index in range(siz...  5.79 us
  transfers between devices with their start and end apart: 20, of which 10 were waited for; matrix products, arithmetic and copies ran while one was open for 10% of the time, Pallas kernels for 0%

profile of v1, /device:TPU:0, one launch (start us, length us, event | category | flops | bytes accessed | tf_op | source)
XLA Modules:
  0.0 121.9 jit_solution(11029922771651028689)
XLA Ops:
  0.6 0.7 compare_and_fusion
  1.3 0.7 compare_select_fusion
  2.0 0.7 gather_fusion.1
  2.8 1.6 %gather_fusion = bf16[8,2,2048]{2,0,1:T(8,128)(2,1)S(1)} fusion(bf16[2,16,2048]{2,1,0:T(8,128)(2,1)} %param.8, s32[1024]{0:T(1024)S(1)} %pad_clamp_fusion), kind=kCustom, calls=%fused_computation.clone | custom fusion | bytes 131104 | tf_op jit(solution)/shard_map/jit(_take)/gather | solution.py:49
  4.4 0.7 bitcast_convert_fusion
  5.2 5.1 %collective-permute-start.3 = (bf16[8,4096]{1,0:T(8,128)(2,1)S(1)}, bf16[8,4096]{1,0:T(8,128)(2,1)S(1)}, u32[]{:S(2)}, u32[]{:S(2)}) collective-permute-start(bf16[8,4096]{1,0:T(8,128)(2,1)S(1)} %bitcast.139), channel_id=1, source_target_pairs={{0,12},{1,13},{2,14},{3,15},{4,8},{5,9},{6,10},{7,11},{8,4},{9,5},... | collective-permute-start | bytes 196616 | tf_op jit(solution)/shard_map/ppermute | solution.py:10
  10.2 0.6 collective-permute-start.1
  10.8 1.7 %collective-permute-start = (bf16[8,4096]{1,0:T(8,128)(2,1)S(1)}, bf16[8,4096]{1,0:T(8,128)(2,1)S(1)}, u32[]{:S(2)}, u32[]{:S(2)}) collective-permute-start(bf16[8,4096]{1,0:T(8,128)(2,1)S(1)} %bitcast.142), channel_id=1, source_target_pairs={{0,2},{1,3},{2,0},{3,1},{4,6},{5,7},{6,4},{7,5},{8,10},{9,11},{10,... | collective-permute-start | bytes 196616 | tf_op jit(solution)/shard_map/ppermute | solution.py:10
  12.5 0.6 constant_dynamic-update-slice_fusion.7
  13.2 2.7 %collective-permute-done.2 = bf16[8,4096]{1,0:T(8,128)(2,1)S(1)} collective-permute-done((bf16[8,4096]{1,0:T(8,128)(2,1)S(1)}, bf16[8,4096]{1,0:T(8,128)(2,1)S(1)}, u32[]{:S(2)}, u32[]{:S(2)}) %collective-permute-start.2) | collective-permute-done | bytes 65568 | tf_op jit(solution)/shard_map/ppermute | solution.py:10
  15.9 1.6 %collective-permute-start.4 = (bf16[24,4096]{1,0:T(8,128)(2,1)S(1)}, bf16[24,4096]{1,0:T(8,128)(2,1)S(1)}, u32[]{:S(2)}, u32[]{:S(2)}) collective-permute-start(bf16[24,4096]{1,0:T(8,128)(2,1)S(1)} %pad_maximum_fusion.2), channel_id=1, source_target_pairs={{0,2},{1,3},{2,0},{3,1},{4,6},{5,7},{6,4},{7,5},{8,10},{9,11},{10,... | collective-permute-start | bytes 589832 | tf_op jit(solution)/shard_map/ppermute | solution.py:10
  17.4 0.6 constant_dynamic-update-slice_fusion.6
  18.1 0.6 constant_dynamic-update-slice_fusion.5
  18.7 3.7 %collective-permute-done.4 = bf16[24,4096]{1,0:T(8,128)(2,1)S(1)} collective-permute-done((bf16[24,4096]{1,0:T(8,128)(2,1)S(1)}, bf16[24,4096]{1,0:T(8,128)(2,1)S(1)}, u32[]{:S(2)}, u32[]{:S(2)}) %collective-permute-start.4) | collective-permute-done | bytes 196640 | tf_op jit(solution)/shard_map/ppermute | solution.py:10
  22.4 0.6 constant_dynamic-update-slice_fusion.4
  23.0 0.6 constant_dynamic-update-slice_fusion.3
  23.6 0.6 constant_dynamic-update-slice_fusion.2
  24.3 0.6 constant_dynamic-update-slice_fusion.1
  24.9 0.6 constant_dynamic-update-slice_fusion
  25.5 0.5 copy.49
  26.0 0.8 fusion.91
  26.8 0.5 copy.46
  27.3 1.3 %copy.44 = bf16[8,4096]{0,1:T(8,128)(2,1)} copy(bf16[8,4096]{1,0:T(8,128)(2,1)S(1)} %collective-permute-done.2) | data formatting | bytes 131072 | tf_op jit(solution)/shard_map/ppermute | solution.py:10
  28.6 1.3 %copy.42 = bf16[8,4096]{0,1:T(8,128)(2,1)} copy(bf16[8,4096]{1,0:T(8,128)(2,1)S(1)} %collective-permute-done.1) | data formatting | bytes 131072 | tf_op jit(solution)/shard_map/ppermute | solution.py:10
  29.9 1.3 %copy.41 = bf16[8,4096]{0,1:T(8,128)(2,1)} copy(bf16[8,4096]{1,0:T(8,128)(2,1)S(1)} %collective-permute-done) | data formatting | bytes 131072 | tf_op jit(solution)/shard_map/ppermute | solution.py:10
  31.2 1.3 %copy.47 = bf16[8,4096]{0,1:T(8,128)(2,1)} copy(bf16[8,4096]{1,0:T(8,128)(2,1)S(1)} %get-tuple-element.16) | data formatting | bytes 131072 | tf_op jit(solution)/shard_map/slice | solution.py:26
  32.5 1.3 %copy.45 = bf16[8,4096]{0,1:T(8,128)(2,1)} copy(bf16[8,4096]{1,0:T(8,128)(2,1)S(1)} %get-tuple-element.17) | data formatting | bytes 131072 | tf_op jit(solution)/shard_map/slice | solution.py:26
  33.9 1.3 %copy.43 = bf16[8,4096]{0,1:T(8,128)(2,1)} copy(bf16[8,4096]{1,0:T(8,128)(2,1)S(1)} %get-tuple-element.18) | data formatting | bytes 131072 | tf_op jit(solution)/shard_map/slice | solution.py:26
  35.2 1.4 %copy.48 = bf16[64,4096]{0,1:T(8,128)(2,1)} copy(bf16[64,4096]{1,0:T(8,128)(2,1)S(1)} %collective-permute-done.5) | data formatting | bytes 1048576 | tf_op jit(solution)/shard_map/ppermute | solution.py:10
  36.6 9.8 %concatenate.50 = bf16[128,2,2048]{0,2,1:T(8,128)(2,1)S(1)} concatenate(bf16[8,2,2048]{0,2,1:T(8,128)(2,1)S(1)} %copy.49, bf16[8,2,2048]{0,2,1:T(8,128)(2,1)} %bitcast.131, bf16[8,2,2048]{0,2,1:T(8,128)(2,1)} %bitcast.130, bf16[8,2,2048]{0,2,1:T(8,128)(2,1)} %bitcast.134, bf16[8,2,2048]{0,2,1:T(8,128)(2,1)} %bitcast.129, bf16[8,2,2048]{0,2,1:T(8,128)(2,1)} %bitcast.133, ...), dimensions={0} | concatenate | bytes 2097152 | tf_op jit(solution)/shard_map/concatenate | solution.py:53
  46.4 2.9 %fusion.36 = f32[128,1024]{1,0:T(8,128)S(1)} fusion(bf16[2,2048,1024]{2,1,0:T(8,128)(2,1)} %param.11, bf16[2,128,2048]{1,2,0:T(8,128)(2,1)S(1)} %bitcast.126, f32[1024]{0:T(1024)S(1)} %bitcast.146), kind=kOutput, calls=%fused_computation.34 | convolution fusion | flops 537001984 | bytes 5246976 | tf_op jit(solution)/shard_map/dot_general | solution.py:55
  49.3 3.1 %fusion.42 = f32[128,1024]{1,0:T(8,128)S(1)} fusion(bf16[2,2048,1024]{2,1,0:T(8,128)(2,1)} %param.11, bf16[2,128,2048]{1,2,0:T(8,128)(2,1)S(1)} %bitcast.127, f32[1024]{0:T(1024)S(1)} %bitcast.145), kind=kOutput, calls=%fused_computation.36 | convolution fusion | flops 537001984 | bytes 5246976 | tf_op jit(solution)/shard_map/dot_general | solution.py:55
  52.5 3.1 %fusion.30 = bf16[128,2048]{1,0:T(8,128)(2,1)S(1)} fusion(bf16[3,1024,2048]{2,1,0:T(8,128)(2,1)} %param.13, f32[128,1024]{1,0:T(8,128)S(1)} %fusion.36), kind=kOutput, calls=%fused_computation.30 | convolution fusion | flops 537395200 | bytes 5242880 | tf_op jit(solution)/shard_map/dot_general | solution.py:64
  55.6 2.9 %fusion.2 = f32[128,2048]{1,0:T(8,128)S(1)} fusion(bf16[3,1024,2048]{2,1,0:T(8,128)(2,1)} %param.13, f32[128,1024]{1,0:T(8,128)S(1)} %fusion.42), kind=kOutput, calls=%fused_computation.6 | convolution fusion | flops 537133056 | bytes 5767168 | tf_op jit(solution)/shard_map/dot_general | solution.py:64
  58.5 3.0 %fusion.27 = bf16[128,2048]{1,0:T(8,128)(2,1)S(1)} fusion(f32[128,2048]{1,0:T(8,128)S(1)} %fusion.2, bf16[3,1024,2048]{2,1,0:T(8,128)(2,1)} %param.13, f32[128,1024]{1,0:T(8,128)S(1)} %fusion.36), kind=kOutput, calls=%fused_computation.29 | convolution fusion | flops 537657344 | bytes 6291456 | tf_op jit(solution)/shard_map/dot_general | solution.py:64
  61.6 0.6 collective-permute-start.6
  62.2 1.5 %collective-permute-done.6 = bf16[8,8,4096]{2,1,0:T(8,128)(2,1)S(1)} collective-permute-done((bf16[8,8,4096]{2,1,0:T(8,128)(2,1)S(1)}, bf16[8,8,4096]{2,1,0:T(8,128)(2,1)S(1)}, u32[]{:S(2)}, u32[]{:S(2)}) %collective-permute-start.6) | collective-permute-done | bytes 524320 | tf_op jit(solution)/shard_map/ppermute | solution.py:10
  63.8 0.1 fusion.63
  63.9 1.7 %collective-permute-start.7 = (bf16[8,4096]{1,0:T(8,128)(2,1)S(1)}, bf16[8,4096]{1,0:T(8,128)(2,1)S(1)}, u32[]{:S(2)}, u32[]{:S(2)}) collective-permute-start(bf16[8,4096]{1,0:T(8,128)(2,1)S(1)} %get-tuple-element.6), channel_id=1, source_target_pairs={{0,2},{1,3},{2,0},{3,1},{4,6},{5,7},{6,4},{7,5},{8,10},{9,11},{10,... | collective-permute-start | bytes 196616 | tf_op jit(solution)/shard_map/ppermute | solution.py:10
  65.6 1.7 %collective-permute-start.13 = (bf16[8,4096]{1,0:T(8,128)(2,1)S(1)}, bf16[8,4096]{1,0:T(8,128)(2,1)S(1)}, u32[]{:S(2)}, u32[]{:S(2)}) collective-permute-start(bf16[8,4096]{1,0:T(8,128)(2,1)S(1)} %get-tuple-element.7), channel_id=1, source_target_pairs={{0,14},{1,15},{2,12},{3,13},{4,10},{5,11},{6,8},{7,9},{8,6},{9,7},... | collective-permute-start | bytes 196616 | tf_op jit(solution)/shard_map/ppermute | solution.py:10
  67.3 2.0 %collective-permute-start.12 = (bf16[8,4096]{1,0:T(8,128)(2,1)S(1)}, bf16[8,4096]{1,0:T(8,128)(2,1)S(1)}, u32[]{:S(2)}, u32[]{:S(2)}) collective-permute-start(bf16[8,4096]{1,0:T(8,128)(2,1)S(1)} %get-tuple-element.8), channel_id=1, source_target_pairs={{0,12},{1,13},{2,14},{3,15},{4,8},{5,9},{6,10},{7,11},{8,4},{9,5},... | collective-permute-start | bytes 196616 | tf_op jit(solution)/shard_map/ppermute | solution.py:10
  69.3 4.0 %collective-permute-start.10 = (bf16[8,4096]{1,0:T(8,128)(2,1)S(1)}, bf16[8,4096]{1,0:T(8,128)(2,1)S(1)}, u32[]{:S(2)}, u32[]{:S(2)}) collective-permute-start(bf16[8,4096]{1,0:T(8,128)(2,1)S(1)} %get-tuple-element.10), channel_id=1, source_target_pairs={{0,8},{1,9},{2,10},{3,11},{4,12},{5,13},{6,14},{7,15},{8,0},{9,1},... | collective-permute-start | bytes 196616 | tf_op jit(solution)/shard_map/ppermute | solution.py:10
  73.3 1.9 %collective-permute-start.8 = (bf16[8,4096]{1,0:T(8,128)(2,1)S(1)}, bf16[8,4096]{1,0:T(8,128)(2,1)S(1)}, u32[]{:S(2)}, u32[]{:S(2)}) collective-permute-start(bf16[8,4096]{1,0:T(8,128)(2,1)S(1)} %get-tuple-element.12), channel_id=1, source_target_pairs={{0,4},{1,5},{2,6},{3,7},{4,0},{5,1},{6,2},{7,3},{8,12},{9,13},{10,... | collective-permute-start | bytes 196616 | tf_op jit(solution)/shard_map/ppermute | solution.py:10
  75.1 0.8 fusion.82
  75.9 3.6 %collective-permute-done.11 = bf16[8,4096]{1,0:T(8,128)(2,1)S(1)} collective-permute-done((bf16[8,4096]{1,0:T(8,128)(2,1)S(1)}, bf16[8,4096]{1,0:T(8,128)(2,1)S(1)}, u32[]{:S(2)}, u32[]{:S(2)}) %collective-permute-start.11) | collective-permute-done | bytes 65568 | tf_op jit(solution)/shard_map/ppermute | solution.py:10
  79.5 1.2 collective-permute-done.9
  80.7 0.1 constant_dynamic-update-slice_fusion.12
  80.8 1.9 %collective-permute-start.17 = (bf16[8,4096]{1,0:T(8,128)(2,1)S(1)}, bf16[8,4096]{1,0:T(8,128)(2,1)S(1)}, u32[]{:S(2)}, u32[]{:S(2)}) collective-permute-start(bf16[8,4096]{1,0:T(8,128)(2,1)S(1)} %get-tuple-element.5), channel_id=1, source_target_pairs={{0,12},{1,13},{2,14},{3,15},{4,8},{5,9},{6,10},{7,11},{8,4},{9,5},... | collective-permute-start | bytes 196616 | tf_op jit(solution)/shard_map/ppermute | solution.py:10
  82.7 2.5 %collective-permute-start.15 = (bf16[8,4096]{1,0:T(8,128)(2,1)S(1)}, bf16[8,4096]{1,0:T(8,128)(2,1)S(1)}, u32[]{:S(2)}, u32[]{:S(2)}) collective-permute-start(bf16[8,4096]{1,0:T(8,128)(2,1)S(1)} %get-tuple-element.5), channel_id=1, source_target_pairs={{0,4},{1,5},{2,6},{3,7},{4,0},{5,1},{6,2},{7,3},{8,12},{9,13},{10,... | collective-permute-start | bytes 196616 | tf_op jit(solution)/shard_map/ppermute | solution.py:10
  85.3 1.3 %collective-permute-start.14 = (bf16[8,4096]{1,0:T(8,128)(2,1)S(1)}, bf16[8,4096]{1,0:T(8,128)(2,1)S(1)}, u32[]{:S(2)}, u32[]{:S(2)}) collective-permute-start(bf16[8,4096]{1,0:T(8,128)(2,1)S(1)} %get-tuple-element.5), channel_id=1, source_target_pairs={{0,2},{1,3},{2,0},{3,1},{4,6},{5,7},{6,4},{7,5},{8,10},{9,11},{10,... | collective-permute-start | bytes 196616 | tf_op jit(solution)/shard_map/ppermute | solution.py:10
  86.5 0.4 collective-permute-done.17
  87.0 1.4 %collective-permute-done.16 = bf16[8,4096]{1,0:T(8,128)(2,1)S(1)} collective-permute-done((bf16[8,4096]{1,0:T(8,128)(2,1)S(1)}, bf16[8,4096]{1,0:T(8,128)(2,1)S(1)}, u32[]{:S(2)}, u32[]{:S(2)}) %collective-permute-start.16) | collective-permute-done | bytes 65568 | tf_op jit(solution)/shard_map/ppermute | solution.py:10
  88.4 1.3 %collective-permute-start.18 = (bf16[24,4096]{1,0:T(8,128)(2,1)S(1)}, bf16[24,4096]{1,0:T(8,128)(2,1)S(1)}, u32[]{:S(2)}, u32[]{:S(2)}) collective-permute-start(bf16[24,4096]{1,0:T(8,128)(2,1)S(1)} %pad_maximum_fusion.3), channel_id=1, source_target_pairs={{0,2},{1,3},{2,0},{3,1},{4,6},{5,7},{6,4},{7,5},{8,10},{9,11},{10,... | collective-permute-start | bytes 589832 | tf_op jit(solution)/shard_map/ppermute | solution.py:10
  89.7 0.5 collective-permute-done.14
  90.3 3.8 %collective-permute-done.18 = bf16[24,4096]{1,0:T(8,128)(2,1)S(1)} collective-permute-done((bf16[24,4096]{1,0:T(8,128)(2,1)S(1)}, bf16[24,4096]{1,0:T(8,128)(2,1)S(1)}, u32[]{:S(2)}, u32[]{:S(2)}) %collective-permute-start.18) | collective-permute-done | bytes 196640 | tf_op jit(solution)/shard_map/ppermute | solution.py:10
  94.3 1.8 %collective-permute-done.19 = bf16[64,4096]{1,0:T(8,128)(2,1)S(1)} collective-permute-done((bf16[64,4096]{1,0:T(8,128)(2,1)S(1)}, bf16[64,4096]{1,0:T(8,128)(2,1)S(1)}, u32[]{:S(2)}, u32[]{:S(2)}) %collective-permute-start.19) | collective-permute-done | bytes 524320 | tf_op jit(solution)/shard_map/ppermute | solution.py:10
  96.2 0.7 copy.50
  96.9 0.5 copy.51
  97.4 3.9 %fusion.60 = f32[1,128,1024]{2,1,0:T(8,128)S(1)} fusion(bf16[3,1024,2048]{2,1,0:T(8,128)(2,1)} %param.13, f32[128,1024]{1,0:T(8,128)} %copy-done.5, bf16[2,128,2048]{2,1,0:T(8,128)(2,1)S(1)} %bitcast.121), kind=kOutput, calls=%fused_computation.42 | convolution fusion | flops 537264128 | bytes 5767168 | tf_op jit(solution)/shard_map/dot_general | solution.py:82
  101.3 3.7 %fusion.6 = f32[128,1024]{1,0:T(8,128)S(1)} fusion(bf16[3,1024,2048]{2,1,0:T(8,128)(2,1)} %param.13, bf16[2,128,2048]{2,1,0:T(8,128)(2,1)S(1)} %bitcast.122), kind=kOutput, calls=%fused_computation.10 | convolution fusion | flops 536870912 | bytes 5242880 | tf_op jit(solution)/shard_map/dot_general | solution.py:82
  105.1 3.8 %fusion.51 = f32[1,128,1024]{2,1,0:T(8,128)S(1)} fusion(f32[128,1024]{1,0:T(8,128)S(1)} %fusion.6, bf16[3,1024,2048]{2,1,0:T(8,128)(2,1)} %param.13, bf16[2,128,2048]{2,1,0:T(8,128)(2,1)S(1)} %bitcast.124, f32[128,1024]{1,0:T(8,128)S(1)} %copy-done.3), kind=kOutput, calls=%fused_computation.39 | convolution fusion | flops 537395200 | bytes 6291456 | tf_op jit(solution)/shard_map/dot_general | solution.py:82
  108.9 0.7 fusion.64
  109.5 5.7 %convolution_convert_fusion = bf16[2,2048,1024]{2,1,0:T(8,128)(2,1)} fusion(f32[1,128,1024]{2,1,0:T(8,128)S(1)} %fusion.60, f32[1,128,1024]{2,1,0:T(8,128)S(1)} %fusion.51, bf16[128,2,2048]{0,2,1:T(8,128)(2,1)S(1)} %concatenate.50), kind=kOutput, calls=%fused_computation.3 | convolution fusion | flops 1078198272 | bytes 10485760 | tf_op jit(solution)/shard_map/lbd,lbf->ldf/dot_general | solution.py:89
  115.3 6.6 %multiply_convert_fusion = bf16[3,1024,2048]{2,1,0:T(8,128)(2,1)} fusion(bf16[1,128,2048]{2,1,0:T(8,128)(2,1)S(1)} %slice.139, bf16[2,128,2048]{2,1,0:T(8,128)(2,1)S(1)} %bitcast.125, bf16[1,128,1024]{2,1,0:T(8,128)(2,1)S(1)} %get-tuple-element.27, bf16[1,128,1024]{2,1,0:T(8,128)(2,1)S(1)} %copy-done.4), kind=kOutput, calls=%fused_computation.2 | convolution fusion | flops 1624768512 | bytes 14680064 | tf_op jit(solution)/shard_map/pbf,pbd->pfd/dot_general | solution.py:78
  (50 shorter events, 0.5 us)
Async XLA Ops:
  0.6 1.4 %copy-start = (bf16[2,16,2048]{2,1,0:T(8,128)(2,1)S(1)}, bf16[2,16,2048]{2,1,0:T(8,128)(2,1)}, u32[]{:S(2)}) copy-start(bf16[2,16,2048]{2,1,0:T(8,128)(2,1)} %param.9) | copy-start | bytes 393220
  5.2 8.0 %collective-permute-start.3 = (bf16[8,4096]{1,0:T(8,128)(2,1)S(1)}, bf16[8,4096]{1,0:T(8,128)(2,1)S(1)}, u32[]{:S(2)}, u32[]{:S(2)}) collective-permute-start(bf16[8,4096]{1,0:T(8,128)(2,1)S(1)} %bitcast.139), channel_id=1, source_target_pairs={{0,12},{1,13},{2,14},{3,15},{4,8},{5,9},{6,10},{7,11},{8,4},{9,5},... | collective-permute-start | bytes 196616 | tf_op jit(solution)/shard_map/ppermute | solution.py:10
  10.2 5.6 %collective-permute-start.2 = (bf16[8,4096]{1,0:T(8,128)(2,1)S(1)}, bf16[8,4096]{1,0:T(8,128)(2,1)S(1)}, u32[]{:S(2)}, u32[]{:S(2)}) collective-permute-start(bf16[8,4096]{1,0:T(8,128)(2,1)S(1)} %bitcast.140), channel_id=1, source_target_pairs={{0,8},{1,9},{2,10},{3,11},{4,12},{5,13},{6,14},{7,15},{8,0},{9,1},... | collective-permute-start | bytes 196616 | tf_op jit(solution)/shard_map/ppermute | solution.py:10
  10.2 5.6 %collective-permute-start.1 = (bf16[8,4096]{1,0:T(8,128)(2,1)S(1)}, bf16[8,4096]{1,0:T(8,128)(2,1)S(1)}, u32[]{:S(2)}, u32[]{:S(2)}) collective-permute-start(bf16[8,4096]{1,0:T(8,128)(2,1)S(1)} %bitcast.141), channel_id=1, source_target_pairs={{0,4},{1,5},{2,6},{3,7},{4,0},{5,1},{6,2},{7,3},{8,12},{9,13},{10,... | collective-permute-start | bytes 196616 | tf_op jit(solution)/shard_map/ppermute | solution.py:10
  10.8 6.6 %collective-permute-start = (bf16[8,4096]{1,0:T(8,128)(2,1)S(1)}, bf16[8,4096]{1,0:T(8,128)(2,1)S(1)}, u32[]{:S(2)}, u32[]{:S(2)}) collective-permute-start(bf16[8,4096]{1,0:T(8,128)(2,1)S(1)} %bitcast.142), channel_id=1, source_target_pairs={{0,2},{1,3},{2,0},{3,1},{4,6},{5,7},{6,4},{7,5},{8,10},{9,11},{10,... | collective-permute-start | bytes 196616 | tf_op jit(solution)/shard_map/ppermute | solution.py:10
  15.9 6.5 %collective-permute-start.4 = (bf16[24,4096]{1,0:T(8,128)(2,1)S(1)}, bf16[24,4096]{1,0:T(8,128)(2,1)S(1)}, u32[]{:S(2)}, u32[]{:S(2)}) collective-permute-start(bf16[24,4096]{1,0:T(8,128)(2,1)S(1)} %pad_maximum_fusion.2), channel_id=1, source_target_pairs={{0,2},{1,3},{2,0},{3,1},{4,6},{5,7},{6,4},{7,5},{8,10},{9,11},{10,... | collective-permute-start | bytes 589832 | tf_op jit(solution)/shard_map/ppermute | solution.py:10
  25.5 9.7 %collective-permute-start.5 = (bf16[64,4096]{1,0:T(8,128)(2,1)}, bf16[64,4096]{1,0:T(8,128)(2,1)S(1)}, u32[]{:S(2)}, u32[]{:S(2)}) collective-permute-start(bf16[64,4096]{1,0:T(8,128)(2,1)} %get-tuple-element.15), channel_id=1, source_target_pairs={{0,1},{1,0},{2,3},{3,2},{4,5},{5,4},{6,7},{7,6},{8,9},{9,8},{10,11... | collective-permute-start | bytes 1572872 | tf_op jit(solution)/shard_map/ppermute | solution.py:10
  49.3 25.8 %copy-start.2 = (f32[128,1024]{1,0:T(8,128)}, f32[128,1024]{1,0:T(8,128)S(1)}, u32[]{:S(2)}) copy-start(f32[128,1024]{1,0:T(8,128)S(1)} %fusion.36) | copy-start | bytes 1572868
  52.5 22.7 %copy-start.5 = (f32[128,1024]{1,0:T(8,128)}, f32[128,1024]{1,0:T(8,128)S(1)}, u32[]{:S(2)}) copy-start(f32[128,1024]{1,0:T(8,128)S(1)} %fusion.42) | copy-start | bytes 1572868
  55.6 25.2 %copy-start.6 = (f32[2,8,2048]{2,1,0:T(8,128)S(1)}, f32[2,8,2048]{2,1,0:T(8,128)}, u32[]{:S(2)}) copy-start(f32[2,8,2048]{2,1,0:T(8,128)} %get-tuple-element.25) | copy-start | bytes 393220
  61.6 2.1 %collective-permute-start.6 = (bf16[8,8,4096]{2,1,0:T(8,128)(2,1)S(1)}, bf16[8,8,4096]{2,1,0:T(8,128)(2,1)S(1)}, u32[]{:S(2)}, u32[]{:S(2)}) collective-permute-start(bf16[8,8,4096]{2,1,0:T(8,128)(2,1)S(1)} %slice_bitcast_fusion.2), channel_id=1, source_target_pairs={{0,1},{1,0},{2,3},{3,2},{4,5},{5,4},{6,7},{7,6},{8,9},{9,8},{10,11... | collective-permute-start | bytes 1572872 | tf_op jit(solution)/shard_map/ppermute | solution.py:10
  63.9 9.3 %collective-permute-start.7 = (bf16[8,4096]{1,0:T(8,128)(2,1)S(1)}, bf16[8,4096]{1,0:T(8,128)(2,1)S(1)}, u32[]{:S(2)}, u32[]{:S(2)}) collective-permute-start(bf16[8,4096]{1,0:T(8,128)(2,1)S(1)} %get-tuple-element.6), channel_id=1, source_target_pairs={{0,2},{1,3},{2,0},{3,1},{4,6},{5,7},{6,4},{7,5},{8,10},{9,11},{10,... | collective-permute-start | bytes 196616 | tf_op jit(solution)/shard_map/ppermute | solution.py:10
  65.6 7.7 %collective-permute-start.13 = (bf16[8,4096]{1,0:T(8,128)(2,1)S(1)}, bf16[8,4096]{1,0:T(8,128)(2,1)S(1)}, u32[]{:S(2)}, u32[]{:S(2)}) collective-permute-start(bf16[8,4096]{1,0:T(8,128)(2,1)S(1)} %get-tuple-element.7), channel_id=1, source_target_pairs={{0,14},{1,15},{2,12},{3,13},{4,10},{5,11},{6,8},{7,9},{8,6},{9,7},... | collective-permute-start | bytes 196616 | tf_op jit(solution)/shard_map/ppermute | solution.py:10
  67.3 8.6 %collective-permute-start.12 = (bf16[8,4096]{1,0:T(8,128)(2,1)S(1)}, bf16[8,4096]{1,0:T(8,128)(2,1)S(1)}, u32[]{:S(2)}, u32[]{:S(2)}) collective-permute-start(bf16[8,4096]{1,0:T(8,128)(2,1)S(1)} %get-tuple-element.8), channel_id=1, source_target_pairs={{0,12},{1,13},{2,14},{3,15},{4,8},{5,9},{6,10},{7,11},{8,4},{9,5},... | collective-permute-start | bytes 196616 | tf_op jit(solution)/shard_map/ppermute | solution.py:10
  69.3 10.3 %collective-permute-start.11 = (bf16[8,4096]{1,0:T(8,128)(2,1)S(1)}, bf16[8,4096]{1,0:T(8,128)(2,1)S(1)}, u32[]{:S(2)}, u32[]{:S(2)}) collective-permute-start(bf16[8,4096]{1,0:T(8,128)(2,1)S(1)} %get-tuple-element.9), channel_id=1, source_target_pairs={{0,10},{1,11},{2,8},{3,9},{4,14},{5,15},{6,12},{7,13},{8,2},{9,3},... | collective-permute-start | bytes 196616 | tf_op jit(solution)/shard_map/ppermute | solution.py:10
  69.3 10.3 %collective-permute-start.10 = (bf16[8,4096]{1,0:T(8,128)(2,1)S(1)}, bf16[8,4096]{1,0:T(8,128)(2,1)S(1)}, u32[]{:S(2)}, u32[]{:S(2)}) collective-permute-start(bf16[8,4096]{1,0:T(8,128)(2,1)S(1)} %get-tuple-element.10), channel_id=1, source_target_pairs={{0,8},{1,9},{2,10},{3,11},{4,12},{5,13},{6,14},{7,15},{8,0},{9,1},... | collective-permute-start | bytes 196616 | tf_op jit(solution)/shard_map/ppermute | solution.py:10
  73.2 7.5 %collective-permute-start.9 = (bf16[8,4096]{1,0:T(8,128)(2,1)S(1)}, bf16[8,4096]{1,0:T(8,128)(2,1)S(1)}, u32[]{:S(2)}, u32[]{:S(2)}) collective-permute-start(bf16[8,4096]{1,0:T(8,128)(2,1)S(1)} %get-tuple-element.11), channel_id=1, source_target_pairs={{0,6},{1,7},{2,4},{3,5},{4,2},{5,3},{6,0},{7,1},{8,14},{9,15},{10,... | collective-permute-start | bytes 196616 | tf_op jit(solution)/shard_map/ppermute | solution.py:10
  73.3 7.5 %collective-permute-start.8 = (bf16[8,4096]{1,0:T(8,128)(2,1)S(1)}, bf16[8,4096]{1,0:T(8,128)(2,1)S(1)}, u32[]{:S(2)}, u32[]{:S(2)}) collective-permute-start(bf16[8,4096]{1,0:T(8,128)(2,1)S(1)} %get-tuple-element.12), channel_id=1, source_target_pairs={{0,4},{1,5},{2,6},{3,7},{4,0},{5,1},{6,2},{7,3},{8,12},{9,13},{10,... | collective-permute-start | bytes 196616 | tf_op jit(solution)/shard_map/ppermute | solution.py:10
  80.8 6.1 %collective-permute-start.17 = (bf16[8,4096]{1,0:T(8,128)(2,1)S(1)}, bf16[8,4096]{1,0:T(8,128)(2,1)S(1)}, u32[]{:S(2)}, u32[]{:S(2)}) collective-permute-start(bf16[8,4096]{1,0:T(8,128)(2,1)S(1)} %get-tuple-element.5), channel_id=1, source_target_pairs={{0,12},{1,13},{2,14},{3,15},{4,8},{5,9},{6,10},{7,11},{8,4},{9,5},... | collective-permute-start | bytes 196616 | tf_op jit(solution)/shard_map/ppermute | solution.py:10
  82.7 5.6 %collective-permute-start.16 = (bf16[8,4096]{1,0:T(8,128)(2,1)S(1)}, bf16[8,4096]{1,0:T(8,128)(2,1)S(1)}, u32[]{:S(2)}, u32[]{:S(2)}) collective-permute-start(bf16[8,4096]{1,0:T(8,128)(2,1)S(1)} %get-tuple-element.5), channel_id=1, source_target_pairs={{0,8},{1,9},{2,10},{3,11},{4,12},{5,13},{6,14},{7,15},{8,0},{9,1},... | collective-permute-start | bytes 196616 | tf_op jit(solution)/shard_map/ppermute | solution.py:10
  82.7 5.6 %collective-permute-start.15 = (bf16[8,4096]{1,0:T(8,128)(2,1)S(1)}, bf16[8,4096]{1,0:T(8,128)(2,1)S(1)}, u32[]{:S(2)}, u32[]{:S(2)}) collective-permute-start(bf16[8,4096]{1,0:T(8,128)(2,1)S(1)} %get-tuple-element.5), channel_id=1, source_target_pairs={{0,4},{1,5},{2,6},{3,7},{4,0},{5,1},{6,2},{7,3},{8,12},{9,13},{10,... | collective-permute-start | bytes 196616 | tf_op jit(solution)/shard_map/ppermute | solution.py:10
  85.3 5.0 %collective-permute-start.14 = (bf16[8,4096]{1,0:T(8,128)(2,1)S(1)}, bf16[8,4096]{1,0:T(8,128)(2,1)S(1)}, u32[]{:S(2)}, u32[]{:S(2)}) collective-permute-start(bf16[8,4096]{1,0:T(8,128)(2,1)S(1)} %get-tuple-element.5), channel_id=1, source_target_pairs={{0,2},{1,3},{2,0},{3,1},{4,6},{5,7},{6,4},{7,5},{8,10},{9,11},{10,... | collective-permute-start | bytes 196616 | tf_op jit(solution)/shard_map/ppermute | solution.py:10
  88.4 5.7 %collective-permute-start.18 = (bf16[24,4096]{1,0:T(8,128)(2,1)S(1)}, bf16[24,4096]{1,0:T(8,128)(2,1)S(1)}, u32[]{:S(2)}, u32[]{:S(2)}) collective-permute-start(bf16[24,4096]{1,0:T(8,128)(2,1)S(1)} %pad_maximum_fusion.3), channel_id=1, source_target_pairs={{0,2},{1,3},{2,0},{3,1},{4,6},{5,7},{6,4},{7,5},{8,10},{9,11},{10,... | collective-permute-start | bytes 589832 | tf_op jit(solution)/shard_map/ppermute | solution.py:10
  94.2 2.0 %collective-permute-start.19 = (bf16[64,4096]{1,0:T(8,128)(2,1)S(1)}, bf16[64,4096]{1,0:T(8,128)(2,1)S(1)}, u32[]{:S(2)}, u32[]{:S(2)}) collective-permute-start(bf16[64,4096]{1,0:T(8,128)(2,1)S(1)} %get-tuple-element.13), channel_id=1, source_target_pairs={{0,1},{1,0},{2,3},{3,2},{4,5},{5,4},{6,7},{7,6},{8,9},{9,8},{10,11... | collective-permute-start | bytes 1572872 | tf_op jit(solution)/shard_map/ppermute | solution.py:10
  97.4 7.7 %copy-start.3 = (f32[128,1024]{1,0:T(8,128)S(1)}, f32[128,1024]{1,0:T(8,128)}, u32[]{:S(2)}) copy-start(f32[128,1024]{1,0:T(8,128)} %copy-done.2) | copy-start | bytes 1572868
  105.1 10.2 %copy-start.4 = (bf16[1,128,1024]{2,1,0:T(8,128)(2,1)S(1)}, bf16[1,128,1024]{2,1,0:T(8,128)(2,1)}, u32[]{:S(2)}) copy-start(bf16[1,128,1024]{2,1,0:T(8,128)(2,1)} %get-tuple-element.28) | copy-start | bytes 786436
  109.5 12.3 %copy-start.1 = (bf16[2,16,2048]{2,1,0:T(8,128)(2,1)S(1)}, bf16[2,16,2048]{2,1,0:T(8,128)(2,1)}, u32[]{:S(2)}) copy-start(bf16[2,16,2048]{2,1,0:T(8,128)(2,1)} %param.9) | copy-start | bytes 393220

commit v2 on v1

v2 whole, which is shorter than its diff:
```python
import functools
import math

import jax
import jax.numpy as jnp
from jax import lax
from jax.experimental import pallas as pl
from jax.experimental.pallas import tpu as pltpu
from jax.sharding import PartitionSpec as P

MIB = 1 << 20
SLOTS = 6
WHOLE = pl.BlockSpec(memory_space=pltpu.VMEM)
HELD = pl.BlockSpec(memory_space=pl.ANY)


def pair_list(layers):
    return [(source, target) for source in range(layers) for target in range(source, layers)]


def params(limit):
    return pltpu.CompilerParams(vmem_limit_bytes=limit)


def cost(flops, moved):
    return pl.CostEstimate(flops=int(flops), transcendentals=0, bytes_accessed=int(moved))


def in_vmem(array):
    return pltpu.with_memory_space_constraint(array, pltpu.VMEM)


def swap(value, mask, size):
    return lax.ppermute(value, "feat", [(index, index ^ mask) for index in range(size)])


def slot_order(size):
    if size < 4:
        return [0]
    far = list(range(0, size, 4))
    return far + [mask + 2 for mask in far]


def gather_rows(own, size):
    if size == 1:
        return own, None
    if size == 2:
        return own, swap(own, 1, size)
    far = [4 * step for step in range(1, size // 4)]
    got = {mask: swap(own, mask, size) for mask in far[::-1]}
    parts = [own] + [got[mask] for mask in far] + [swap(own, 2, size)]
    if far:
        parts.append(swap(jnp.concatenate([got[mask] for mask in far], axis=0), 2, size))
    even = jnp.concatenate(parts, axis=0)
    return even, swap(even, 1, size)


def scatter_sums(keep, send, size, rows):
    got = swap(send, 1, size)
    pair = (keep.astype(jnp.float32) + got.astype(jnp.float32)).astype(jnp.bfloat16)
    total = pair[:rows].astype(jnp.float32)
    for slot, mask in enumerate(slot_order(size)):
        if mask:
            total = total + swap(pair[slot * rows : (slot + 1) * rows], mask, size).astype(jnp.float32)
    return total


def pick_kernel(ids_ref, in_ref, out_ref, picked_in, picked_out):
    layers, buf, width = in_ref.shape
    rows = ids_ref.shape[0]
    place = lax.broadcasted_iota(jnp.int32, (rows, buf), 0)
    wanted = jnp.zeros((rows, buf), jnp.int32)
    for row in range(rows):
        wanted = jnp.where(place == row, ids_ref[row], wanted)
    hot = jnp.where(wanted == lax.broadcasted_iota(jnp.int32, (rows, buf), 1), 1.0, 0.0).astype(jnp.bfloat16)
    for layer in range(layers):
        columns = slice(layer * width, (layer + 1) * width)
        picked_in[:, columns] = jnp.dot(hot, in_ref[layer], preferred_element_type=jnp.float32).astype(
            jnp.bfloat16
        )
        picked_out[:, columns] = jnp.dot(hot, out_ref[layer], preferred_element_type=jnp.float32).astype(
            jnp.bfloat16
        )


def pick(row_ids, store_inputs, store_targets):
    layers, _, width = store_inputs.shape
    shape = jax.ShapeDtypeStruct((row_ids.shape[0], layers * width), jnp.bfloat16)
    return pl.pallas_call(
        pick_kernel,
        out_shape=(shape, shape),
        in_specs=[pl.BlockSpec(memory_space=pltpu.SMEM), WHOLE, WHOLE],
        out_specs=[WHOLE, WHOLE],
        compiler_params=params(4 * MIB),
        name="pick",
    )(row_ids, store_inputs, store_targets)


def load_kernel(enc_ref, dec_ref, enc_out, dec_out, sems):
    copies = [
        pltpu.make_async_copy(enc_ref.at[layer], enc_out.at[layer], sems.at[layer])
        for layer in range(enc_ref.shape[0])
    ]
    copies += [
        pltpu.make_async_copy(dec_ref.at[index], dec_out.at[index], sems.at[len(copies) + index])
        for index in range(dec_ref.shape[0])
    ]
    for copy in copies:
        copy.start()
    for copy in copies:
        copy.wait()


def load_weights(enc_weight, dec_weight):
    moved = 4 * (enc_weight.size + dec_weight.size)
    return pl.pallas_call(
        load_kernel,
        out_shape=(
            pltpu.VMEM(enc_weight.shape, enc_weight.dtype),
            pltpu.VMEM(dec_weight.shape, dec_weight.dtype),
        ),
        in_specs=[HELD, HELD],
        out_specs=[WHOLE, WHOLE],
        scratch_shapes=[pltpu.SemaphoreType.DMA((enc_weight.shape[0] + dec_weight.shape[0],))],
        compiler_params=params(2 * MIB),
        cost_estimate=cost(moved * 100, moved),
        name="load_weights",
    )(
        pltpu.with_memory_space_constraint(enc_weight, pltpu.HBM),
        pltpu.with_memory_space_constraint(dec_weight, pltpu.HBM),
    )


def forward_kernel(even_ref, odd_ref, enc_ref, bias_ref, dec_ref, keep_ref, send_ref, feat_ref, x_ref):
    layers, width, tile = enc_ref.shape
    half = even_ref.shape[0]
    x_ref[:half] = even_ref[...]
    x_ref[half:] = odd_ref[...]
    chunk = min(256, tile)
    for layer in range(layers):

        @pl.loop(0, tile // chunk)
        def _(step):
            columns = pl.ds(pl.multiple_of(step * chunk, chunk), chunk)
            value = jnp.dot(
                x_ref[:, layer * width : (layer + 1) * width],
                enc_ref[layer, :, columns],
                preferred_element_type=jnp.float32,
            )
            value = value + bias_ref[layer : layer + 1, columns]
            feat_ref[layer, :, columns] = jnp.maximum(value, 0.0).astype(jnp.bfloat16)

    span = min(512, width)
    for target in range(layers):

        @pl.loop(0, width // span)
        def _(step):
            columns = pl.ds(pl.multiple_of(step * span, span), span)
            total = None
            for index, (source, goal) in enumerate(pair_list(layers)):
                if goal == target:
                    term = jnp.dot(
                        feat_ref[source], dec_ref[index, :, columns], preferred_element_type=jnp.float32
                    )
                    total = term if total is None else total + term
            total = total.astype(jnp.bfloat16)
            places = pl.ds(pl.multiple_of(target * width + step * span, span), span)
            keep_ref[:, places] = total[:half]
            send_ref[:, places] = total[half:]


def forward(even, odd, enc_weight, enc_bias, dec_weight):
    layers, width, tile = enc_weight.shape
    half, wide = even.shape
    side = jax.ShapeDtypeStruct((half, wide), jnp.bfloat16)
    return pl.pallas_call(
        forward_kernel,
        out_shape=(
            side,
            side,
            jax.ShapeDtypeStruct((layers, 2 * half, tile), jnp.bfloat16),
            jax.ShapeDtypeStruct((2 * half, wide), jnp.bfloat16),
        ),
        in_specs=[WHOLE] * 5,
        out_specs=[WHOLE] * 4,
        compiler_params=params(16 * MIB),
        cost_estimate=cost(4 * half * (enc_weight.size + dec_weight.size), 0),
        name="forward",
    )(even, odd, in_vmem(enc_weight), enc_bias, in_vmem(dec_weight))


def turn_kernel(x_ref, feat_ref, x_out, feat_out):
    x_out[...] = x_ref[...].T
    for layer in range(feat_ref.shape[0]):
        feat_out[layer] = feat_ref[layer].T


def turn(x, feats):
    layers, tokens, tile = feats.shape
    return pl.pallas_call(
        turn_kernel,
        out_shape=(
            jax.ShapeDtypeStruct((x.shape[1], tokens), jnp.bfloat16),
            jax.ShapeDtypeStruct((layers, tile, tokens), jnp.bfloat16),
        ),
        in_specs=[WHOLE] * 2,
        out_specs=[WHOLE] * 2,
        compiler_params=params(16 * MIB),
        cost_estimate=cost(2000 * (x.size + feats.size), 0),
        name="turn",
    )(x, feats)


def backward_kernel(
    scale,
    even_ref,
    odd_ref,
    feat_ref,
    feat_t_ref,
    x_t_ref,
    dec_ref,
    enc_out,
    bias_out,
    dec_out,
    e_ref,
    pre_ref,
    stage_dec,
    stage_enc,
    sems_dec,
    sems_enc,
):
    pairs, tile, width = dec_ref.shape
    layers = feat_ref.shape[0]
    half = even_ref.shape[0]
    e_ref[:half] = even_ref[...]
    e_ref[half:] = odd_ref[...]
    chunk = stage_dec.shape[1]
    steps = tile // chunk

    def dec_copy(index, step, slot):
        rows = pl.ds(pl.multiple_of(step * chunk, chunk), chunk)
        return pltpu.make_async_copy(stage_dec.at[slot], dec_out.at[index, rows], sems_dec.at[slot])

    for index, (source, target) in enumerate(pair_list(layers)):

        @pl.loop(0, steps)
        def _(step):
            slot = lax.rem(index * steps + step, SLOTS)

            @pl.when(index * steps + step >= SLOTS)
            def _():
                dec_copy(index, step, slot).wait()

            rows = pl.ds(pl.multiple_of(step * chunk, chunk), chunk)
            value = jnp.dot(
                feat_t_ref[source, rows, :],
                e_ref[:, target * width : (target + 1) * width],
                preferred_element_type=jnp.float32,
            )
            stage_dec[slot] = (scale * value).astype(jnp.bfloat16)
            dec_copy(index, step, slot).start()

    for layer in range(layers):

        @pl.loop(0, steps)
        def _(step):
            columns = pl.ds(pl.multiple_of(step * chunk, chunk), chunk)
            total = None
            for index, (source, target) in enumerate(pair_list(layers)):
                if source == layer:
                    term = lax.dot_general(
                        e_ref[:, target * width : (target + 1) * width],
                        dec_ref[index, columns, :],
                        (((1,), (1,)), ((), ())),
                        preferred_element_type=jnp.float32,
                    )
                    total = term if total is None else total + term
            pre = jnp.where(feat_ref[layer, :, columns] > 0, total, 0.0) * scale
            bias_out[layer : layer + 1, columns] = jnp.sum(pre, axis=0, keepdims=True)
            pre_ref[layer, :, columns] = pre.astype(jnp.bfloat16)

    span = stage_enc.shape[1]
    enc_steps = width // span

    def enc_copy(layer, step, slot):
        rows = pl.ds(pl.multiple_of(step * span, span), span)
        return pltpu.make_async_copy(stage_enc.at[slot], enc_out.at[layer, rows], sems_enc.at[slot])

    for layer in range(layers):

        @pl.loop(0, enc_steps)
        def _(step):
            slot = lax.rem(layer * enc_steps + step, SLOTS)

            @pl.when(layer * enc_steps + step >= SLOTS)
            def _():
                enc_copy(layer, step, slot).wait()

            rows = pl.ds(pl.multiple_of(layer * width + step * span, span), span)
            value = jnp.dot(x_t_ref[rows, :], pre_ref[layer], preferred_element_type=jnp.float32)
            stage_enc[slot] = value.astype(jnp.bfloat16)
            enc_copy(layer, step, slot).start()

    for slot in range(min(SLOTS, pairs * steps)):
        dec_copy(0, 0, slot).wait()
    for slot in range(min(SLOTS, layers * enc_steps)):
        enc_copy(0, 0, slot).wait()


def backward(scale, even, odd, feats, feats_t, x_t, dec_weight):
    layers, tokens, tile = feats.shape
    pairs, _, width = dec_weight.shape
    chunk = min(256, tile)
    span = min(512, width)
    return pl.pallas_call(
        functools.partial(backward_kernel, scale),
        out_shape=(
            jax.ShapeDtypeStruct((layers, width, tile), jnp.bfloat16),
            jax.ShapeDtypeStruct((layers, tile), jnp.float32),
            jax.ShapeDtypeStruct((pairs, tile, width), jnp.bfloat16),
        ),
        in_specs=[WHOLE] * 6,
        out_specs=[HELD, WHOLE, HELD],
        scratch_shapes=[
            pltpu.VMEM((tokens, layers * width), jnp.bfloat16),
            pltpu.VMEM((layers, tokens, tile), jnp.bfloat16),
            pltpu.VMEM((SLOTS, chunk, width), jnp.bfloat16),
            pltpu.VMEM((SLOTS, span, tile), jnp.bfloat16),
            pltpu.SemaphoreType.DMA((SLOTS,)),
            pltpu.SemaphoreType.DMA((SLOTS,)),
        ],
        compiler_params=params(28 * MIB),
        cost_estimate=cost(10 * tokens * dec_weight.size, 0),
        name="backward",
    )(even, odd, feats, feats_t, x_t, in_vmem(dec_weight))


def local(store_inputs, store_targets, row_ids, enc_weight, enc_bias, dec_weight):
    size = lax.axis_size("feat")
    rows = row_ids.shape[0]
    scale = 1.0 / math.sqrt(rows * size)
    picked_in, picked_out = pick(row_ids, store_inputs, store_targets)
    enc_near, dec_near = load_weights(enc_weight, dec_weight)
    even, odd = gather_rows(picked_in, size)
    keep, send, feats, x = forward(even, odd, enc_near, enc_bias, dec_near)
    x_t, feats_t = turn(x, feats)
    own = scatter_sums(keep, send, size, rows)
    errors_own = (own - picked_out.astype(jnp.float32)).astype(jnp.bfloat16)
    even, odd = gather_rows(errors_own, size)
    return backward(scale, even, odd, feats, feats_t, x_t, dec_near)


def solution(mesh):
    in_specs = (
        P(None, ("group", "feat"), None),
        P(None, ("group", "feat"), None),
        P(("group", "feat")),
        P(None, None, "feat"),
        P(None, "feat"),
        P(None, "feat", None),
    )
    out_specs = (P("group", None, "feat"), P("group", "feat"), P("group", "feat", None))
    return jax.shard_map(local, mesh=mesh, in_specs=in_specs, out_specs=out_specs, check_vma=False)
```

time: 123 us -> 85.7 us (0.70)
  matrix products: 38.7 us -> 0 us
  Pallas kernels: 0 us -> 29.8 us
  local copies, waits for them, and re-layouts: 29.7 us -> 2.57 us
  other arithmetic: 3.85 us -> 0.23 us
  waiting for transfers between devices: 20.8 us -> 24 us
    dot_general x10 -> x0, matrix products: 38.7 us -> none  [the longest x3 11.4 us: local(): lax.dot_general(errors[target], dec_weight[index], (((1,), (1,)), ((), ()...]
    pallas_call x0 -> x5, Pallas kernels: none -> 29.8 us  [the longest x1 15.6 us: backward(): pl.pallas_call(functools.partial(backward_kernel, scale), out_shape=(jax....]
    concatenate x5 -> x2, local copies, waits for them, and re-layouts: 11.1 us -> 0.03 us  [gather_rows(): even = jnp.concatenate(parts, axis=0)]
    ppermute x5 -> x0, local copies, waits for them, and re-layouts: 5.79 us -> none  [swap(): lax.ppermute(value, 'feat', [(index, index ^ mask) for index in range(siz...]
    slice x5 -> x1, local copies, waits for them, and re-layouts: 4.78 us -> 0.03 us  [scatter_sums(): pair[slot * rows:(slot + 1) * rows]]
    ppermute x20, waiting for transfers between devices: 20.8 us -> 24 us  [swap(): lax.ppermute(value, 'feat', [(index, index ^ mask) for index in range(siz...]
    gather x2 -> x0, local copies, waits for them, and re-layouts: 2.39 us -> none  [the longest x1 1.65 us: local(): jnp.take(store_inputs, row_ids, axis=1).transpose(1, 0, 2)]
    unnamed x32 -> x17, local copies, waits for them, and re-layouts: 4.48 us -> 2.51 us
  transfers between devices with their start and end apart: 20 -> 20, of which waited for: 10 -> 9; matrix products, arithmetic and copies ran while one was open for 10% -> 0% of each run, Pallas kernels for 0% -> 9%
where the time goes in v2:
time: 85.7 us; the launch traced here: 85.6 us
  Pallas kernels  29.8 us (35%)
  starting transfers between devices  28.2 us (33%)
  waiting for transfers between devices  24 us (28%)
  local copies, waits for them, and re-layouts  2.57 us (3%)
    ppermute x20, starting transfers between devices, swap(): lax.ppermute(value, 'feat', [(index, index ^ mask) for index in range(siz...  28.2 us
    ppermute x20, waiting for transfers between devices, swap(): lax.ppermute(value, 'feat', [(index, index ^ mask) for index in range(siz...  24 us
    pallas_call x1, Pallas kernels, backward(): pl.pallas_call(functools.partial(backward_kernel, scale), out_shape=(jax....  15.6 us
    pallas_call x1, Pallas kernels, load_weights(): pl.pallas_call(load_kernel, out_shape=(pltpu.VMEM(enc_weight.shape, enc_w...  7.1 us
    pallas_call x1, Pallas kernels, forward(): pl.pallas_call(forward_kernel, out_shape=(side, side, jax.ShapeDtypeStruc...  5.9 us
    unnamed x17, local copies, waits for them, and re-layouts  2.51 us
  transfers between devices with their start and end apart: 20, of which 9 were waited for; matrix products, arithmetic and copies ran while one was open for 0% of the time, Pallas kernels for 9%

profile of v2, /device:TPU:0, one launch (start us, length us, event | category | flops | bytes accessed | tf_op | source)
XLA Modules:
  0.0 85.6 jit_solution(11036690716352421271)
XLA Ops:
  0.6 0.0 copy-start
  0.6 0.9 %copy-done = bf16[2,16,2048]{2,1,0:T(8,128)(2,1)S(1)} copy-done((bf16[2,16,2048]{2,1,0:T(8,128)(2,1)S(1)}, bf16[2,16,2048]{2,1,0:T(8,128)(2,1)}, u32[]{:S(2)}) %copy-start) | copy-done | bytes 131096
  1.5 0.0 copy-start.1
  1.5 0.9 %copy-done.1 = bf16[2,16,2048]{2,1,0:T(8,128)(2,1)S(1)} copy-done((bf16[2,16,2048]{2,1,0:T(8,128)(2,1)S(1)}, bf16[2,16,2048]{2,1,0:T(8,128)(2,1)}, u32[]{:S(2)}) %copy-start.1) | copy-done | bytes 131096
  2.4 0.0 copy-start.3
  2.4 0.7 copy-done.3
  3.1 0.0 copy-start.2
  3.1 0.7 pick.1
  3.8 3.1 %collective-permute-start.3 = (bf16[8,4096]{1,0:T(8,128)(2,1)S(1)}, bf16[8,4096]{1,0:T(8,128)(2,1)S(1)}, u32[]{:S(2)}, u32[]{:S(2)}) collective-permute-start(bf16[8,4096]{1,0:T(8,128)(2,1)S(1)} %get-tuple-element.13), channel_id=1, source_target_pairs={{0,2},{1,3},{2,0},{3,1},{4,6},{5,7},{6,4},{7,5},{8,10},{9,11},{10,... | collective-permute-start | bytes 196616 | tf_op jit(solution)/shard_map/ppermute | solution.py:34
  6.9 3.6 %collective-permute-start.2 = (bf16[8,4096]{1,0:T(8,128)(2,1)S(1)}, bf16[8,4096]{1,0:T(8,128)(2,1)S(1)}, u32[]{:S(2)}, u32[]{:S(2)}) collective-permute-start(bf16[8,4096]{1,0:T(8,128)(2,1)S(1)} %get-tuple-element.13), channel_id=1, source_target_pairs={{0,12},{1,13},{2,14},{3,15},{4,8},{5,9},{6,10},{7,11},{8,4},{9,5},... | collective-permute-start | bytes 196616 | tf_op jit(solution)/shard_map/ppermute | solution.py:34
  10.5 0.0 collective-permute-start.1
  10.5 0.8 collective-permute-start
  11.3 2.5 %collective-permute-done.2 = bf16[8,4096]{1,0:T(8,128)(2,1)S(1)} collective-permute-done((bf16[8,4096]{1,0:T(8,128)(2,1)S(1)}, bf16[8,4096]{1,0:T(8,128)(2,1)S(1)}, u32[]{:S(2)}, u32[]{:S(2)}) %collective-permute-start.2) | collective-permute-done | bytes 65568 | tf_op jit(solution)/shard_map/ppermute | solution.py:34
  13.8 2.2 %collective-permute-done.1 = bf16[8,4096]{1,0:T(8,128)(2,1)S(1)} collective-permute-done((bf16[8,4096]{1,0:T(8,128)(2,1)S(1)}, bf16[8,4096]{1,0:T(8,128)(2,1)S(1)}, u32[]{:S(2)}, u32[]{:S(2)}) %collective-permute-start.1) | collective-permute-done | bytes 65568 | tf_op jit(solution)/shard_map/ppermute | solution.py:34
  15.9 0.0 collective-permute-done
  16.0 0.5 collective-permute-start.4
  16.5 0.0 collective-permute-done.3
  16.5 5.8 %collective-permute-done.4 = bf16[24,4096]{1,0:T(8,128)(2,1)S(1)} collective-permute-done((bf16[24,4096]{1,0:T(8,128)(2,1)S(1)}, bf16[24,4096]{1,0:T(8,128)(2,1)S(1)}, u32[]{:S(2)}, u32[]{:S(2)}) %collective-permute-start.4) | collective-permute-done | bytes 196640 | tf_op jit(solution)/shard_map/ppermute | solution.py:34
  22.3 0.1 collective-permute-start.5
  22.4 7.1 %load_weights.1 = (bf16[2,2048,1024]{2,1,0:T(8,128)(2,1)S(1)}, bf16[3,1024,2048]{2,1,0:T(8,128)(2,1)S(1)}) custom-call(bf16[2,2048,1024]{2,1,0:T(8,128)(2,1)} %enc_ref.1, bf16[3,1024,2048]{2,1,0:T(8,128)(2,1)} %dec_ref.1), custom_call_target="tpu_custom_call" | custom-call | flops 4194304000 | bytes 41943040 | tf_op jit(solution)/shard_map/load_weights/pallas_call | solution.py:116
  29.5 0.0 collective-permute-done.5.odd_ref
  29.5 0.0 copy-done.2
  29.5 5.9 %forward.1 = (bf16[64,4096]{1,0:T(8,128)(2,1)S(1)}, bf16[64,4096]{1,0:T(8,128)(2,1)S(1)}, bf16[2,128,1024]{2,1,0:T(8,128)(2,1)S(1)}, bf16[128,4096]{1,0:T(8,128)(2,1)S(1)}) custom-call(bf16[64,4096]{1,0:T(8,128)(2,1)S(1)} %constant_dynamic-update-slice_fusion.even_ref, bf16[64,4096]{1,0:T(8,128)(2,1)S(1)} %collective-permute-done.5.odd_ref, ...), custom_call_target="tpu_custom_call" | custom-call | flops 2684354560 | tf_op jit(solution)/shard_map/forward/pallas_call | solution.py:176
  35.4 0.6 collective-permute-start.6
  36.0 1.5 %collective-permute-done.6 = bf16[64,4096]{1,0:T(8,128)(2,1)S(1)} collective-permute-done((bf16[64,4096]{1,0:T(8,128)(2,1)S(1)}, bf16[64,4096]{1,0:T(8,128)(2,1)S(1)}, u32[]{:S(2)}, u32[]{:S(2)}) %collective-permute-start.6) | collective-permute-done | bytes 524320 | tf_op jit(solution)/shard_map/ppermute | solution.py:34
  37.5 0.1 add_convert_fusion
  37.7 0.4 collective-permute-start.7
  38.1 2.2 %collective-permute-start.13 = (bf16[8,4096]{1,0:T(8,128)(2,1)S(1)}, bf16[8,4096]{1,0:T(8,128)(2,1)S(1)}, u32[]{:S(2)}, u32[]{:S(2)}) collective-permute-start(bf16[8,4096]{1,0:T(8,128)(2,1)S(1)} %get-tuple-element.26), channel_id=1, source_target_pairs={{0,14},{1,15},{2,12},{3,13},{4,10},{5,11},{6,8},{7,9},{8,6},{9,7},... | collective-permute-start | bytes 196616 | tf_op jit(solution)/shard_map/ppermute | solution.py:34
  40.3 1.8 %collective-permute-start.12 = (bf16[8,4096]{1,0:T(8,128)(2,1)S(1)}, bf16[8,4096]{1,0:T(8,128)(2,1)S(1)}, u32[]{:S(2)}, u32[]{:S(2)}) collective-permute-start(bf16[8,4096]{1,0:T(8,128)(2,1)S(1)} %get-tuple-element.27), channel_id=1, source_target_pairs={{0,10},{1,11},{2,8},{3,9},{4,14},{5,15},{6,12},{7,13},{8,2},{9,3},... | collective-permute-start | bytes 196616 | tf_op jit(solution)/shard_map/ppermute | solution.py:34
  42.1 1.2 %collective-permute-start.11 = (bf16[8,4096]{1,0:T(8,128)(2,1)S(1)}, bf16[8,4096]{1,0:T(8,128)(2,1)S(1)}, u32[]{:S(2)}, u32[]{:S(2)}) collective-permute-start(bf16[8,4096]{1,0:T(8,128)(2,1)S(1)} %get-tuple-element.28), channel_id=1, source_target_pairs={{0,6},{1,7},{2,4},{3,5},{4,2},{5,3},{6,0},{7,1},{8,14},{9,15},{10,... | collective-permute-start | bytes 196616 | tf_op jit(solution)/shard_map/ppermute | solution.py:34
  43.4 1.5 %collective-permute-start.10 = (bf16[8,4096]{1,0:T(8,128)(2,1)S(1)}, bf16[8,4096]{1,0:T(8,128)(2,1)S(1)}, u32[]{:S(2)}, u32[]{:S(2)}) collective-permute-start(bf16[8,4096]{1,0:T(8,128)(2,1)S(1)} %get-tuple-element.29), channel_id=1, source_target_pairs={{0,2},{1,3},{2,0},{3,1},{4,6},{5,7},{6,4},{7,5},{8,10},{9,11},{10,... | collective-permute-start | bytes 196616 | tf_op jit(solution)/shard_map/ppermute | solution.py:34
  44.9 0.0 collective-permute-done.7
  44.9 2.2 %collective-permute-start.9 = (bf16[8,4096]{1,0:T(8,128)(2,1)S(1)}, bf16[8,4096]{1,0:T(8,128)(2,1)S(1)}, u32[]{:S(2)}, u32[]{:S(2)}) collective-permute-start(bf16[8,4096]{1,0:T(8,128)(2,1)S(1)} %get-tuple-element.30), channel_id=1, source_target_pairs={{0,12},{1,13},{2,14},{3,15},{4,8},{5,9},{6,10},{7,11},{8,4},{9,5},... | collective-permute-start | bytes 196616 | tf_op jit(solution)/shard_map/ppermute | solution.py:34
  47.1 0.0 collective-permute-done.13
  47.1 1.9 %collective-permute-start.8 = (bf16[8,4096]{1,0:T(8,128)(2,1)S(1)}, bf16[8,4096]{1,0:T(8,128)(2,1)S(1)}, u32[]{:S(2)}, u32[]{:S(2)}) collective-permute-start(bf16[8,4096]{1,0:T(8,128)(2,1)S(1)} %get-tuple-element.31), channel_id=1, source_target_pairs={{0,8},{1,9},{2,10},{3,11},{4,12},{5,13},{6,14},{7,15},{8,0},{9,1},... | collective-permute-start | bytes 196616 | tf_op jit(solution)/shard_map/ppermute | solution.py:34
  49.1 2.0 %collective-permute-done.12 = bf16[8,4096]{1,0:T(8,128)(2,1)S(1)} collective-permute-done((bf16[8,4096]{1,0:T(8,128)(2,1)S(1)}, bf16[8,4096]{1,0:T(8,128)(2,1)S(1)}, u32[]{:S(2)}, u32[]{:S(2)}) %collective-permute-start.12) | collective-permute-done | bytes 65568 | tf_op jit(solution)/shard_map/ppermute | solution.py:34
  51.1 0.0 collective-permute-done.11
  51.1 0.0 collective-permute-done.10
  51.1 0.0 collective-permute-done.9
  51.1 1.4 %collective-permute-done.8 = bf16[8,4096]{1,0:T(8,128)(2,1)S(1)} collective-permute-done((bf16[8,4096]{1,0:T(8,128)(2,1)S(1)}, bf16[8,4096]{1,0:T(8,128)(2,1)S(1)}, u32[]{:S(2)}, u32[]{:S(2)}) %collective-permute-start.8) | collective-permute-done | bytes 65568 | tf_op jit(solution)/shard_map/ppermute | solution.py:34
  52.5 0.1 constant_dynamic-update-slice_fusion.11
  52.6 3.2 %collective-permute-start.16 = (bf16[8,4096]{1,0:T(8,128)(2,1)S(1)}, bf16[8,4096]{1,0:T(8,128)(2,1)S(1)}, u32[]{:S(2)}, u32[]{:S(2)}) collective-permute-start(bf16[8,4096]{1,0:T(8,128)(2,1)S(1)} %get-tuple-element.24), channel_id=1, source_target_pairs={{0,12},{1,13},{2,14},{3,15},{4,8},{5,9},{6,10},{7,11},{8,4},{9,5},... | collective-permute-start | bytes 196616 | tf_op jit(solution)/shard_map/ppermute | solution.py:34
  55.7 0.0 collective-permute-start.15
  55.7 1.3 %collective-permute-start.14 = (bf16[8,4096]{1,0:T(8,128)(2,1)S(1)}, bf16[8,4096]{1,0:T(8,128)(2,1)S(1)}, u32[]{:S(2)}, u32[]{:S(2)}) collective-permute-start(bf16[8,4096]{1,0:T(8,128)(2,1)S(1)} %get-tuple-element.24), channel_id=1, source_target_pairs={{0,4},{1,5},{2,6},{3,7},{4,0},{5,1},{6,2},{7,3},{8,12},{9,13},{10,... | collective-permute-start | bytes 196616 | tf_op jit(solution)/shard_map/ppermute | solution.py:34
  57.0 2.1 %collective-permute-start.17 = (bf16[8,4096]{1,0:T(8,128)(2,1)S(1)}, bf16[8,4096]{1,0:T(8,128)(2,1)S(1)}, u32[]{:S(2)}, u32[]{:S(2)}) collective-permute-start(bf16[8,4096]{1,0:T(8,128)(2,1)S(1)} %get-tuple-element.24), channel_id=1, source_target_pairs={{0,2},{1,3},{2,0},{3,1},{4,6},{5,7},{6,4},{7,5},{8,10},{9,11},{10,... | collective-permute-start | bytes 196616 | tf_op jit(solution)/shard_map/ppermute | solution.py:34
  59.1 0.0 collective-permute-done.16
  59.2 2.2 %collective-permute-done.15 = bf16[8,4096]{1,0:T(8,128)(2,1)S(1)} collective-permute-done((bf16[8,4096]{1,0:T(8,128)(2,1)S(1)}, bf16[8,4096]{1,0:T(8,128)(2,1)S(1)}, u32[]{:S(2)}, u32[]{:S(2)}) %collective-permute-start.15) | collective-permute-done | bytes 65568 | tf_op jit(solution)/shard_map/ppermute | solution.py:34
  61.4 0.0 collective-permute-done.14
  61.4 1.6 %collective-permute-start.18 = (bf16[24,4096]{1,0:T(8,128)(2,1)S(1)}, bf16[24,4096]{1,0:T(8,128)(2,1)S(1)}, u32[]{:S(2)}, u32[]{:S(2)}) collective-permute-start(bf16[24,4096]{1,0:T(8,128)(2,1)S(1)} %pad_maximum_fusion.1), channel_id=1, source_target_pairs={{0,2},{1,3},{2,0},{3,1},{4,6},{5,7},{6,4},{7,5},{8,10},{9,11},{10,... | collective-permute-start | bytes 589832 | tf_op jit(solution)/shard_map/ppermute | solution.py:34
  63.1 0.0 collective-permute-done.17
  63.1 4.9 %collective-permute-done.18 = bf16[24,4096]{1,0:T(8,128)(2,1)S(1)} collective-permute-done((bf16[24,4096]{1,0:T(8,128)(2,1)S(1)}, bf16[24,4096]{1,0:T(8,128)(2,1)S(1)}, u32[]{:S(2)}, u32[]{:S(2)}) %collective-permute-start.18) | collective-permute-done | bytes 196640 | tf_op jit(solution)/shard_map/ppermute | solution.py:34
  68.0 0.1 collective-permute-start.19
  68.1 0.5 turn.1
  68.6 1.4 %collective-permute-done.19.odd_ref = bf16[64,4096]{1,0:T(8,128)(2,1)S(1)} collective-permute-done((bf16[64,4096]{1,0:T(8,128)(2,1)S(1)}, bf16[64,4096]{1,0:T(8,128)(2,1)S(1)}, u32[]{:S(2)}, u32[]{:S(2)}) %collective-permute-start.19) | collective-permute-done | bytes 524320 | tf_op jit(solution)/shard_map/ppermute | solution.py:34
  70.0 15.6 %backward.1 = (bf16[2,2048,1024]{2,1,0:T(8,128)(2,1)}, f32[2,1024]{1,0:T(2,128)}, bf16[3,1024,2048]{2,1,0:T(8,128)(2,1)}) custom-call(bf16[64,4096]{1,0:T(8,128)(2,1)S(1)} %constant_dynamic-update-slice_fusion.6.even_ref, bf16[64,4096]{1,0:T(8,128)(2,1)S(1)} %collective-permute-done.19.odd_ref, bf16[2,128,1024]{2,1,0:T(8,128)(2,1)S(1)} %get-tuple-element.19.feat_ref, ...), custom_call_target="tpu_custom_call" | custom-call | flops 8053063680 | tf_op jit(solution)/shard_map/backward/pallas_call | solution.py:315
  (14 shorter events, 0.1 us)
Async XLA Ops:
  0.6 0.9 %copy-start = (bf16[2,16,2048]{2,1,0:T(8,128)(2,1)S(1)}, bf16[2,16,2048]{2,1,0:T(8,128)(2,1)}, u32[]{:S(2)}) copy-start(bf16[2,16,2048]{2,1,0:T(8,128)(2,1)} %in_ref.1) | copy-start | bytes 393220
  1.5 0.9 %copy-start.1 = (bf16[2,16,2048]{2,1,0:T(8,128)(2,1)S(1)}, bf16[2,16,2048]{2,1,0:T(8,128)(2,1)}, u32[]{:S(2)}) copy-start(bf16[2,16,2048]{2,1,0:T(8,128)(2,1)} %out_ref.1) | copy-start | bytes 393220
  2.4 0.7 copy-start.3
  3.1 26.4 %copy-start.2 = (f32[2,1024]{1,0:T(2,128)S(1)}, f32[2,1024]{1,0:T(2,128)}, u32[]{:S(2)}) copy-start(f32[2,1024]{1,0:T(2,128)} %bias_ref.1) | copy-start | bytes 24580
  3.8 12.6 %collective-permute-start.3 = (bf16[8,4096]{1,0:T(8,128)(2,1)S(1)}, bf16[8,4096]{1,0:T(8,128)(2,1)S(1)}, u32[]{:S(2)}, u32[]{:S(2)}) collective-permute-start(bf16[8,4096]{1,0:T(8,128)(2,1)S(1)} %get-tuple-element.13), channel_id=1, source_target_pairs={{0,2},{1,3},{2,0},{3,1},{4,6},{5,7},{6,4},{7,5},{8,10},{9,11},{10,... | collective-permute-start | bytes 196616 | tf_op jit(solution)/shard_map/ppermute | solution.py:34
  6.9 6.9 %collective-permute-start.2 = (bf16[8,4096]{1,0:T(8,128)(2,1)S(1)}, bf16[8,4096]{1,0:T(8,128)(2,1)S(1)}, u32[]{:S(2)}, u32[]{:S(2)}) collective-permute-start(bf16[8,4096]{1,0:T(8,128)(2,1)S(1)} %get-tuple-element.13), channel_id=1, source_target_pairs={{0,12},{1,13},{2,14},{3,15},{4,8},{5,9},{6,10},{7,11},{8,4},{9,5},... | collective-permute-start | bytes 196616 | tf_op jit(solution)/shard_map/ppermute | solution.py:34
  10.5 5.4 %collective-permute-start.1 = (bf16[8,4096]{1,0:T(8,128)(2,1)S(1)}, bf16[8,4096]{1,0:T(8,128)(2,1)S(1)}, u32[]{:S(2)}, u32[]{:S(2)}) collective-permute-start(bf16[8,4096]{1,0:T(8,128)(2,1)S(1)} %get-tuple-element.13), channel_id=1, source_target_pairs={{0,8},{1,9},{2,10},{3,11},{4,12},{5,13},{6,14},{7,15},{8,0},{9,1},... | collective-permute-start | bytes 196616 | tf_op jit(solution)/shard_map/ppermute | solution.py:34
  10.5 5.4 %collective-permute-start = (bf16[8,4096]{1,0:T(8,128)(2,1)S(1)}, bf16[8,4096]{1,0:T(8,128)(2,1)S(1)}, u32[]{:S(2)}, u32[]{:S(2)}) collective-permute-start(bf16[8,4096]{1,0:T(8,128)(2,1)S(1)} %get-tuple-element.13), channel_id=1, source_target_pairs={{0,4},{1,5},{2,6},{3,7},{4,0},{5,1},{6,2},{7,3},{8,12},{9,13},{10,... | collective-permute-start | bytes 196616 | tf_op jit(solution)/shard_map/ppermute | solution.py:34
  16.0 6.3 %collective-permute-start.4 = (bf16[24,4096]{1,0:T(8,128)(2,1)S(1)}, bf16[24,4096]{1,0:T(8,128)(2,1)S(1)}, u32[]{:S(2)}, u32[]{:S(2)}) collective-permute-start(bf16[24,4096]{1,0:T(8,128)(2,1)S(1)} %pad_maximum_fusion), channel_id=1, source_target_pairs={{0,2},{1,3},{2,0},{3,1},{4,6},{5,7},{6,4},{7,5},{8,10},{9,11},{10,... | collective-permute-start | bytes 589832 | tf_op jit(solution)/shard_map/ppermute | solution.py:34
  22.3 7.2 %collective-permute-start.5 = (bf16[64,4096]{1,0:T(8,128)(2,1)S(1)}, bf16[64,4096]{1,0:T(8,128)(2,1)S(1)}, u32[]{:S(2)}, u32[]{:S(2)}) collective-permute-start(bf16[64,4096]{1,0:T(8,128)(2,1)S(1)} %constant_dynamic-update-slice_fusion.even_ref), channel_id=1, source_target_pairs={{0,1},{1,0},{2,3},{3,2},{4,5},{5,4},{6,7},{7,6},{8,9},{9,8},{10,11... | collective-permute-start | bytes 1572872 | tf_op jit(solution)/shard_map/ppermute | solution.py:34
  35.4 2.1 %collective-permute-start.6 = (bf16[64,4096]{1,0:T(8,128)(2,1)S(1)}, bf16[64,4096]{1,0:T(8,128)(2,1)S(1)}, u32[]{:S(2)}, u32[]{:S(2)}) collective-permute-start(bf16[64,4096]{1,0:T(8,128)(2,1)S(1)} %get-tuple-element.17), channel_id=1, source_target_pairs={{0,1},{1,0},{2,3},{3,2},{4,5},{5,4},{6,7},{7,6},{8,9},{9,8},{10,11... | collective-permute-start | bytes 1572872 | tf_op jit(solution)/shard_map/ppermute | solution.py:34
  37.7 7.2 %collective-permute-start.7 = (bf16[8,4096]{1,0:T(8,128)(2,1)S(1)}, bf16[8,4096]{1,0:T(8,128)(2,1)S(1)}, u32[]{:S(2)}, u32[]{:S(2)}) collective-permute-start(bf16[8,4096]{1,0:T(8,128)(2,1)S(1)} %get-tuple-element.25), channel_id=1, source_target_pairs={{0,4},{1,5},{2,6},{3,7},{4,0},{5,1},{6,2},{7,3},{8,12},{9,13},{10,... | collective-permute-start | bytes 196616 | tf_op jit(solution)/shard_map/ppermute | solution.py:34
  38.1 9.0 %collective-permute-start.13 = (bf16[8,4096]{1,0:T(8,128)(2,1)S(1)}, bf16[8,4096]{1,0:T(8,128)(2,1)S(1)}, u32[]{:S(2)}, u32[]{:S(2)}) collective-permute-start(bf16[8,4096]{1,0:T(8,128)(2,1)S(1)} %get-tuple-element.26), channel_id=1, source_target_pairs={{0,14},{1,15},{2,12},{3,13},{4,10},{5,11},{6,8},{7,9},{8,6},{9,7},... | collective-permute-start | bytes 196616 | tf_op jit(solution)/shard_map/ppermute | solution.py:34
  40.3 10.7 %collective-permute-start.12 = (bf16[8,4096]{1,0:T(8,128)(2,1)S(1)}, bf16[8,4096]{1,0:T(8,128)(2,1)S(1)}, u32[]{:S(2)}, u32[]{:S(2)}) collective-permute-start(bf16[8,4096]{1,0:T(8,128)(2,1)S(1)} %get-tuple-element.27), channel_id=1, source_target_pairs={{0,10},{1,11},{2,8},{3,9},{4,14},{5,15},{6,12},{7,13},{8,2},{9,3},... | collective-permute-start | bytes 196616 | tf_op jit(solution)/shard_map/ppermute | solution.py:34
  42.1 8.9 %collective-permute-start.11 = (bf16[8,4096]{1,0:T(8,128)(2,1)S(1)}, bf16[8,4096]{1,0:T(8,128)(2,1)S(1)}, u32[]{:S(2)}, u32[]{:S(2)}) collective-permute-start(bf16[8,4096]{1,0:T(8,128)(2,1)S(1)} %get-tuple-element.28), channel_id=1, source_target_pairs={{0,6},{1,7},{2,4},{3,5},{4,2},{5,3},{6,0},{7,1},{8,14},{9,15},{10,... | collective-permute-start | bytes 196616 | tf_op jit(solution)/shard_map/ppermute | solution.py:34
  43.4 7.7 %collective-permute-start.10 = (bf16[8,4096]{1,0:T(8,128)(2,1)S(1)}, bf16[8,4096]{1,0:T(8,128)(2,1)S(1)}, u32[]{:S(2)}, u32[]{:S(2)}) collective-permute-start(bf16[8,4096]{1,0:T(8,128)(2,1)S(1)} %get-tuple-element.29), channel_id=1, source_target_pairs={{0,2},{1,3},{2,0},{3,1},{4,6},{5,7},{6,4},{7,5},{8,10},{9,11},{10,... | collective-permute-start | bytes 196616 | tf_op jit(solution)/shard_map/ppermute | solution.py:34
  44.9 6.2 %collective-permute-start.9 = (bf16[8,4096]{1,0:T(8,128)(2,1)S(1)}, bf16[8,4096]{1,0:T(8,128)(2,1)S(1)}, u32[]{:S(2)}, u32[]{:S(2)}) collective-permute-start(bf16[8,4096]{1,0:T(8,128)(2,1)S(1)} %get-tuple-element.30), channel_id=1, source_target_pairs={{0,12},{1,13},{2,14},{3,15},{4,8},{5,9},{6,10},{7,11},{8,4},{9,5},... | collective-permute-start | bytes 196616 | tf_op jit(solution)/shard_map/ppermute | solution.py:34
  47.1 5.3 %collective-permute-start.8 = (bf16[8,4096]{1,0:T(8,128)(2,1)S(1)}, bf16[8,4096]{1,0:T(8,128)(2,1)S(1)}, u32[]{:S(2)}, u32[]{:S(2)}) collective-permute-start(bf16[8,4096]{1,0:T(8,128)(2,1)S(1)} %get-tuple-element.31), channel_id=1, source_target_pairs={{0,8},{1,9},{2,10},{3,11},{4,12},{5,13},{6,14},{7,15},{8,0},{9,1},... | collective-permute-start | bytes 196616 | tf_op jit(solution)/shard_map/ppermute | solution.py:34
  52.6 6.6 %collective-permute-start.16 = (bf16[8,4096]{1,0:T(8,128)(2,1)S(1)}, bf16[8,4096]{1,0:T(8,128)(2,1)S(1)}, u32[]{:S(2)}, u32[]{:S(2)}) collective-permute-start(bf16[8,4096]{1,0:T(8,128)(2,1)S(1)} %get-tuple-element.24), channel_id=1, source_target_pairs={{0,12},{1,13},{2,14},{3,15},{4,8},{5,9},{6,10},{7,11},{8,4},{9,5},... | collective-permute-start | bytes 196616 | tf_op jit(solution)/shard_map/ppermute | solution.py:34
  55.7 5.7 %collective-permute-start.15 = (bf16[8,4096]{1,0:T(8,128)(2,1)S(1)}, bf16[8,4096]{1,0:T(8,128)(2,1)S(1)}, u32[]{:S(2)}, u32[]{:S(2)}) collective-permute-start(bf16[8,4096]{1,0:T(8,128)(2,1)S(1)} %get-tuple-element.24), channel_id=1, source_target_pairs={{0,8},{1,9},{2,10},{3,11},{4,12},{5,13},{6,14},{7,15},{8,0},{9,1},... | collective-permute-start | bytes 196616 | tf_op jit(solution)/shard_map/ppermute | solution.py:34
  55.7 5.7 %collective-permute-start.14 = (bf16[8,4096]{1,0:T(8,128)(2,1)S(1)}, bf16[8,4096]{1,0:T(8,128)(2,1)S(1)}, u32[]{:S(2)}, u32[]{:S(2)}) collective-permute-start(bf16[8,4096]{1,0:T(8,128)(2,1)S(1)} %get-tuple-element.24), channel_id=1, source_target_pairs={{0,4},{1,5},{2,6},{3,7},{4,0},{5,1},{6,2},{7,3},{8,12},{9,13},{10,... | collective-permute-start | bytes 196616 | tf_op jit(solution)/shard_map/ppermute | solution.py:34
  57.0 6.1 %collective-permute-start.17 = (bf16[8,4096]{1,0:T(8,128)(2,1)S(1)}, bf16[8,4096]{1,0:T(8,128)(2,1)S(1)}, u32[]{:S(2)}, u32[]{:S(2)}) collective-permute-start(bf16[8,4096]{1,0:T(8,128)(2,1)S(1)} %get-tuple-element.24), channel_id=1, source_target_pairs={{0,2},{1,3},{2,0},{3,1},{4,6},{5,7},{6,4},{7,5},{8,10},{9,11},{10,... | collective-permute-start | bytes 196616 | tf_op jit(solution)/shard_map/ppermute | solution.py:34
  61.4 6.6 %collective-permute-start.18 = (bf16[24,4096]{1,0:T(8,128)(2,1)S(1)}, bf16[24,4096]{1,0:T(8,128)(2,1)S(1)}, u32[]{:S(2)}, u32[]{:S(2)}) collective-permute-start(bf16[24,4096]{1,0:T(8,128)(2,1)S(1)} %pad_maximum_fusion.1), channel_id=1, source_target_pairs={{0,2},{1,3},{2,0},{3,1},{4,6},{5,7},{6,4},{7,5},{8,10},{9,11},{10,... | collective-permute-start | bytes 589832 | tf_op jit(solution)/shard_map/ppermute | solution.py:34
  68.0 2.0 %collective-permute-start.19 = (bf16[64,4096]{1,0:T(8,128)(2,1)S(1)}, bf16[64,4096]{1,0:T(8,128)(2,1)S(1)}, u32[]{:S(2)}, u32[]{:S(2)}) collective-permute-start(bf16[64,4096]{1,0:T(8,128)(2,1)S(1)} %constant_dynamic-update-slice_fusion.6.even_ref), channel_id=1, source_target_pairs={{0,1},{1,0},{2,3},{3,2},{4,5},{5,4},{6,7},{7,6},{8,9},{9,8},{10,11... | collective-permute-start | bytes 1572872 | tf_op jit(solution)/shard_map/ppermute | solution.py:34

commit v3 on v2

v3 whole, which is shorter than its diff:
```python
import functools
import math

import jax
import jax.numpy as jnp
from jax import lax
from jax.experimental import pallas as pl
from jax.experimental.pallas import tpu as pltpu
from jax.sharding import PartitionSpec as P

MIB = 1 << 20
WHOLE = pl.BlockSpec(memory_space=pltpu.VMEM)
HELD = pl.BlockSpec(memory_space=pl.ANY)


def pair_list(layers):
    return [(source, target) for source in range(layers) for target in range(source, layers)]


def params(limit):
    return pltpu.CompilerParams(vmem_limit_bytes=limit)


def cost(flops, moved):
    return pl.CostEstimate(flops=int(flops), transcendentals=0, bytes_accessed=int(moved))


def in_vmem(array):
    return pltpu.with_memory_space_constraint(array, pltpu.VMEM)


def swap(value, mask, size):
    return lax.ppermute(value, "feat", [(index, index ^ mask) for index in range(size)])


def slot_order(size):
    if size < 4:
        return [0]
    far = list(range(0, size, 4))
    return far + [mask + 2 for mask in far]


def gather_rows(own, size, beside=(), later=None):
    if size < 8:
        even = own if size == 2 else jnp.concatenate([own, swap(own, 2, size)], axis=0)
        return [even, swap(even, 1, size)], beside, later(()) if later else None
    far = [4 * step for step in range(1, size // 4)]
    got = {mask: swap(own, mask, size) for mask in far}
    side = swap(own, 2, size)
    late = [swap(got[far[0]], 2, size)]
    rest, beside = lax.optimization_barrier(([got[mask] for mask in far[1:]], beside))
    late.append(swap(jnp.concatenate(rest, axis=0), 2, size))
    early = jnp.concatenate([own, got[far[0]]] + rest + [side], axis=0)
    early_pair = swap(early, 1, size)
    late = jnp.concatenate(late, axis=0)
    made = None
    if later:
        late, made = lax.optimization_barrier((late, later(rest[:1])))
    return [early, late, early_pair, swap(late, 1, size)], beside, made


def scatter_sums(keep, send, size, rows):
    got = swap(send, 1, size)
    pair = (keep.astype(jnp.float32) + got.astype(jnp.float32)).astype(jnp.bfloat16)
    total = pair[:rows].astype(jnp.float32)
    for slot, mask in enumerate(slot_order(size)):
        if mask:
            total = total + swap(pair[slot * rows : (slot + 1) * rows], mask, size).astype(jnp.float32)
    return total


def pick_kernel(ids_hbm, in_hbm, out_hbm, picked_in, picked_out, ids_ref, in_ref, out_ref, sems):
    layers, buf, width = in_ref.shape
    rows = ids_ref.shape[0]
    copies = [
        pltpu.make_async_copy(ids_hbm, ids_ref, sems.at[0]),
        pltpu.make_async_copy(in_hbm, in_ref, sems.at[1]),
        pltpu.make_async_copy(out_hbm, out_ref, sems.at[2]),
    ]
    for copy in copies:
        copy.start()
    for copy in copies:
        copy.wait()
    place = lax.broadcasted_iota(jnp.int32, (rows, buf), 0)
    wanted = jnp.zeros((rows, buf), jnp.int32)
    for row in range(rows):
        wanted = jnp.where(place == row, ids_ref[row], wanted)
    hot = jnp.where(wanted == lax.broadcasted_iota(jnp.int32, (rows, buf), 1), 1.0, 0.0).astype(jnp.bfloat16)
    for layer in range(layers):
        columns = slice(layer * width, (layer + 1) * width)
        for ref, picked in ((in_ref, picked_in), (out_ref, picked_out)):
            picked[:, columns] = jnp.dot(hot, ref[layer], preferred_element_type=jnp.float32).astype(jnp.bfloat16)


def pick(row_ids, store_inputs, store_targets):
    layers, _, width = store_inputs.shape
    shape = jax.ShapeDtypeStruct((row_ids.shape[0], layers * width), jnp.bfloat16)
    return pl.pallas_call(
        pick_kernel,
        out_shape=(shape, shape),
        in_specs=[HELD] * 3,
        out_specs=[WHOLE, WHOLE],
        scratch_shapes=[
            pltpu.SMEM(row_ids.shape, jnp.int32),
            pltpu.VMEM(store_inputs.shape, jnp.bfloat16),
            pltpu.VMEM(store_targets.shape, jnp.bfloat16),
            pltpu.SemaphoreType.DMA((3,)),
        ],
        compiler_params=params(4 * MIB),
        name="pick",
    )(*(pltpu.with_memory_space_constraint(array, pltpu.HBM) for array in (row_ids, store_inputs, store_targets)))


def load_kernel(ref, *refs):
    out, sems = refs[-2:]
    copies = [
        pltpu.make_async_copy(ref.at[index], out.at[index], sems.at[index]) for index in range(ref.shape[0])
    ]
    for copy in copies:
        copy.start()
    for copy in copies:
        copy.wait()


def load(weight, after=()):
    moved = 4 * weight.size
    return pl.pallas_call(
        load_kernel,
        out_shape=pltpu.VMEM(weight.shape, weight.dtype),
        in_specs=[HELD] * (1 + len(after)),
        out_specs=WHOLE,
        scratch_shapes=[pltpu.SemaphoreType.DMA((weight.shape[0],))],
        compiler_params=params(2 * MIB),
        cost_estimate=cost(moved * 100, moved),
        name="load",
    )(pltpu.with_memory_space_constraint(weight, pltpu.HBM), *after)


def join(part_refs, out_ref):
    start = 0
    for ref in part_refs:
        out_ref[start : start + ref.shape[0]] = ref[...]
        start += ref.shape[0]


def forward_kernel(*refs):
    enc_ref, bias_ref, dec_ref, keep_ref, send_ref, feat_ref, x_ref = refs[-7:]
    layers, width, tile = enc_ref.shape
    half = keep_ref.shape[0]
    join(refs[:-7], x_ref)
    chunk = min(256, tile)
    for layer in range(layers):

        for step in range(tile // chunk):
            columns = pl.ds(step * chunk, chunk)
            value = jnp.dot(
                x_ref[:, layer * width : (layer + 1) * width],
                enc_ref[layer, :, columns],
                preferred_element_type=jnp.float32,
            )
            value = value + bias_ref[layer : layer + 1, columns]
            feat_ref[layer, :, columns] = jnp.maximum(value, 0.0).astype(jnp.bfloat16)

    span = min(512, width)
    for target in range(layers):

        for step in range(width // span):
            columns = pl.ds(step * span, span)
            total = None
            for index, (source, goal) in enumerate(pair_list(layers)):
                if goal == target:
                    term = jnp.dot(
                        feat_ref[source], dec_ref[index, :, columns], preferred_element_type=jnp.float32
                    )
                    total = term if total is None else total + term
            total = total.astype(jnp.bfloat16)
            places = pl.ds(target * width + step * span, span)
            keep_ref[:, places] = total[:half]
            send_ref[:, places] = total[half:]


def forward(parts, enc_weight, enc_bias, dec_weight):
    layers, width, tile = enc_weight.shape
    half, wide = sum(part.shape[0] for part in parts) // 2, parts[0].shape[1]
    side = jax.ShapeDtypeStruct((half, wide), jnp.bfloat16)
    return pl.pallas_call(
        forward_kernel,
        out_shape=(
            side,
            side,
            jax.ShapeDtypeStruct((layers, 2 * half, tile), jnp.bfloat16),
            jax.ShapeDtypeStruct((2 * half, wide), jnp.bfloat16),
        ),
        in_specs=[WHOLE] * (len(parts) + 3),
        out_specs=[WHOLE] * 4,
        compiler_params=params(16 * MIB),
        cost_estimate=cost(4 * half * (enc_weight.size + dec_weight.size), 0),
        name="forward",
    )(*parts, in_vmem(enc_weight), enc_bias, in_vmem(dec_weight))


def turn_kernel(x_ref, feat_ref, x_out, feat_out):
    x_out[...] = x_ref[...].T
    for layer in range(feat_ref.shape[0]):
        feat_out[layer] = feat_ref[layer].T


def turn(x, feats):
    layers, tokens, tile = feats.shape
    return pl.pallas_call(
        turn_kernel,
        out_shape=(
            jax.ShapeDtypeStruct((x.shape[1], tokens), jnp.bfloat16),
            jax.ShapeDtypeStruct((layers, tile, tokens), jnp.bfloat16),
        ),
        in_specs=[WHOLE] * 2,
        out_specs=[WHOLE] * 2,
        compiler_params=params(16 * MIB),
        cost_estimate=cost(2000 * (x.size + feats.size), 0),
        name="turn",
    )(x, feats)


def backward_kernel(scale, *refs):
    parts, refs = refs[:-13], refs[-13:]
    feat_ref, feat_t_ref, x_t_ref, dec_ref, enc_out, bias_out, dec_out = refs[:7]
    e_ref, pre_ref, stage_dec, stage_enc, dec_sem, enc_sem = refs[7:]
    pairs, tile, width = dec_ref.shape
    layers = feat_ref.shape[0]
    pair_of = pair_list(layers)
    join(parts, e_ref)
    chunk = min(256, tile)
    span = min(512, width)

    def dec_step(index, step):
        source, target = pair_of[index]
        place = pl.ds(step * chunk, chunk)
        value = jnp.dot(
            feat_t_ref[source, place, :],
            e_ref[:, target * width : (target + 1) * width],
            preferred_element_type=jnp.float32,
        )
        stage_dec[index, place, :] = (scale * value).astype(jnp.bfloat16)
        pltpu.make_async_copy(stage_dec.at[index, place], dec_out.at[index, place], dec_sem).start()

    def pre_step(layer, step):
        place = pl.ds(step * chunk, chunk)
        total = None
        for index, (source, target) in enumerate(pair_of):
            if source == layer:
                term = lax.dot_general(
                    e_ref[:, target * width : (target + 1) * width],
                    dec_ref[index, place, :],
                    (((1,), (1,)), ((), ())),
                    preferred_element_type=jnp.float32,
                )
                total = term if total is None else total + term
        pre = jnp.where(feat_ref[layer, :, place] > 0, total, 0.0) * scale
        bias_out[layer : layer + 1, place] = jnp.sum(pre, axis=0, keepdims=True)
        pre_ref[layer, :, place] = pre.astype(jnp.bfloat16)

    def enc_step(layer, step):
        place = pl.ds(step * span, span)
        rows = pl.ds(layer * width + step * span, span)
        value = jnp.dot(x_t_ref[rows, :], pre_ref[layer], preferred_element_type=jnp.float32)
        stage_enc[layer, place, :] = value.astype(jnp.bfloat16)
        pltpu.make_async_copy(stage_enc.at[layer, place], enc_out.at[layer, place], enc_sem).start()

    steps, enc_steps = tile // chunk, width // span
    writes = [(dec_step, index, step) for index in reversed(range(pairs)) for step in range(steps)]
    first = 2 * len(writes) // 3
    for step_of, *place in writes[:first]:
        step_of(*place)
    writes = writes[first:]
    for layer in reversed(range(layers)):
        share = -(-len(writes) // steps)
        for step in range(steps):
            pre_step(layer, step)
            if layer < layers - 1:
                for step_of, *place in writes[step * share : (step + 1) * share]:
                    step_of(*place)
        if layer < layers - 1:
            writes = []
        writes = writes + [(enc_step, layer, step) for step in range(enc_steps)]
    for step_of, *place in writes:
        step_of(*place)

    pltpu.make_async_copy(stage_dec, dec_out, dec_sem).wait()
    pltpu.make_async_copy(stage_enc, enc_out, enc_sem).wait()


def backward(scale, parts, feats, feats_t, x_t, dec_weight):
    layers, tokens, tile = feats.shape
    pairs, _, width = dec_weight.shape
    return pl.pallas_call(
        functools.partial(backward_kernel, scale),
        out_shape=(
            jax.ShapeDtypeStruct((layers, width, tile), jnp.bfloat16),
            jax.ShapeDtypeStruct((layers, tile), jnp.float32),
            jax.ShapeDtypeStruct((pairs, tile, width), jnp.bfloat16),
        ),
        in_specs=[WHOLE] * (len(parts) + 4),
        out_specs=[HELD, WHOLE, HELD],
        scratch_shapes=[
            pltpu.VMEM((tokens, layers * width), jnp.bfloat16),
            pltpu.VMEM((layers, tokens, tile), jnp.bfloat16),
            pltpu.VMEM((pairs, tile, width), jnp.bfloat16),
            pltpu.VMEM((layers, width, tile), jnp.bfloat16),
            pltpu.SemaphoreType.DMA,
            pltpu.SemaphoreType.DMA,
        ],
        compiler_params=params(28 * MIB),
        cost_estimate=cost(10 * tokens * dec_weight.size, 0),
        name="backward",
    )(*parts, feats, feats_t, x_t, in_vmem(dec_weight))


def local(store_inputs, store_targets, row_ids, enc_weight, enc_bias, dec_weight):
    size = lax.axis_size("feat")
    rows = row_ids.shape[0]
    scale = 1.0 / math.sqrt(rows * size)
    picked_in, picked_out = pick(row_ids, store_inputs, store_targets)
    parts, enc_near, dec_near = gather_rows(
        picked_in, size, load(enc_weight), functools.partial(load, dec_weight)
    )
    keep, send, feats, x = forward(parts, enc_near, enc_bias, dec_near)
    turned = turn(x, feats)
    own = scatter_sums(keep, send, size, rows)
    errors_own = (own - picked_out.astype(jnp.float32)).astype(jnp.bfloat16)
    parts, (x_t, feats_t), _ = gather_rows(errors_own, size, turned)
    return backward(scale, parts, feats, feats_t, x_t, dec_near)


def solution(mesh):
    in_specs = (
        P(None, ("group", "feat"), None),
        P(None, ("group", "feat"), None),
        P(("group", "feat")),
        P(None, None, "feat"),
        P(None, "feat"),
        P(None, "feat", None),
    )
    out_specs = (P("group", None, "feat"), P("group", "feat"), P("group", "feat", None))
    return jax.shard_map(local, mesh=mesh, in_specs=in_specs, out_specs=out_specs, check_vma=False)
```

time: 85.7 us -> 71.1 us (0.83)
  waiting for transfers between devices: 24 us -> 15.8 us
  Pallas kernels: 29.8 us -> 24 us
  local copies, waits for them, and re-layouts: 2.57 us -> 0.11 us
  starting transfers between devices: 28.2 us -> 30 us
    ppermute x20 -> x24, waiting for transfers between devices: 24 us -> 15.8 us  [swap(): lax.ppermute(value, 'feat', [(index, index ^ mask) for index in range(siz...]
    pallas_call x1, Pallas kernels: 15.6 us -> 11.1 us  [backward(): pl.pallas_call(functools.partial(backward_kernel, scale), out_shape=(jax....]
    pallas_call x1, Pallas kernels: 5.9 us -> 3.02 us  [forward(): pl.pallas_call(forward_kernel, out_shape=(side, side, jax.ShapeDtypeStruc...]
    unnamed x17 -> x10, local copies, waits for them, and re-layouts: 2.51 us -> 0.05 us
    ppermute x20 -> x24, starting transfers between devices: 28.2 us -> 30 us  [swap(): lax.ppermute(value, 'feat', [(index, index ^ mask) for index in range(siz...]
    pallas_call x2 -> x3, Pallas kernels: 7.83 us -> 9.37 us  [the longest x2 8.17 us: load(): pl.pallas_call(load_kernel, out_shape=pltpu.VMEM(weight.shape, weight.dty...]
  transfers between devices with their start and end apart: 20 -> 24, of which waited for: 9 -> 10; matrix products, arithmetic and copies ran while one was open for 0% -> 0% of each run, Pallas kernels for 9% -> 12%
where the time goes in v3:
time: 71.1 us; the launch traced here: 71 us
  starting transfers between devices  30 us (42%)
  Pallas kernels  24 us (34%)
  waiting for transfers between devices  15.8 us (22%)
  between operations  0.83 us (1%)
    ppermute x24, starting transfers between devices, swap(): lax.ppermute(value, 'feat', [(index, index ^ mask) for index in range(siz...  30 us
    ppermute x24, waiting for transfers between devices, swap(): lax.ppermute(value, 'feat', [(index, index ^ mask) for index in range(siz...  15.8 us
    pallas_call x1, Pallas kernels, backward(): pl.pallas_call(functools.partial(backward_kernel, scale), out_shape=(jax....  11.1 us
    pallas_call x2, Pallas kernels, load(): pl.pallas_call(load_kernel, out_shape=pltpu.VMEM(weight.shape, weight.dty...  8.17 us
    pallas_call x1, Pallas kernels, forward(): pl.pallas_call(forward_kernel, out_shape=(side, side, jax.ShapeDtypeStruc...  3.02 us
  transfers between devices with their start and end apart: 24, of which 10 were waited for; matrix products, arithmetic and copies ran while one was open for 0% of the time, Pallas kernels for 12%

profile of v3, /device:TPU:0, one launch (start us, length us, event | category | flops | bytes accessed | tf_op | source)
XLA Modules:
  0.0 71.0 jit_solution(13455146035402182954)
XLA Ops:
  0.6 1.2 %pick.1 = (bf16[8,4096]{1,0:T(8,128)(2,1)S(1)}, bf16[8,4096]{1,0:T(8,128)(2,1)S(1)}) custom-call(s32[8]{0:T(128)} %ids_hbm.1, bf16[2,16,2048]{2,1,0:T(8,128)(2,1)} %in_hbm.1, bf16[2,16,2048]{2,1,0:T(8,128)(2,1)} %out_hbm.1), custom_call_target="tpu_custom_call" | custom-call | tf_op jit(solution)/shard_map/pick/pallas_call | solution.py:98
  1.8 3.1 %collective-permute-start.3 = (bf16[8,4096]{1,0:T(8,128)(2,1)S(1)}, bf16[8,4096]{1,0:T(8,128)(2,1)S(1)}, u32[]{:S(2)}, u32[]{:S(2)}) collective-permute-start(bf16[8,4096]{1,0:T(8,128)(2,1)S(1)} %get-tuple-element.20), channel_id=1, source_target_pairs={{0,2},{1,3},{2,0},{3,1},{4,6},{5,7},{6,4},{7,5},{8,10},{9,11},{10,... | collective-permute-start | bytes 196616 | tf_op jit(solution)/shard_map/ppermute | solution.py:33
  4.9 3.6 %collective-permute-start.2 = (bf16[8,4096]{1,0:T(8,128)(2,1)S(1)}, bf16[8,4096]{1,0:T(8,128)(2,1)S(1)}, u32[]{:S(2)}, u32[]{:S(2)}) collective-permute-start(bf16[8,4096]{1,0:T(8,128)(2,1)S(1)} %get-tuple-element.20), channel_id=1, source_target_pairs={{0,12},{1,13},{2,14},{3,15},{4,8},{5,9},{6,10},{7,11},{8,4},{9,5},... | collective-permute-start | bytes 196616 | tf_op jit(solution)/shard_map/ppermute | solution.py:33
  8.5 0.0 collective-permute-start.1
  8.5 0.8 %collective-permute-start = (bf16[8,4096]{1,0:T(8,128)(2,1)S(1)}, bf16[8,4096]{1,0:T(8,128)(2,1)S(1)}, u32[]{:S(2)}, u32[]{:S(2)}) collective-permute-start(bf16[8,4096]{1,0:T(8,128)(2,1)S(1)} %get-tuple-element.20), channel_id=1, source_target_pairs={{0,4},{1,5},{2,6},{3,7},{4,0},{5,1},{6,2},{7,3},{8,12},{9,13},{10,... | collective-permute-start | bytes 196616 | tf_op jit(solution)/shard_map/ppermute | solution.py:33
  9.3 3.5 %load.2.refs_4_ = bf16[2,2048,1024]{2,1,0:T(8,128)(2,1)S(1)} custom-call(bf16[2,2048,1024]{2,1,0:T(8,128)(2,1)} %ref.2), custom_call_target="tpu_custom_call" | custom-call | flops 1677721600 | bytes 16777216 | tf_op jit(solution)/shard_map/load/pallas_call | solution.py:127
  12.8 0.0 collective-permute-done.2
  12.8 1.1 %collective-permute-done.1.refs_0_ = bf16[8,4096]{1,0:T(8,128)(2,1)S(1)} collective-permute-done((bf16[8,4096]{1,0:T(8,128)(2,1)S(1)}, bf16[8,4096]{1,0:T(8,128)(2,1)S(1)}, u32[]{:S(2)}, u32[]{:S(2)}) %collective-permute-start.1) | collective-permute-done | bytes 65568 | tf_op jit(solution)/shard_map/ppermute | solution.py:33
  13.9 0.0 collective-permute-done
  14.0 0.5 collective-permute-start.5
  14.5 0.0 collective-permute-done.3
  14.5 0.0 copy-start
  14.5 0.1 collective-permute-start.6
  14.6 1.7 %collective-permute-start.4 = (bf16[8,4096]{1,0:T(8,128)(2,1)S(1)}, bf16[8,4096]{1,0:T(8,128)(2,1)S(1)}, u32[]{:S(2)}, u32[]{:S(2)}) collective-permute-start(bf16[8,4096]{1,0:T(8,128)(2,1)S(1)} %collective-permute-done), channel_id=1, source_target_pairs={{0,2},{1,3},{2,0},{3,1},{4,6},{5,7},{6,4},{7,5},{8,10},{9,11},{10,... | collective-permute-start | bytes 196616 | tf_op jit(solution)/shard_map/ppermute | solution.py:33
  16.2 4.7 %load.3.refs_6_.refs_7_ = bf16[3,1024,2048]{2,1,0:T(8,128)(2,1)S(1)} custom-call(bf16[3,1024,2048]{2,1,0:T(8,128)(2,1)} %ref.3, bf16[8,4096]{1,0:T(8,128)(2,1)S(1)} %collective-permute-done.1.refs_0_), custom_call_target="tpu_custom_call" | custom-call | flops 2516582400 | bytes 25165824 | tf_op jit(solution)/shard_map/load/pallas_call | solution.py:127
  20.9 0.0 collective-permute-done.4
  20.9 0.0 collective-permute-done.5
  21.0 0.2 collective-permute-start.7
  21.2 1.3 %collective-permute-done.7.refs_3_ = bf16[24,4096]{1,0:T(8,128)(2,1)S(1)} collective-permute-done((bf16[24,4096]{1,0:T(8,128)(2,1)S(1)}, bf16[24,4096]{1,0:T(8,128)(2,1)S(1)}, u32[]{:S(2)}, u32[]{:S(2)}) %collective-permute-start.7) | collective-permute-done | bytes 196640 | tf_op jit(solution)/shard_map/ppermute | solution.py:33
  22.5 0.0 collective-permute-done.6.refs_2_
  22.5 0.0 copy-done
  22.5 3.0 %forward.1 = (bf16[64,4096]{1,0:T(8,128)(2,1)S(1)}, bf16[64,4096]{1,0:T(8,128)(2,1)S(1)}, bf16[2,128,1024]{2,1,0:T(8,128)(2,1)S(1)}, bf16[128,4096]{1,0:T(8,128)(2,1)S(1)}) custom-call(bf16[40,4096]{1,0:T(8,128)(2,1)S(1)} %constant_dynamic-update-slice_fusion.refs_0_, bf16[24,4096]{1,0:T(8,128)(2,1)S(1)} %pad_maximum_fusion.refs_1_, ...), custom_call_target="tpu_custom_call" | custom-call | flops 2684354560 | tf_op jit(solution)/shard_map/forward/pallas_call | solution.py:186
  25.5 0.2 collective-permute-start.8
  25.7 1.8 %collective-permute-done.8 = bf16[64,4096]{1,0:T(8,128)(2,1)S(1)} collective-permute-done((bf16[64,4096]{1,0:T(8,128)(2,1)S(1)}, bf16[64,4096]{1,0:T(8,128)(2,1)S(1)}, u32[]{:S(2)}, u32[]{:S(2)}) %collective-permute-start.8) | collective-permute-done | bytes 524320 | tf_op jit(solution)/shard_map/ppermute | solution.py:33
  27.5 0.1 add_convert_fusion
  27.7 1.0 %collective-permute-start.9 = (bf16[8,4096]{1,0:T(8,128)(2,1)S(1)}, bf16[8,4096]{1,0:T(8,128)(2,1)S(1)}, u32[]{:S(2)}, u32[]{:S(2)}) collective-permute-start(bf16[8,4096]{1,0:T(8,128)(2,1)S(1)} %get-tuple-element.39), channel_id=1, source_target_pairs={{0,4},{1,5},{2,6},{3,7},{4,0},{5,1},{6,2},{7,3},{8,12},{9,13},{10,... | collective-permute-start | bytes 196616 | tf_op jit(solution)/shard_map/ppermute | solution.py:33
  28.7 2.2 %collective-permute-start.15 = (bf16[8,4096]{1,0:T(8,128)(2,1)S(1)}, bf16[8,4096]{1,0:T(8,128)(2,1)S(1)}, u32[]{:S(2)}, u32[]{:S(2)}) collective-permute-start(bf16[8,4096]{1,0:T(8,128)(2,1)S(1)} %get-tuple-element.40), channel_id=1, source_target_pairs={{0,14},{1,15},{2,12},{3,13},{4,10},{5,11},{6,8},{7,9},{8,6},{9,7},... | collective-permute-start | bytes 196616 | tf_op jit(solution)/shard_map/ppermute | solution.py:33
  30.9 1.2 %collective-permute-start.14 = (bf16[8,4096]{1,0:T(8,128)(2,1)S(1)}, bf16[8,4096]{1,0:T(8,128)(2,1)S(1)}, u32[]{:S(2)}, u32[]{:S(2)}) collective-permute-start(bf16[8,4096]{1,0:T(8,128)(2,1)S(1)} %get-tuple-element.41), channel_id=1, source_target_pairs={{0,10},{1,11},{2,8},{3,9},{4,14},{5,15},{6,12},{7,13},{8,2},{9,3},... | collective-permute-start | bytes 196616 | tf_op jit(solution)/shard_map/ppermute | solution.py:33
  32.1 1.8 %collective-permute-start.13 = (bf16[8,4096]{1,0:T(8,128)(2,1)S(1)}, bf16[8,4096]{1,0:T(8,128)(2,1)S(1)}, u32[]{:S(2)}, u32[]{:S(2)}) collective-permute-start(bf16[8,4096]{1,0:T(8,128)(2,1)S(1)} %get-tuple-element.42), channel_id=1, source_target_pairs={{0,6},{1,7},{2,4},{3,5},{4,2},{5,3},{6,0},{7,1},{8,14},{9,15},{10,... | collective-permute-start | bytes 196616 | tf_op jit(solution)/shard_map/ppermute | solution.py:33
  33.9 1.5 %collective-permute-start.12 = (bf16[8,4096]{1,0:T(8,128)(2,1)S(1)}, bf16[8,4096]{1,0:T(8,128)(2,1)S(1)}, u32[]{:S(2)}, u32[]{:S(2)}) collective-permute-start(bf16[8,4096]{1,0:T(8,128)(2,1)S(1)} %get-tuple-element.43), channel_id=1, source_target_pairs={{0,2},{1,3},{2,0},{3,1},{4,6},{5,7},{6,4},{7,5},{8,10},{9,11},{10,... | collective-permute-start | bytes 196616 | tf_op jit(solution)/shard_map/ppermute | solution.py:33
  35.5 0.0 collective-permute-done.9
  35.5 2.2 %collective-permute-start.11 = (bf16[8,4096]{1,0:T(8,128)(2,1)S(1)}, bf16[8,4096]{1,0:T(8,128)(2,1)S(1)}, u32[]{:S(2)}, u32[]{:S(2)}) collective-permute-start(bf16[8,4096]{1,0:T(8,128)(2,1)S(1)} %get-tuple-element.44), channel_id=1, source_target_pairs={{0,12},{1,13},{2,14},{3,15},{4,8},{5,9},{6,10},{7,11},{8,4},{9,5},... | collective-permute-start | bytes 196616 | tf_op jit(solution)/shard_map/ppermute | solution.py:33
  37.7 0.0 collective-permute-done.15
  37.7 2.0 %collective-permute-start.10 = (bf16[8,4096]{1,0:T(8,128)(2,1)S(1)}, bf16[8,4096]{1,0:T(8,128)(2,1)S(1)}, u32[]{:S(2)}, u32[]{:S(2)}) collective-permute-start(bf16[8,4096]{1,0:T(8,128)(2,1)S(1)} %get-tuple-element.45), channel_id=1, source_target_pairs={{0,8},{1,9},{2,10},{3,11},{4,12},{5,13},{6,14},{7,15},{8,0},{9,1},... | collective-permute-start | bytes 196616 | tf_op jit(solution)/shard_map/ppermute | solution.py:33
  39.7 0.0 collective-permute-done.14
  39.7 0.0 collective-permute-done.13
  39.7 0.2 collective-permute-done.12
  39.8 1.8 %collective-permute-done.11 = bf16[8,4096]{1,0:T(8,128)(2,1)S(1)} collective-permute-done((bf16[8,4096]{1,0:T(8,128)(2,1)S(1)}, bf16[8,4096]{1,0:T(8,128)(2,1)S(1)}, u32[]{:S(2)}, u32[]{:S(2)}) %collective-permute-start.11) | collective-permute-done | bytes 65568 | tf_op jit(solution)/shard_map/ppermute | solution.py:33
  41.6 2.0 %collective-permute-done.10 = bf16[8,4096]{1,0:T(8,128)(2,1)S(1)} collective-permute-done((bf16[8,4096]{1,0:T(8,128)(2,1)S(1)}, bf16[8,4096]{1,0:T(8,128)(2,1)S(1)}, u32[]{:S(2)}, u32[]{:S(2)}) %collective-permute-start.10) | collective-permute-done | bytes 65568 | tf_op jit(solution)/shard_map/ppermute | solution.py:33
  43.6 0.1 constant_dynamic-update-slice_fusion.9
  43.7 1.6 %collective-permute-start.18 = (bf16[8,4096]{1,0:T(8,128)(2,1)S(1)}, bf16[8,4096]{1,0:T(8,128)(2,1)S(1)}, u32[]{:S(2)}, u32[]{:S(2)}) collective-permute-start(bf16[8,4096]{1,0:T(8,128)(2,1)S(1)} %get-tuple-element.38), channel_id=1, source_target_pairs={{0,12},{1,13},{2,14},{3,15},{4,8},{5,9},{6,10},{7,11},{8,4},{9,5},... | collective-permute-start | bytes 196616 | tf_op jit(solution)/shard_map/ppermute | solution.py:33
  45.2 0.2 collective-permute-start.17
  45.4 2.7 %collective-permute-start.16 = (bf16[8,4096]{1,0:T(8,128)(2,1)S(1)}, bf16[8,4096]{1,0:T(8,128)(2,1)S(1)}, u32[]{:S(2)}, u32[]{:S(2)}) collective-permute-start(bf16[8,4096]{1,0:T(8,128)(2,1)S(1)} %get-tuple-element.38), channel_id=1, source_target_pairs={{0,4},{1,5},{2,6},{3,7},{4,0},{5,1},{6,2},{7,3},{8,12},{9,13},{10,... | collective-permute-start | bytes 196616 | tf_op jit(solution)/shard_map/ppermute | solution.py:33
  48.1 0.5 turn.1
  48.6 1.2 %collective-permute-start.19 = (bf16[8,4096]{1,0:T(8,128)(2,1)S(1)}, bf16[8,4096]{1,0:T(8,128)(2,1)S(1)}, u32[]{:S(2)}, u32[]{:S(2)}) collective-permute-start(bf16[8,4096]{1,0:T(8,128)(2,1)S(1)} %get-tuple-element.38), channel_id=1, source_target_pairs={{0,2},{1,3},{2,0},{3,1},{4,6},{5,7},{6,4},{7,5},{8,10},{9,11},{10,... | collective-permute-start | bytes 196616 | tf_op jit(solution)/shard_map/ppermute | solution.py:33
  49.8 0.4 collective-permute-done.18
  50.2 1.3 %collective-permute-done.17 = bf16[8,4096]{1,0:T(8,128)(2,1)S(1)} collective-permute-done((bf16[8,4096]{1,0:T(8,128)(2,1)S(1)}, bf16[8,4096]{1,0:T(8,128)(2,1)S(1)}, u32[]{:S(2)}, u32[]{:S(2)}) %collective-permute-start.17) | collective-permute-done | bytes 65568 | tf_op jit(solution)/shard_map/ppermute | solution.py:33
  51.5 0.0 collective-permute-done.16
  51.6 1.9 %collective-permute-start.21 = (bf16[16,4096]{1,0:T(8,128)(2,1)S(1)}, bf16[16,4096]{1,0:T(8,128)(2,1)S(1)}, u32[]{:S(2)}, u32[]{:S(2)}) collective-permute-start(bf16[16,4096]{1,0:T(8,128)(2,1)S(1)} %pad_maximum_fusion.2), channel_id=1, source_target_pairs={{0,2},{1,3},{2,0},{3,1},{4,6},{5,7},{6,4},{7,5},{8,10},{9,11},{10,... | collective-permute-start | bytes 393224 | tf_op jit(solution)/shard_map/ppermute | solution.py:33
  53.4 0.2 collective-permute-start.20
  53.6 0.0 collective-permute-done.19
  53.7 0.1 collective-permute-start.22
  53.7 4.6 %collective-permute-done.20 = bf16[8,4096]{1,0:T(8,128)(2,1)S(1)} collective-permute-done((bf16[8,4096]{1,0:T(8,128)(2,1)S(1)}, bf16[8,4096]{1,0:T(8,128)(2,1)S(1)}, u32[]{:S(2)}, u32[]{:S(2)}) %collective-permute-start.20) | collective-permute-done | bytes 65568 | tf_op jit(solution)/shard_map/ppermute | solution.py:33
  58.3 0.0 collective-permute-done.21
  58.3 0.1 collective-permute-start.23
  58.4 1.4 %collective-permute-done.23.refs_3_ = bf16[24,4096]{1,0:T(8,128)(2,1)S(1)} collective-permute-done((bf16[24,4096]{1,0:T(8,128)(2,1)S(1)}, bf16[24,4096]{1,0:T(8,128)(2,1)S(1)}, u32[]{:S(2)}, u32[]{:S(2)}) %collective-permute-start.23) | collective-permute-done | bytes 196640 | tf_op jit(solution)/shard_map/ppermute | solution.py:33
  59.8 0.0 collective-permute-done.22.refs_2_
  59.9 11.1 %backward.1 = (bf16[2,2048,1024]{2,1,0:T(8,128)(2,1)}, f32[2,1024]{1,0:T(2,128)}, bf16[3,1024,2048]{2,1,0:T(8,128)(2,1)}) custom-call(bf16[40,4096]{1,0:T(8,128)(2,1)S(1)} %constant_dynamic-update-slice_fusion.5.refs_0_, bf16[24,4096]{1,0:T(8,128)(2,1)S(1)} %constant_dynamic-update-slice_fusion.10.refs_1_, ...), custom_call_target="tpu_custom_call" | custom-call | flops 8053063680 | tf_op jit(solution)/shard_map/backward/pallas_call | solution.py:295
  (15 shorter events, 0.1 us)
Async XLA Ops:
  1.8 12.6 %collective-permute-start.3 = (bf16[8,4096]{1,0:T(8,128)(2,1)S(1)}, bf16[8,4096]{1,0:T(8,128)(2,1)S(1)}, u32[]{:S(2)}, u32[]{:S(2)}) collective-permute-start(bf16[8,4096]{1,0:T(8,128)(2,1)S(1)} %get-tuple-element.20), channel_id=1, source_target_pairs={{0,2},{1,3},{2,0},{3,1},{4,6},{5,7},{6,4},{7,5},{8,10},{9,11},{10,... | collective-permute-start | bytes 196616 | tf_op jit(solution)/shard_map/ppermute | solution.py:33
  4.9 7.9 %collective-permute-start.2 = (bf16[8,4096]{1,0:T(8,128)(2,1)S(1)}, bf16[8,4096]{1,0:T(8,128)(2,1)S(1)}, u32[]{:S(2)}, u32[]{:S(2)}) collective-permute-start(bf16[8,4096]{1,0:T(8,128)(2,1)S(1)} %get-tuple-element.20), channel_id=1, source_target_pairs={{0,12},{1,13},{2,14},{3,15},{4,8},{5,9},{6,10},{7,11},{8,4},{9,5},... | collective-permute-start | bytes 196616 | tf_op jit(solution)/shard_map/ppermute | solution.py:33
  8.5 5.4 %collective-permute-start.1 = (bf16[8,4096]{1,0:T(8,128)(2,1)S(1)}, bf16[8,4096]{1,0:T(8,128)(2,1)S(1)}, u32[]{:S(2)}, u32[]{:S(2)}) collective-permute-start(bf16[8,4096]{1,0:T(8,128)(2,1)S(1)} %get-tuple-element.20), channel_id=1, source_target_pairs={{0,8},{1,9},{2,10},{3,11},{4,12},{5,13},{6,14},{7,15},{8,0},{9,1},... | collective-permute-start | bytes 196616 | tf_op jit(solution)/shard_map/ppermute | solution.py:33
  8.5 5.4 %collective-permute-start = (bf16[8,4096]{1,0:T(8,128)(2,1)S(1)}, bf16[8,4096]{1,0:T(8,128)(2,1)S(1)}, u32[]{:S(2)}, u32[]{:S(2)}) collective-permute-start(bf16[8,4096]{1,0:T(8,128)(2,1)S(1)} %get-tuple-element.20), channel_id=1, source_target_pairs={{0,4},{1,5},{2,6},{3,7},{4,0},{5,1},{6,2},{7,3},{8,12},{9,13},{10,... | collective-permute-start | bytes 196616 | tf_op jit(solution)/shard_map/ppermute | solution.py:33
  14.0 7.0 %collective-permute-start.5 = (bf16[16,4096]{1,0:T(8,128)(2,1)S(1)}, bf16[16,4096]{1,0:T(8,128)(2,1)S(1)}, u32[]{:S(2)}, u32[]{:S(2)}) collective-permute-start(bf16[16,4096]{1,0:T(8,128)(2,1)S(1)} %pad_maximum_fusion.1), channel_id=1, source_target_pairs={{0,2},{1,3},{2,0},{3,1},{4,6},{5,7},{6,4},{7,5},{8,10},{9,11},{10,... | collective-permute-start | bytes 393224 | tf_op jit(solution)/shard_map/ppermute | solution.py:33
  14.5 8.0 %copy-start = (f32[2,1024]{1,0:T(2,128)S(1)}, f32[2,1024]{1,0:T(2,128)}, u32[]{:S(2)}) copy-start(f32[2,1024]{1,0:T(2,128)} %refs_5_.1) | copy-start | bytes 24580
  14.5 8.0 %collective-permute-start.6 = (bf16[40,4096]{1,0:T(8,128)(2,1)S(1)}, bf16[40,4096]{1,0:T(8,128)(2,1)S(1)}, u32[]{:S(2)}, u32[]{:S(2)}) collective-permute-start(bf16[40,4096]{1,0:T(8,128)(2,1)S(1)} %constant_dynamic-update-slice_fusion.refs_0_), channel_id=1, source_target_pairs={{0,1},{1,0},{2,3},{3,2},{4,5},{5,4},{6,7},{7,6},{8,9},{9,8},{10,11... | collective-permute-start | bytes 983048 | tf_op jit(solution)/shard_map/ppermute | solution.py:33
  14.6 6.4 %collective-permute-start.4 = (bf16[8,4096]{1,0:T(8,128)(2,1)S(1)}, bf16[8,4096]{1,0:T(8,128)(2,1)S(1)}, u32[]{:S(2)}, u32[]{:S(2)}) collective-permute-start(bf16[8,4096]{1,0:T(8,128)(2,1)S(1)} %collective-permute-done), channel_id=1, source_target_pairs={{0,2},{1,3},{2,0},{3,1},{4,6},{5,7},{6,4},{7,5},{8,10},{9,11},{10,... | collective-permute-start | bytes 196616 | tf_op jit(solution)/shard_map/ppermute | solution.py:33
  21.0 1.5 %collective-permute-start.7 = (bf16[24,4096]{1,0:T(8,128)(2,1)S(1)}, bf16[24,4096]{1,0:T(8,128)(2,1)S(1)}, u32[]{:S(2)}, u32[]{:S(2)}) collective-permute-start(bf16[24,4096]{1,0:T(8,128)(2,1)S(1)} %pad_maximum_fusion.refs_1_), channel_id=1, source_target_pairs={{0,1},{1,0},{2,3},{3,2},{4,5},{5,4},{6,7},{7,6},{8,9},{9,8},{10,11... | collective-permute-start | bytes 589832 | tf_op jit(solution)/shard_map/ppermute | solution.py:33
  25.5 2.0 %collective-permute-start.8 = (bf16[64,4096]{1,0:T(8,128)(2,1)S(1)}, bf16[64,4096]{1,0:T(8,128)(2,1)S(1)}, u32[]{:S(2)}, u32[]{:S(2)}) collective-permute-start(bf16[64,4096]{1,0:T(8,128)(2,1)S(1)} %get-tuple-element.27), channel_id=1, source_target_pairs={{0,1},{1,0},{2,3},{3,2},{4,5},{5,4},{6,7},{7,6},{8,9},{9,8},{10,11... | collective-permute-start | bytes 1572872 | tf_op jit(solution)/shard_map/ppermute | solution.py:33
  27.7 7.8 %collective-permute-start.9 = (bf16[8,4096]{1,0:T(8,128)(2,1)S(1)}, bf16[8,4096]{1,0:T(8,128)(2,1)S(1)}, u32[]{:S(2)}, u32[]{:S(2)}) collective-permute-start(bf16[8,4096]{1,0:T(8,128)(2,1)S(1)} %get-tuple-element.39), channel_id=1, source_target_pairs={{0,4},{1,5},{2,6},{3,7},{4,0},{5,1},{6,2},{7,3},{8,12},{9,13},{10,... | collective-permute-start | bytes 196616 | tf_op jit(solution)/shard_map/ppermute | solution.py:33
  28.7 9.0 %collective-permute-start.15 = (bf16[8,4096]{1,0:T(8,128)(2,1)S(1)}, bf16[8,4096]{1,0:T(8,128)(2,1)S(1)}, u32[]{:S(2)}, u32[]{:S(2)}) collective-permute-start(bf16[8,4096]{1,0:T(8,128)(2,1)S(1)} %get-tuple-element.40), channel_id=1, source_target_pairs={{0,14},{1,15},{2,12},{3,13},{4,10},{5,11},{6,8},{7,9},{8,6},{9,7},... | collective-permute-start | bytes 196616 | tf_op jit(solution)/shard_map/ppermute | solution.py:33
  30.9 8.8 %collective-permute-start.14 = (bf16[8,4096]{1,0:T(8,128)(2,1)S(1)}, bf16[8,4096]{1,0:T(8,128)(2,1)S(1)}, u32[]{:S(2)}, u32[]{:S(2)}) collective-permute-start(bf16[8,4096]{1,0:T(8,128)(2,1)S(1)} %get-tuple-element.41), channel_id=1, source_target_pairs={{0,10},{1,11},{2,8},{3,9},{4,14},{5,15},{6,12},{7,13},{8,2},{9,3},... | collective-permute-start | bytes 196616 | tf_op jit(solution)/shard_map/ppermute | solution.py:33
  32.1 7.5 %collective-permute-start.13 = (bf16[8,4096]{1,0:T(8,128)(2,1)S(1)}, bf16[8,4096]{1,0:T(8,128)(2,1)S(1)}, u32[]{:S(2)}, u32[]{:S(2)}) collective-permute-start(bf16[8,4096]{1,0:T(8,128)(2,1)S(1)} %get-tuple-element.42), channel_id=1, source_target_pairs={{0,6},{1,7},{2,4},{3,5},{4,2},{5,3},{6,0},{7,1},{8,14},{9,15},{10,... | collective-permute-start | bytes 196616 | tf_op jit(solution)/shard_map/ppermute | solution.py:33
  33.9 5.9 %collective-permute-start.12 = (bf16[8,4096]{1,0:T(8,128)(2,1)S(1)}, bf16[8,4096]{1,0:T(8,128)(2,1)S(1)}, u32[]{:S(2)}, u32[]{:S(2)}) collective-permute-start(bf16[8,4096]{1,0:T(8,128)(2,1)S(1)} %get-tuple-element.43), channel_id=1, source_target_pairs={{0,2},{1,3},{2,0},{3,1},{4,6},{5,7},{6,4},{7,5},{8,10},{9,11},{10,... | collective-permute-start | bytes 196616 | tf_op jit(solution)/shard_map/ppermute | solution.py:33
  35.5 6.2 %collective-permute-start.11 = (bf16[8,4096]{1,0:T(8,128)(2,1)S(1)}, bf16[8,4096]{1,0:T(8,128)(2,1)S(1)}, u32[]{:S(2)}, u32[]{:S(2)}) collective-permute-start(bf16[8,4096]{1,0:T(8,128)(2,1)S(1)} %get-tuple-element.44), channel_id=1, source_target_pairs={{0,12},{1,13},{2,14},{3,15},{4,8},{5,9},{6,10},{7,11},{8,4},{9,5},... | collective-permute-start | bytes 196616 | tf_op jit(solution)/shard_map/ppermute | solution.py:33
  37.7 5.9 %collective-permute-start.10 = (bf16[8,4096]{1,0:T(8,128)(2,1)S(1)}, bf16[8,4096]{1,0:T(8,128)(2,1)S(1)}, u32[]{:S(2)}, u32[]{:S(2)}) collective-permute-start(bf16[8,4096]{1,0:T(8,128)(2,1)S(1)} %get-tuple-element.45), channel_id=1, source_target_pairs={{0,8},{1,9},{2,10},{3,11},{4,12},{5,13},{6,14},{7,15},{8,0},{9,1},... | collective-permute-start | bytes 196616 | tf_op jit(solution)/shard_map/ppermute | solution.py:33
  43.7 6.6 %collective-permute-start.18 = (bf16[8,4096]{1,0:T(8,128)(2,1)S(1)}, bf16[8,4096]{1,0:T(8,128)(2,1)S(1)}, u32[]{:S(2)}, u32[]{:S(2)}) collective-permute-start(bf16[8,4096]{1,0:T(8,128)(2,1)S(1)} %get-tuple-element.38), channel_id=1, source_target_pairs={{0,12},{1,13},{2,14},{3,15},{4,8},{5,9},{6,10},{7,11},{8,4},{9,5},... | collective-permute-start | bytes 196616 | tf_op jit(solution)/shard_map/ppermute | solution.py:33
  45.2 6.3 %collective-permute-start.17 = (bf16[8,4096]{1,0:T(8,128)(2,1)S(1)}, bf16[8,4096]{1,0:T(8,128)(2,1)S(1)}, u32[]{:S(2)}, u32[]{:S(2)}) collective-permute-start(bf16[8,4096]{1,0:T(8,128)(2,1)S(1)} %get-tuple-element.38), channel_id=1, source_target_pairs={{0,8},{1,9},{2,10},{3,11},{4,12},{5,13},{6,14},{7,15},{8,0},{9,1},... | collective-permute-start | bytes 196616 | tf_op jit(solution)/shard_map/ppermute | solution.py:33
  45.4 6.1 %collective-permute-start.16 = (bf16[8,4096]{1,0:T(8,128)(2,1)S(1)}, bf16[8,4096]{1,0:T(8,128)(2,1)S(1)}, u32[]{:S(2)}, u32[]{:S(2)}) collective-permute-start(bf16[8,4096]{1,0:T(8,128)(2,1)S(1)} %get-tuple-element.38), channel_id=1, source_target_pairs={{0,4},{1,5},{2,6},{3,7},{4,0},{5,1},{6,2},{7,3},{8,12},{9,13},{10,... | collective-permute-start | bytes 196616 | tf_op jit(solution)/shard_map/ppermute | solution.py:33
  48.6 5.1 %collective-permute-start.19 = (bf16[8,4096]{1,0:T(8,128)(2,1)S(1)}, bf16[8,4096]{1,0:T(8,128)(2,1)S(1)}, u32[]{:S(2)}, u32[]{:S(2)}) collective-permute-start(bf16[8,4096]{1,0:T(8,128)(2,1)S(1)} %get-tuple-element.38), channel_id=1, source_target_pairs={{0,2},{1,3},{2,0},{3,1},{4,6},{5,7},{6,4},{7,5},{8,10},{9,11},{10,... | collective-permute-start | bytes 196616 | tf_op jit(solution)/shard_map/ppermute | solution.py:33
  51.6 6.8 %collective-permute-start.21 = (bf16[16,4096]{1,0:T(8,128)(2,1)S(1)}, bf16[16,4096]{1,0:T(8,128)(2,1)S(1)}, u32[]{:S(2)}, u32[]{:S(2)}) collective-permute-start(bf16[16,4096]{1,0:T(8,128)(2,1)S(1)} %pad_maximum_fusion.2), channel_id=1, source_target_pairs={{0,2},{1,3},{2,0},{3,1},{4,6},{5,7},{6,4},{7,5},{8,10},{9,11},{10,... | collective-permute-start | bytes 393224 | tf_op jit(solution)/shard_map/ppermute | solution.py:33
  53.4 4.9 %collective-permute-start.20 = (bf16[8,4096]{1,0:T(8,128)(2,1)S(1)}, bf16[8,4096]{1,0:T(8,128)(2,1)S(1)}, u32[]{:S(2)}, u32[]{:S(2)}) collective-permute-start(bf16[8,4096]{1,0:T(8,128)(2,1)S(1)} %collective-permute-done.16), channel_id=1, source_target_pairs={{0,2},{1,3},{2,0},{3,1},{4,6},{5,7},{6,4},{7,5},{8,10},{9,11},{10,... | collective-permute-start | bytes 196616 | tf_op jit(solution)/shard_map/ppermute | solution.py:33
  53.7 6.2 %collective-permute-start.22 = (bf16[40,4096]{1,0:T(8,128)(2,1)S(1)}, bf16[40,4096]{1,0:T(8,128)(2,1)S(1)}, u32[]{:S(2)}, u32[]{:S(2)}) collective-permute-start(bf16[40,4096]{1,0:T(8,128)(2,1)S(1)} %constant_dynamic-update-slice_fusion.5.refs_0_), channel_id=1, source_target_pairs={{0,1},{1,0},{2,3},{3,2},{4,5},{5,4},{6,7},{7,6},{8,9},{9,8},{10,11... | collective-permute-start | bytes 983048 | tf_op jit(solution)/shard_map/ppermute | solution.py:33
  58.3 1.5 %collective-permute-start.23 = (bf16[24,4096]{1,0:T(8,128)(2,1)S(1)}, bf16[24,4096]{1,0:T(8,128)(2,1)S(1)}, u32[]{:S(2)}, u32[]{:S(2)}) collective-permute-start(bf16[24,4096]{1,0:T(8,128)(2,1)S(1)} %constant_dynamic-update-slice_fusion.10.refs_1_), channel_id=1, source_target_pairs={{0,1},{1,0},{2,3},{3,2},{4,5},{5,4},{6,7},{7,6},{8,9},{9,8},{10,11... | collective-permute-start | bytes 589832 | tf_op jit(solution)/shard_map/ppermute | solution.py:33

commit v4 on v3

--- a/solution.py
+++ b/solution.py
@@ -8,6 +8,7 @@
 from jax.experimental.pallas import tpu as pltpu
 from jax.sharding import PartitionSpec as P
 
+
 MIB = 1 << 20
 WHOLE = pl.BlockSpec(memory_space=pltpu.VMEM)
 HELD = pl.BlockSpec(memory_space=pl.ANY)
@@ -33,17 +34,10 @@
     return lax.ppermute(value, "feat", [(index, index ^ mask) for index in range(size)])
 
 
-def slot_order(size):
-    if size < 4:
-        return [0]
-    far = list(range(0, size, 4))
-    return far + [mask + 2 for mask in far]
-
-
 def gather_rows(own, size, beside=(), later=None):
     if size < 8:
         even = own if size == 2 else jnp.concatenate([own, swap(own, 2, size)], axis=0)
-        return [even, swap(even, 1, size)], beside, later(()) if later else None
+        return [even, swap(even, 1, size)], beside, later() if later else None
     far = [4 * step for step in range(1, size // 4)]
     got = {mask: swap(own, mask, size) for mask in far}
     side = swap(own, 2, size)
@@ -55,18 +49,39 @@
     late = jnp.concatenate(late, axis=0)
     made = None
     if later:
-        late, made = lax.optimization_barrier((late, later(rest[:1])))
+        late, made = lax.optimization_barrier((late, later(after=rest[:1])))
     return [early, late, early_pair, swap(late, 1, size)], beside, made
 
 
-def scatter_sums(keep, send, size, rows):
-    got = swap(send, 1, size)
+def scatter_sums(keep, send, size, rows, beside):
+    got = swap(send, 1, size) if size > 1 else send
     pair = (keep.astype(jnp.float32) + got.astype(jnp.float32)).astype(jnp.bfloat16)
-    total = pair[:rows].astype(jnp.float32)
-    for slot, mask in enumerate(slot_order(size)):
-        if mask:
-            total = total + swap(pair[slot * rows : (slot + 1) * rows], mask, size).astype(jnp.float32)
-    return total
+    count = max(size // 4, 1)
+
+    def block(start, stop):
+        return pair[start * rows : stop * rows]
+
+    def total(left, right):
+        return left.astype(jnp.float32) + right.astype(jnp.float32)
+
+    own = block(0, 1).astype(jnp.float32)
+    if size < 4:
+        return own, beside
+    if size < 8:
+        return own + swap(block(1, 2), 2, size).astype(jnp.float32), beside
+    outer = swap(block(count + 2, 2 * count), 2, size)
+    inner = swap(block(count, count + 2), 2, size)
+    outer, beside = lax.optimization_barrier((outer, beside))
+    far = total(block(2, count), outer).astype(jnp.bfloat16)
+    near = total(block(1, 2), inner[rows:]).astype(jnp.bfloat16)
+    own = own + inner[:rows].astype(jnp.float32)
+    sums = [
+        swap(far[(slot - 2) * rows : (slot - 1) * rows], 4 * slot, size) for slot in reversed(range(2, count))
+    ]
+    sums.append(swap(near, 4, size))
+    for value in sums:
+        own = own + value.astype(jnp.float32)
+    return own, beside
 
 
 def pick_kernel(ids_hbm, in_hbm, out_hbm, picked_in, picked_out, ids_ref, in_ref, out_ref, sems):
@@ -111,29 +126,33 @@
     )(*(pltpu.with_memory_space_constraint(array, pltpu.HBM) for array in (row_ids, store_inputs, store_targets)))
 
 
-def load_kernel(ref, *refs):
-    out, sems = refs[-2:]
-    copies = [
-        pltpu.make_async_copy(ref.at[index], out.at[index], sems.at[index]) for index in range(ref.shape[0])
-    ]
+def load_kernel(pieces, *refs):
+    sources, outs, sems = refs[: len(pieces)], refs[-1 - len(pieces) : -1], refs[-1]
+    copies = []
+    for source, out, (first, count) in zip(sources, outs, pieces):
+        for index in range(count):
+            copies.append(
+                pltpu.make_async_copy(source.at[first + index], out.at[index], sems.at[len(copies)])
+            )
     for copy in copies:
         copy.start()
     for copy in copies:
         copy.wait()
 
 
-def load(weight, after=()):
-    moved = 4 * weight.size
-    return pl.pallas_call(
-        load_kernel,
-        out_shape=pltpu.VMEM(weight.shape, weight.dtype),
-        in_specs=[HELD] * (1 + len(after)),
-        out_specs=WHOLE,
-        scratch_shapes=[pltpu.SemaphoreType.DMA((weight.shape[0],))],
+def load(pieces, after=()):
+    shapes = [(count,) + weight.shape[1:] for weight, _, count in pieces]
+    moved = sum(4 * math.prod(shape) for shape in shapes)
+    return pl.pallas_call(
+        functools.partial(load_kernel, [(first, count) for _, first, count in pieces]),
+        out_shape=[pltpu.VMEM(shape, jnp.bfloat16) for shape in shapes],
+        in_specs=[HELD] * (len(pieces) + len(after)),
+        out_specs=[WHOLE] * len(pieces),
+        scratch_shapes=[pltpu.SemaphoreType.DMA((sum(count for _, _, count in pieces),))],
         compiler_params=params(2 * MIB),
         cost_estimate=cost(moved * 100, moved),
         name="load",
-    )(pltpu.with_memory_space_constraint(weight, pltpu.HBM), *after)
+    )(*(pltpu.with_memory_space_constraint(weight, pltpu.HBM) for weight, _, _ in pieces), *after)
 
 
 def join(part_refs, out_ref):
@@ -144,13 +163,14 @@
 
 
 def forward_kernel(*refs):
-    enc_ref, bias_ref, dec_ref, keep_ref, send_ref, feat_ref, x_ref = refs[-7:]
+    parts, refs = refs[:-8], refs[-8:]
+    enc_ref, bias_ref, dec_ref, last_ref, keep_ref, send_ref, feat_ref, x_ref = refs
     layers, width, tile = enc_ref.shape
     half = keep_ref.shape[0]
-    join(refs[:-7], x_ref)
+    held = dec_ref.shape[0]
+    join(parts, x_ref)
     chunk = min(256, tile)
     for layer in range(layers):
-
         for step in range(tile // chunk):
             columns = pl.ds(step * chunk, chunk)
             value = jnp.dot(
@@ -163,24 +183,22 @@
 
     span = min(512, width)
     for target in range(layers):
-
+        wanted = [(index, source) for index, (source, goal) in enumerate(pair_list(layers)) if goal == target]
         for step in range(width // span):
             columns = pl.ds(step * span, span)
             total = None
-            for index, (source, goal) in enumerate(pair_list(layers)):
-                if goal == target:
-                    term = jnp.dot(
-                        feat_ref[source], dec_ref[index, :, columns], preferred_element_type=jnp.float32
-                    )
-                    total = term if total is None else total + term
+            for index, source in wanted:
+                weight = dec_ref[index, :, columns] if index < held else last_ref[index - held, :, columns]
+                term = jnp.dot(feat_ref[source], weight, preferred_element_type=jnp.float32)
+                total = term if total is None else total + term
             total = total.astype(jnp.bfloat16)
             places = pl.ds(target * width + step * span, span)
             keep_ref[:, places] = total[:half]
             send_ref[:, places] = total[half:]
 
 
-def forward(parts, enc_weight, enc_bias, dec_weight):
-    layers, width, tile = enc_weight.shape
+def forward(parts, enc_weight, enc_bias, dec_near, dec_last):
+    layers, _, tile = enc_weight.shape
     half, wide = sum(part.shape[0] for part in parts) // 2, parts[0].shape[1]
     side = jax.ShapeDtypeStruct((half, wide), jnp.bfloat16)
     return pl.pallas_call(
@@ -191,41 +209,50 @@
             jax.ShapeDtypeStruct((layers, 2 * half, tile), jnp.bfloat16),
             jax.ShapeDtypeStruct((2 * half, wide), jnp.bfloat16),
         ),
-        in_specs=[WHOLE] * (len(parts) + 3),
+        in_specs=[WHOLE] * (len(parts) + 4),
         out_specs=[WHOLE] * 4,
-        compiler_params=params(16 * MIB),
-        cost_estimate=cost(4 * half * (enc_weight.size + dec_weight.size), 0),
+        compiler_params=params(12 * MIB),
+        cost_estimate=cost(4 * half * (enc_weight.size + dec_near.size + dec_last.size), 0),
         name="forward",
-    )(*parts, in_vmem(enc_weight), enc_bias, in_vmem(dec_weight))
-
-
-def turn_kernel(x_ref, feat_ref, x_out, feat_out):
-    x_out[...] = x_ref[...].T
-    for layer in range(feat_ref.shape[0]):
-        feat_out[layer] = feat_ref[layer].T
-
-
-def turn(x, feats):
-    layers, tokens, tile = feats.shape
+    )(
+        *parts,
+        in_vmem(enc_weight),
+        enc_bias,
+        in_vmem(dec_near),
+        in_vmem(dec_last),
+    )
+
+
+def turn_kernel(*refs):
+    outs = iter(refs[len(refs) // 2 :])
+    for ref in refs[: len(refs) // 2]:
+        out = next(outs)
+        if len(ref.shape) == 2:
+            out[...] = ref[...].T
+        else:
+            for index in range(ref.shape[0]):
+                out[index] = ref[index].T
+
+
+def turn(arrays):
+    shapes = [array.shape[:-2] + (array.shape[-1], array.shape[-2]) for array in arrays]
     return pl.pallas_call(
         turn_kernel,
-        out_shape=(
-            jax.ShapeDtypeStruct((x.shape[1], tokens), jnp.bfloat16),
-            jax.ShapeDtypeStruct((layers, tile, tokens), jnp.bfloat16),
-        ),
-        in_specs=[WHOLE] * 2,
-        out_specs=[WHOLE] * 2,
-        compiler_params=params(16 * MIB),
-        cost_estimate=cost(2000 * (x.size + feats.size), 0),
+        out_shape=[pltpu.VMEM(shape, jnp.bfloat16) for shape in shapes],
+        in_specs=[WHOLE] * len(arrays),
+        out_specs=[WHOLE] * len(arrays),
+        compiler_params=params(8 * MIB),
+        cost_estimate=cost(1000 * sum(array.size for array in arrays), 0),
         name="turn",
-    )(x, feats)
+    )(*(in_vmem(array) for array in arrays))
 
 
 def backward_kernel(scale, *refs):
-    parts, refs = refs[:-13], refs[-13:]
-    feat_ref, feat_t_ref, x_t_ref, dec_ref, enc_out, bias_out, dec_out = refs[:7]
-    e_ref, pre_ref, stage_dec, stage_enc, dec_sem, enc_sem = refs[7:]
-    pairs, tile, width = dec_ref.shape
+    parts, refs = refs[:-14], refs[-14:]
+    feat_ref, feat_t_ref, x_t_ref, near_t_ref, last_t_ref, enc_out, bias_out, dec_out = refs[:8]
+    e_ref, pre_ref, stage_dec, stage_enc, dec_sem, enc_sem = refs[8:]
+    pairs, tile, width = stage_dec.shape
+    held = near_t_ref.shape[0]
     layers = feat_ref.shape[0]
     pair_of = pair_list(layers)
     join(parts, e_ref)
@@ -248,11 +275,9 @@
         total = None
         for index, (source, target) in enumerate(pair_of):
             if source == layer:
-                term = lax.dot_general(
-                    e_ref[:, target * width : (target + 1) * width],
-                    dec_ref[index, place, :],
-                    (((1,), (1,)), ((), ())),
-                    preferred_element_type=jnp.float32,
+                weight = near_t_ref[index, :, place] if index < held else last_t_ref[index - held, :, place]
+                term = jnp.dot(
+                    e_ref[:, target * width : (target + 1) * width], weight, preferred_element_type=jnp.float32
                 )
                 total = term if total is None else total + term
         pre = jnp.where(feat_ref[layer, :, place] > 0, total, 0.0) * scale
@@ -289,9 +314,9 @@
     pltpu.make_async_copy(stage_enc, enc_out, enc_sem).wait()
 
 
-def backward(scale, parts, feats, feats_t, x_t, dec_weight):
+def backward(scale, parts, feats, feats_t, x_t, near_t, last_t):
     layers, tokens, tile = feats.shape
-    pairs, _, width = dec_weight.shape
+    pairs, width = near_t.shape[0] + last_t.shape[0], near_t.shape[1]
     return pl.pallas_call(
         functools.partial(backward_kernel, scale),
         out_shape=(
@@ -299,7 +324,7 @@
             jax.ShapeDtypeStruct((layers, tile), jnp.float32),
             jax.ShapeDtypeStruct((pairs, tile, width), jnp.bfloat16),
         ),
-        in_specs=[WHOLE] * (len(parts) + 4),
+        in_specs=[WHOLE] * (len(parts) + 5),
         out_specs=[HELD, WHOLE, HELD],
         scratch_shapes=[
             pltpu.VMEM((tokens, layers * width), jnp.bfloat16),
@@ -310,9 +335,9 @@
             pltpu.SemaphoreType.DMA,
         ],
         compiler_params=params(28 * MIB),
-        cost_estimate=cost(10 * tokens * dec_weight.size, 0),
+        cost_estimate=cost(10 * tokens * pairs * tile * width, 0),
         name="backward",
-    )(*parts, feats, feats_t, x_t, in_vmem(dec_weight))
+    )(*parts, feats, *(in_vmem(array) for array in (feats_t, x_t, near_t, last_t)))
 
 
 def local(store_inputs, store_targets, row_ids, enc_weight, enc_bias, dec_weight):
@@ -320,15 +345,19 @@
     rows = row_ids.shape[0]
     scale = 1.0 / math.sqrt(rows * size)
     picked_in, picked_out = pick(row_ids, store_inputs, store_targets)
-    parts, enc_near, dec_near = gather_rows(
-        picked_in, size, load(enc_weight), functools.partial(load, dec_weight)
+    held = dec_weight.shape[0] - 1
+    parts, (enc_near, dec_last), (dec_near,) = gather_rows(
+        picked_in,
+        size,
+        load([(enc_weight, 0, enc_weight.shape[0]), (dec_weight, held, 1)]),
+        functools.partial(load, [(dec_weight, 0, held)]),
     )
-    keep, send, feats, x = forward(parts, enc_near, enc_bias, dec_near)
-    turned = turn(x, feats)
-    own = scatter_sums(keep, send, size, rows)
+    keep, send, feats, x = forward(parts, enc_near, enc_bias, dec_near, dec_last)
+    flipped = turn([dec_near, dec_last])
+    own, (near_t, last_t) = scatter_sums(keep, send, size, rows, flipped)
     errors_own = (own - picked_out.astype(jnp.float32)).astype(jnp.bfloat16)
-    parts, (x_t, feats_t), _ = gather_rows(errors_own, size, turned)
-    return backward(scale, parts, feats, feats_t, x_t, dec_near)
+    parts, (x_t, feats_t), _ = gather_rows(errors_own, size, turn([x, feats]))
+    return backward(scale, parts, feats, feats_t, x_t, near_t, last_t)
 
 
 def solution(mesh):

time: 71.1 us -> 68.8 us (0.968)
  starting transfers between devices: 30 us -> 24.3 us
  Pallas kernels: 24 us -> 26.1 us
  waiting for transfers between devices: 15.8 us -> 16.8 us
    ppermute x24 -> x22, starting transfers between devices: 30 us -> 24.3 us  [swap(): lax.ppermute(value, 'feat', [(index, index ^ mask) for index in range(siz...]
    pallas_call x3 -> x4, Pallas kernels: 8.62 us -> 12.3 us  [the longest x2 8.17 us: load(): pl.pallas_call(functools.partial(load_kernel, [(first, count) for _, firs...]
    pallas_call x1, Pallas kernels: 11.1 us -> 9.71 us  [backward(): pl.pallas_call(functools.partial(backward_kernel, scale), out_shape=(jax....]
    ppermute x24 -> x22, waiting for transfers between devices: 15.8 us -> 16.8 us  [swap(): lax.ppermute(value, 'feat', [(index, index ^ mask) for index in range(siz...]
  transfers between devices with their start and end apart: 24 -> 22, of which waited for: 10 -> 11; matrix products, arithmetic and copies ran while one was open for 0% -> 0% of each run, Pallas kernels for 12% -> 18%
where the time goes in v4:
time: 68.8 us; the launch traced here: 68.6 us
  Pallas kernels  26.1 us (38%)
  starting transfers between devices  24.3 us (35%)
  waiting for transfers between devices  16.8 us (24%)
  between operations  1.03 us (1%)
    ppermute x22, starting transfers between devices, swap(): lax.ppermute(value, 'feat', [(index, index ^ mask) for index in range(siz...  24.3 us
    ppermute x22, waiting for transfers between devices, swap(): lax.ppermute(value, 'feat', [(index, index ^ mask) for index in range(siz...  16.8 us
    pallas_call x1, Pallas kernels, backward(): pl.pallas_call(functools.partial(backward_kernel, scale), out_shape=(jax....  9.71 us
    pallas_call x2, Pallas kernels, load(): pl.pallas_call(functools.partial(load_kernel, [(first, count) for _, firs...  8.17 us
    pallas_call x2, Pallas kernels, turn(): pl.pallas_call(turn_kernel, out_shape=[pltpu.VMEM(shape, jnp.bfloat16) fo...  4.09 us
    pallas_call x1, Pallas kernels, forward(): pl.pallas_call(forward_kernel, out_shape=(side, side, jax.ShapeDtypeStruc...  2.97 us
  transfers between devices with their start and end apart: 22, of which 11 were waited for; matrix products, arithmetic and copies ran while one was open for 0% of the time, Pallas kernels for 18%

profile of v4, /device:TPU:0, one launch (start us, length us, event | category | flops | bytes accessed | tf_op | source)
XLA Modules:
  0.0 68.6 jit_solution(14454870034110547338)
XLA Ops:
  0.6 1.2 %pick.1 = (bf16[8,4096]{1,0:T(8,128)(2,1)S(1)}, bf16[8,4096]{1,0:T(8,128)(2,1)S(1)}) custom-call(s32[8]{0:T(128)} %ids_hbm.1, bf16[2,16,2048]{2,1,0:T(8,128)(2,1)} %in_hbm.1, bf16[2,16,2048]{2,1,0:T(8,128)(2,1)} %out_hbm.1), custom_call_target="tpu_custom_call" | custom-call | tf_op jit(solution)/shard_map/pick/pallas_call | solution.py:113
  1.8 3.1 %collective-permute-start.3 = (bf16[8,4096]{1,0:T(8,128)(2,1)S(1)}, bf16[8,4096]{1,0:T(8,128)(2,1)S(1)}, u32[]{:S(2)}, u32[]{:S(2)}) collective-permute-start(bf16[8,4096]{1,0:T(8,128)(2,1)S(1)} %get-tuple-element.28), channel_id=1, source_target_pairs={{0,2},{1,3},{2,0},{3,1},{4,6},{5,7},{6,4},{7,5},{8,10},{9,11},{10,... | collective-permute-start | bytes 196616 | tf_op jit(solution)/shard_map/ppermute | solution.py:34
  4.9 3.6 %collective-permute-start.2 = (bf16[8,4096]{1,0:T(8,128)(2,1)S(1)}, bf16[8,4096]{1,0:T(8,128)(2,1)S(1)}, u32[]{:S(2)}, u32[]{:S(2)}) collective-permute-start(bf16[8,4096]{1,0:T(8,128)(2,1)S(1)} %get-tuple-element.28), channel_id=1, source_target_pairs={{0,12},{1,13},{2,14},{3,15},{4,8},{5,9},{6,10},{7,11},{8,4},{9,5},... | collective-permute-start | bytes 196616 | tf_op jit(solution)/shard_map/ppermute | solution.py:34
  8.5 0.0 collective-permute-start.1
  8.5 0.8 %collective-permute-start = (bf16[8,4096]{1,0:T(8,128)(2,1)S(1)}, bf16[8,4096]{1,0:T(8,128)(2,1)S(1)}, u32[]{:S(2)}, u32[]{:S(2)}) collective-permute-start(bf16[8,4096]{1,0:T(8,128)(2,1)S(1)} %get-tuple-element.28), channel_id=1, source_target_pairs={{0,4},{1,5},{2,6},{3,7},{4,0},{5,1},{6,2},{7,3},{8,12},{9,13},{10,... | collective-permute-start | bytes 196616 | tf_op jit(solution)/shard_map/ppermute | solution.py:34
  9.3 4.7 %load.2 = (bf16[2,2048,1024]{2,1,0:T(8,128)(2,1)S(1)}, bf16[1,1024,2048]{2,1,0:T(8,128)(2,1)S(1)}) custom-call(bf16[2,2048,1024]{2,1,0:T(8,128)(2,1)} %refs_0_.2, bf16[3,1024,2048]{2,1,0:T(8,128)(2,1)} %refs_0_.3), custom_call_target="tpu_custom_call" | custom-call | flops 2516582400 | bytes 25165824 | tf_op jit(solution)/shard_map/load/pallas_call | solution.py:146
  14.0 0.0 collective-permute-done.2
  14.0 0.0 collective-permute-done.1.refs_1_
  14.0 0.0 collective-permute-done
  14.1 0.4 collective-permute-start.5
  14.5 1.7 %collective-permute-start.4 = (bf16[8,4096]{1,0:T(8,128)(2,1)S(1)}, bf16[8,4096]{1,0:T(8,128)(2,1)S(1)}, u32[]{:S(2)}, u32[]{:S(2)}) collective-permute-start(bf16[8,4096]{1,0:T(8,128)(2,1)S(1)} %collective-permute-done), channel_id=1, source_target_pairs={{0,2},{1,3},{2,0},{3,1},{4,6},{5,7},{6,4},{7,5},{8,10},{9,11},{10,... | collective-permute-start | bytes 196616 | tf_op jit(solution)/shard_map/ppermute | solution.py:34
  16.2 0.0 collective-permute-done.3
  16.2 0.0 copy-start
  16.2 3.5 %load.3.refs_6_.refs_0_ = bf16[2,1024,2048]{2,1,0:T(8,128)(2,1)S(1)} custom-call(bf16[3,1024,2048]{2,1,0:T(8,128)(2,1)} %refs_0_.3, bf16[8,4096]{1,0:T(8,128)(2,1)S(1)} %collective-permute-done.1.refs_1_), custom_call_target="tpu_custom_call" | custom-call | flops 1677721600 | bytes 16777216 | tf_op jit(solution)/shard_map/load/pallas_call | solution.py:146
  19.7 0.1 collective-permute-start.6
  19.8 0.6 collective-permute-done.4
  20.3 0.0 collective-permute-done.5
  20.3 0.1 collective-permute-start.7
  20.4 1.4 %collective-permute-done.7.refs_3_ = bf16[24,4096]{1,0:T(8,128)(2,1)S(1)} collective-permute-done((bf16[24,4096]{1,0:T(8,128)(2,1)S(1)}, bf16[24,4096]{1,0:T(8,128)(2,1)S(1)}, u32[]{:S(2)}, u32[]{:S(2)}) %collective-permute-start.7) | collective-permute-done | bytes 196640 | tf_op jit(solution)/shard_map/ppermute | solution.py:34
  21.9 0.0 collective-permute-done.6.refs_2_
  21.9 0.0 copy-done
  21.9 3.0 %forward.1 = (bf16[64,4096]{1,0:T(8,128)(2,1)S(1)}, bf16[64,4096]{1,0:T(8,128)(2,1)S(1)}, bf16[2,128,1024]{2,1,0:T(8,128)(2,1)S(1)}, bf16[128,4096]{1,0:T(8,128)(2,1)S(1)}) custom-call(bf16[40,4096]{1,0:T(8,128)(2,1)S(1)} %constant_dynamic-update-slice_fusion.refs_0_, bf16[24,4096]{1,0:T(8,128)(2,1)S(1)} %pad_maximum_fusion.refs_1_, ...), custom_call_target="tpu_custom_call" | custom-call | flops 2684354560 | tf_op jit(solution)/shard_map/forward/pallas_call | solution.py:204
  24.8 0.2 collective-permute-start.8
  25.0 1.8 %collective-permute-done.8 = bf16[64,4096]{1,0:T(8,128)(2,1)S(1)} collective-permute-done((bf16[64,4096]{1,0:T(8,128)(2,1)S(1)}, bf16[64,4096]{1,0:T(8,128)(2,1)S(1)}, u32[]{:S(2)}, u32[]{:S(2)}) %collective-permute-start.8) | collective-permute-done | bytes 524320 | tf_op jit(solution)/shard_map/ppermute | solution.py:34
  26.8 0.1 add_convert_fusion
  27.0 0.6 collective-permute-start.10
  27.5 3.6 %turn.2 = (bf16[2,2048,1024]{2,1,0:T(8,128)(2,1)S(1)}, bf16[1,2048,1024]{2,1,0:T(8,128)(2,1)S(1)}) custom-call(bf16[2,1024,2048]{2,1,0:T(8,128)(2,1)S(1)} %load.3.refs_6_.refs_0_, bf16[1,1024,2048]{2,1,0:T(8,128)(2,1)S(1)} %get-tuple-element.36.refs_7_.refs_1_), custom_call_target="tpu_custom_call" | custom-call | flops 6291456000 | tf_op jit(solution)/shard_map/turn/pallas_call | solution.py:239
  31.2 1.6 %collective-permute-start.9 = (bf16[16,4096]{1,0:T(8,128)(2,1)S(1)}, bf16[16,4096]{1,0:T(8,128)(2,1)S(1)}, u32[]{:S(2)}, u32[]{:S(2)}) collective-permute-start(bf16[16,4096]{1,0:T(8,128)(2,1)S(1)} %get-tuple-element.56), channel_id=1, source_target_pairs={{0,2},{1,3},{2,0},{3,1},{4,6},{5,7},{6,4},{7,5},{8,10},{9,11},{10,... | collective-permute-start | bytes 393224 | tf_op jit(solution)/shard_map/ppermute | solution.py:34
  32.8 0.0 collective-permute-done.10
  32.8 3.5 %collective-permute-start.11 = (bf16[8,4096]{1,0:T(8,128)(2,1)S(1)}, bf16[8,4096]{1,0:T(8,128)(2,1)S(1)}, u32[]{:S(2)}, u32[]{:S(2)}) collective-permute-start(bf16[8,4096]{1,0:T(8,128)(2,1)S(1)} %get-tuple-element.57), channel_id=1, source_target_pairs={{0,12},{1,13},{2,14},{3,15},{4,8},{5,9},{6,10},{7,11},{8,4},{9,5},... | collective-permute-start | bytes 196616 | tf_op jit(solution)/shard_map/ppermute | solution.py:34
  36.3 0.0 collective-permute-start.12
  36.3 0.2 collective-permute-done.9
  36.5 1.1 %collective-permute-start.13 = (bf16[8,4096]{1,0:T(8,128)(2,1)S(1)}, bf16[8,4096]{1,0:T(8,128)(2,1)S(1)}, u32[]{:S(2)}, u32[]{:S(2)}) collective-permute-start(bf16[8,4096]{1,0:T(8,128)(2,1)S(1)} %add_convert_fusion.2), channel_id=1, source_target_pairs={{0,4},{1,5},{2,6},{3,7},{4,0},{5,1},{6,2},{7,3},{8,12},{9,13},{10,... | collective-permute-start | bytes 196616 | tf_op jit(solution)/shard_map/ppermute | solution.py:34
  37.7 1.5 %collective-permute-done.11 = bf16[8,4096]{1,0:T(8,128)(2,1)S(1)} collective-permute-done((bf16[8,4096]{1,0:T(8,128)(2,1)S(1)}, bf16[8,4096]{1,0:T(8,128)(2,1)S(1)}, u32[]{:S(2)}, u32[]{:S(2)}) %collective-permute-start.11) | collective-permute-done | bytes 65568 | tf_op jit(solution)/shard_map/ppermute | solution.py:34
  39.2 2.7 %collective-permute-done.12 = bf16[8,4096]{1,0:T(8,128)(2,1)S(1)} collective-permute-done((bf16[8,4096]{1,0:T(8,128)(2,1)S(1)}, bf16[8,4096]{1,0:T(8,128)(2,1)S(1)}, u32[]{:S(2)}, u32[]{:S(2)}) %collective-permute-start.12) | collective-permute-done | bytes 65568 | tf_op jit(solution)/shard_map/ppermute | solution.py:34
  41.9 0.2 collective-permute-done.13
  42.1 0.1 constant_dynamic-update-slice_fusion.9
  42.1 2.7 %collective-permute-start.16 = (bf16[8,4096]{1,0:T(8,128)(2,1)S(1)}, bf16[8,4096]{1,0:T(8,128)(2,1)S(1)}, u32[]{:S(2)}, u32[]{:S(2)}) collective-permute-start(bf16[8,4096]{1,0:T(8,128)(2,1)S(1)} %get-tuple-element.54), channel_id=1, source_target_pairs={{0,12},{1,13},{2,14},{3,15},{4,8},{5,9},{6,10},{7,11},{8,4},{9,5},... | collective-permute-start | bytes 196616 | tf_op jit(solution)/shard_map/ppermute | solution.py:34
  44.8 0.0 collective-permute-start.15
  44.8 1.8 %collective-permute-start.14 = (bf16[8,4096]{1,0:T(8,128)(2,1)S(1)}, bf16[8,4096]{1,0:T(8,128)(2,1)S(1)}, u32[]{:S(2)}, u32[]{:S(2)}) collective-permute-start(bf16[8,4096]{1,0:T(8,128)(2,1)S(1)} %get-tuple-element.54), channel_id=1, source_target_pairs={{0,4},{1,5},{2,6},{3,7},{4,0},{5,1},{6,2},{7,3},{8,12},{9,13},{10,... | collective-permute-start | bytes 196616 | tf_op jit(solution)/shard_map/ppermute | solution.py:34
  46.6 0.5 turn.3
  47.1 1.0 %collective-permute-start.17 = (bf16[8,4096]{1,0:T(8,128)(2,1)S(1)}, bf16[8,4096]{1,0:T(8,128)(2,1)S(1)}, u32[]{:S(2)}, u32[]{:S(2)}) collective-permute-start(bf16[8,4096]{1,0:T(8,128)(2,1)S(1)} %get-tuple-element.54), channel_id=1, source_target_pairs={{0,2},{1,3},{2,0},{3,1},{4,6},{5,7},{6,4},{7,5},{8,10},{9,11},{10,... | collective-permute-start | bytes 196616 | tf_op jit(solution)/shard_map/ppermute | solution.py:34
  48.0 0.3 collective-permute-done.16
  48.3 2.4 %collective-permute-done.15 = bf16[8,4096]{1,0:T(8,128)(2,1)S(1)} collective-permute-done((bf16[8,4096]{1,0:T(8,128)(2,1)S(1)}, bf16[8,4096]{1,0:T(8,128)(2,1)S(1)}, u32[]{:S(2)}, u32[]{:S(2)}) %collective-permute-start.15) | collective-permute-done | bytes 65568 | tf_op jit(solution)/shard_map/ppermute | solution.py:34
  50.8 0.0 collective-permute-done.14
  50.8 0.6 collective-permute-start.19
  51.4 1.5 %collective-permute-start.18 = (bf16[8,4096]{1,0:T(8,128)(2,1)S(1)}, bf16[8,4096]{1,0:T(8,128)(2,1)S(1)}, u32[]{:S(2)}, u32[]{:S(2)}) collective-permute-start(bf16[8,4096]{1,0:T(8,128)(2,1)S(1)} %collective-permute-done.14), channel_id=1, source_target_pairs={{0,2},{1,3},{2,0},{3,1},{4,6},{5,7},{6,4},{7,5},{8,10},{9,11},{10,... | collective-permute-start | bytes 196616 | tf_op jit(solution)/shard_map/ppermute | solution.py:34
  52.9 0.0 collective-permute-done.17
  52.9 0.1 collective-permute-start.20
  53.0 4.2 %collective-permute-done.18 = bf16[8,4096]{1,0:T(8,128)(2,1)S(1)} collective-permute-done((bf16[8,4096]{1,0:T(8,128)(2,1)S(1)}, bf16[8,4096]{1,0:T(8,128)(2,1)S(1)}, u32[]{:S(2)}, u32[]{:S(2)}) %collective-permute-start.18) | collective-permute-done | bytes 65568 | tf_op jit(solution)/shard_map/ppermute | solution.py:34
  57.2 0.0 collective-permute-done.19
  57.2 0.1 collective-permute-start.21
  57.3 1.4 %collective-permute-done.21.refs_3_ = bf16[24,4096]{1,0:T(8,128)(2,1)S(1)} collective-permute-done((bf16[24,4096]{1,0:T(8,128)(2,1)S(1)}, bf16[24,4096]{1,0:T(8,128)(2,1)S(1)}, u32[]{:S(2)}, u32[]{:S(2)}) %collective-permute-start.21) | collective-permute-done | bytes 196640 | tf_op jit(solution)/shard_map/ppermute | solution.py:34
  58.7 0.0 collective-permute-done.20.refs_2_
  58.7 9.7 %backward.1 = (bf16[2,2048,1024]{2,1,0:T(8,128)(2,1)}, f32[2,1024]{1,0:T(2,128)}, bf16[3,1024,2048]{2,1,0:T(8,128)(2,1)}) custom-call(bf16[40,4096]{1,0:T(8,128)(2,1)S(1)} %constant_dynamic-update-slice_fusion.5.refs_0_, bf16[24,4096]{1,0:T(8,128)(2,1)S(1)} %constant_dynamic-update-slice_fusion.10.refs_1_, ...), custom_call_target="tpu_custom_call" | custom-call | flops 8053063680 | tf_op jit(solution)/shard_map/backward/pallas_call | solution.py:320
  (18 shorter events, 0.2 us)
Async XLA Ops:
  1.8 14.3 %collective-permute-start.3 = (bf16[8,4096]{1,0:T(8,128)(2,1)S(1)}, bf16[8,4096]{1,0:T(8,128)(2,1)S(1)}, u32[]{:S(2)}, u32[]{:S(2)}) collective-permute-start(bf16[8,4096]{1,0:T(8,128)(2,1)S(1)} %get-tuple-element.28), channel_id=1, source_target_pairs={{0,2},{1,3},{2,0},{3,1},{4,6},{5,7},{6,4},{7,5},{8,10},{9,11},{10,... | collective-permute-start | bytes 196616 | tf_op jit(solution)/shard_map/ppermute | solution.py:34
  4.9 9.1 %collective-permute-start.2 = (bf16[8,4096]{1,0:T(8,128)(2,1)S(1)}, bf16[8,4096]{1,0:T(8,128)(2,1)S(1)}, u32[]{:S(2)}, u32[]{:S(2)}) collective-permute-start(bf16[8,4096]{1,0:T(8,128)(2,1)S(1)} %get-tuple-element.28), channel_id=1, source_target_pairs={{0,12},{1,13},{2,14},{3,15},{4,8},{5,9},{6,10},{7,11},{8,4},{9,5},... | collective-permute-start | bytes 196616 | tf_op jit(solution)/shard_map/ppermute | solution.py:34
  8.5 5.5 %collective-permute-start.1 = (bf16[8,4096]{1,0:T(8,128)(2,1)S(1)}, bf16[8,4096]{1,0:T(8,128)(2,1)S(1)}, u32[]{:S(2)}, u32[]{:S(2)}) collective-permute-start(bf16[8,4096]{1,0:T(8,128)(2,1)S(1)} %get-tuple-element.28), channel_id=1, source_target_pairs={{0,8},{1,9},{2,10},{3,11},{4,12},{5,13},{6,14},{7,15},{8,0},{9,1},... | collective-permute-start | bytes 196616 | tf_op jit(solution)/shard_map/ppermute | solution.py:34
  8.5 5.5 %collective-permute-start = (bf16[8,4096]{1,0:T(8,128)(2,1)S(1)}, bf16[8,4096]{1,0:T(8,128)(2,1)S(1)}, u32[]{:S(2)}, u32[]{:S(2)}) collective-permute-start(bf16[8,4096]{1,0:T(8,128)(2,1)S(1)} %get-tuple-element.28), channel_id=1, source_target_pairs={{0,4},{1,5},{2,6},{3,7},{4,0},{5,1},{6,2},{7,3},{8,12},{9,13},{10,... | collective-permute-start | bytes 196616 | tf_op jit(solution)/shard_map/ppermute | solution.py:34
  14.1 6.3 %collective-permute-start.5 = (bf16[16,4096]{1,0:T(8,128)(2,1)S(1)}, bf16[16,4096]{1,0:T(8,128)(2,1)S(1)}, u32[]{:S(2)}, u32[]{:S(2)}) collective-permute-start(bf16[16,4096]{1,0:T(8,128)(2,1)S(1)} %pad_maximum_fusion.1), channel_id=1, source_target_pairs={{0,2},{1,3},{2,0},{3,1},{4,6},{5,7},{6,4},{7,5},{8,10},{9,11},{10,... | collective-permute-start | bytes 393224 | tf_op jit(solution)/shard_map/ppermute | solution.py:34
  14.5 5.8 %collective-permute-start.4 = (bf16[8,4096]{1,0:T(8,128)(2,1)S(1)}, bf16[8,4096]{1,0:T(8,128)(2,1)S(1)}, u32[]{:S(2)}, u32[]{:S(2)}) collective-permute-start(bf16[8,4096]{1,0:T(8,128)(2,1)S(1)} %collective-permute-done), channel_id=1, source_target_pairs={{0,2},{1,3},{2,0},{3,1},{4,6},{5,7},{6,4},{7,5},{8,10},{9,11},{10,... | collective-permute-start | bytes 196616 | tf_op jit(solution)/shard_map/ppermute | solution.py:34
  16.2 5.7 %copy-start = (f32[2,1024]{1,0:T(2,128)S(1)}, f32[2,1024]{1,0:T(2,128)}, u32[]{:S(2)}) copy-start(f32[2,1024]{1,0:T(2,128)} %refs_5_.1) | copy-start | bytes 24580
  19.7 2.2 %collective-permute-start.6 = (bf16[40,4096]{1,0:T(8,128)(2,1)S(1)}, bf16[40,4096]{1,0:T(8,128)(2,1)S(1)}, u32[]{:S(2)}, u32[]{:S(2)}) collective-permute-start(bf16[40,4096]{1,0:T(8,128)(2,1)S(1)} %constant_dynamic-update-slice_fusion.refs_0_), channel_id=1, source_target_pairs={{0,1},{1,0},{2,3},{3,2},{4,5},{5,4},{6,7},{7,6},{8,9},{9,8},{10,11... | collective-permute-start | bytes 983048 | tf_op jit(solution)/shard_map/ppermute | solution.py:34
  20.3 1.5 %collective-permute-start.7 = (bf16[24,4096]{1,0:T(8,128)(2,1)S(1)}, bf16[24,4096]{1,0:T(8,128)(2,1)S(1)}, u32[]{:S(2)}, u32[]{:S(2)}) collective-permute-start(bf16[24,4096]{1,0:T(8,128)(2,1)S(1)} %pad_maximum_fusion.refs_1_), channel_id=1, source_target_pairs={{0,1},{1,0},{2,3},{3,2},{4,5},{5,4},{6,7},{7,6},{8,9},{9,8},{10,11... | collective-permute-start | bytes 589832 | tf_op jit(solution)/shard_map/ppermute | solution.py:34
  24.8 2.0 %collective-permute-start.8 = (bf16[64,4096]{1,0:T(8,128)(2,1)S(1)}, bf16[64,4096]{1,0:T(8,128)(2,1)S(1)}, u32[]{:S(2)}, u32[]{:S(2)}) collective-permute-start(bf16[64,4096]{1,0:T(8,128)(2,1)S(1)} %get-tuple-element.38), channel_id=1, source_target_pairs={{0,1},{1,0},{2,3},{3,2},{4,5},{5,4},{6,7},{7,6},{8,9},{9,8},{10,11... | collective-permute-start | bytes 1572872 | tf_op jit(solution)/shard_map/ppermute | solution.py:34
  27.0 5.8 %collective-permute-start.10 = (bf16[16,4096]{1,0:T(8,128)(2,1)S(1)}, bf16[16,4096]{1,0:T(8,128)(2,1)S(1)}, u32[]{:S(2)}, u32[]{:S(2)}) collective-permute-start(bf16[16,4096]{1,0:T(8,128)(2,1)S(1)} %get-tuple-element.55), channel_id=1, source_target_pairs={{0,2},{1,3},{2,0},{3,1},{4,6},{5,7},{6,4},{7,5},{8,10},{9,11},{10,... | collective-permute-start | bytes 393224 | tf_op jit(solution)/shard_map/ppermute | solution.py:34
  31.2 5.3 %collective-permute-start.9 = (bf16[16,4096]{1,0:T(8,128)(2,1)S(1)}, bf16[16,4096]{1,0:T(8,128)(2,1)S(1)}, u32[]{:S(2)}, u32[]{:S(2)}) collective-permute-start(bf16[16,4096]{1,0:T(8,128)(2,1)S(1)} %get-tuple-element.56), channel_id=1, source_target_pairs={{0,2},{1,3},{2,0},{3,1},{4,6},{5,7},{6,4},{7,5},{8,10},{9,11},{10,... | collective-permute-start | bytes 393224 | tf_op jit(solution)/shard_map/ppermute | solution.py:34
  32.8 6.3 %collective-permute-start.11 = (bf16[8,4096]{1,0:T(8,128)(2,1)S(1)}, bf16[8,4096]{1,0:T(8,128)(2,1)S(1)}, u32[]{:S(2)}, u32[]{:S(2)}) collective-permute-start(bf16[8,4096]{1,0:T(8,128)(2,1)S(1)} %get-tuple-element.57), channel_id=1, source_target_pairs={{0,12},{1,13},{2,14},{3,15},{4,8},{5,9},{6,10},{7,11},{8,4},{9,5},... | collective-permute-start | bytes 196616 | tf_op jit(solution)/shard_map/ppermute | solution.py:34
  36.3 5.6 %collective-permute-start.12 = (bf16[8,4096]{1,0:T(8,128)(2,1)S(1)}, bf16[8,4096]{1,0:T(8,128)(2,1)S(1)}, u32[]{:S(2)}, u32[]{:S(2)}) collective-permute-start(bf16[8,4096]{1,0:T(8,128)(2,1)S(1)} %get-tuple-element.58), channel_id=1, source_target_pairs={{0,8},{1,9},{2,10},{3,11},{4,12},{5,13},{6,14},{7,15},{8,0},{9,1},... | collective-permute-start | bytes 196616 | tf_op jit(solution)/shard_map/ppermute | solution.py:34
  36.5 5.6 %collective-permute-start.13 = (bf16[8,4096]{1,0:T(8,128)(2,1)S(1)}, bf16[8,4096]{1,0:T(8,128)(2,1)S(1)}, u32[]{:S(2)}, u32[]{:S(2)}) collective-permute-start(bf16[8,4096]{1,0:T(8,128)(2,1)S(1)} %add_convert_fusion.2), channel_id=1, source_target_pairs={{0,4},{1,5},{2,6},{3,7},{4,0},{5,1},{6,2},{7,3},{8,12},{9,13},{10,... | collective-permute-start | bytes 196616 | tf_op jit(solution)/shard_map/ppermute | solution.py:34
  42.1 6.2 %collective-permute-start.16 = (bf16[8,4096]{1,0:T(8,128)(2,1)S(1)}, bf16[8,4096]{1,0:T(8,128)(2,1)S(1)}, u32[]{:S(2)}, u32[]{:S(2)}) collective-permute-start(bf16[8,4096]{1,0:T(8,128)(2,1)S(1)} %get-tuple-element.54), channel_id=1, source_target_pairs={{0,12},{1,13},{2,14},{3,15},{4,8},{5,9},{6,10},{7,11},{8,4},{9,5},... | collective-permute-start | bytes 196616 | tf_op jit(solution)/shard_map/ppermute | solution.py:34
  44.8 5.9 %collective-permute-start.15 = (bf16[8,4096]{1,0:T(8,128)(2,1)S(1)}, bf16[8,4096]{1,0:T(8,128)(2,1)S(1)}, u32[]{:S(2)}, u32[]{:S(2)}) collective-permute-start(bf16[8,4096]{1,0:T(8,128)(2,1)S(1)} %get-tuple-element.54), channel_id=1, source_target_pairs={{0,8},{1,9},{2,10},{3,11},{4,12},{5,13},{6,14},{7,15},{8,0},{9,1},... | collective-permute-start | bytes 196616 | tf_op jit(solution)/shard_map/ppermute | solution.py:34
  44.8 5.9 %collective-permute-start.14 = (bf16[8,4096]{1,0:T(8,128)(2,1)S(1)}, bf16[8,4096]{1,0:T(8,128)(2,1)S(1)}, u32[]{:S(2)}, u32[]{:S(2)}) collective-permute-start(bf16[8,4096]{1,0:T(8,128)(2,1)S(1)} %get-tuple-element.54), channel_id=1, source_target_pairs={{0,4},{1,5},{2,6},{3,7},{4,0},{5,1},{6,2},{7,3},{8,12},{9,13},{10,... | collective-permute-start | bytes 196616 | tf_op jit(solution)/shard_map/ppermute | solution.py:34
  47.1 5.8 %collective-permute-start.17 = (bf16[8,4096]{1,0:T(8,128)(2,1)S(1)}, bf16[8,4096]{1,0:T(8,128)(2,1)S(1)}, u32[]{:S(2)}, u32[]{:S(2)}) collective-permute-start(bf16[8,4096]{1,0:T(8,128)(2,1)S(1)} %get-tuple-element.54), channel_id=1, source_target_pairs={{0,2},{1,3},{2,0},{3,1},{4,6},{5,7},{6,4},{7,5},{8,10},{9,11},{10,... | collective-permute-start | bytes 196616 | tf_op jit(solution)/shard_map/ppermute | solution.py:34
  50.8 6.4 %collective-permute-start.19 = (bf16[16,4096]{1,0:T(8,128)(2,1)S(1)}, bf16[16,4096]{1,0:T(8,128)(2,1)S(1)}, u32[]{:S(2)}, u32[]{:S(2)}) collective-permute-start(bf16[16,4096]{1,0:T(8,128)(2,1)S(1)} %pad_maximum_fusion.2), channel_id=1, source_target_pairs={{0,2},{1,3},{2,0},{3,1},{4,6},{5,7},{6,4},{7,5},{8,10},{9,11},{10,... | collective-permute-start | bytes 393224 | tf_op jit(solution)/shard_map/ppermute | solution.py:34
  51.4 5.8 %collective-permute-start.18 = (bf16[8,4096]{1,0:T(8,128)(2,1)S(1)}, bf16[8,4096]{1,0:T(8,128)(2,1)S(1)}, u32[]{:S(2)}, u32[]{:S(2)}) collective-permute-start(bf16[8,4096]{1,0:T(8,128)(2,1)S(1)} %collective-permute-done.14), channel_id=1, source_target_pairs={{0,2},{1,3},{2,0},{3,1},{4,6},{5,7},{6,4},{7,5},{8,10},{9,11},{10,... | collective-permute-start | bytes 196616 | tf_op jit(solution)/shard_map/ppermute | solution.py:34
  52.9 5.8 %collective-permute-start.20 = (bf16[40,4096]{1,0:T(8,128)(2,1)S(1)}, bf16[40,4096]{1,0:T(8,128)(2,1)S(1)}, u32[]{:S(2)}, u32[]{:S(2)}) collective-permute-start(bf16[40,4096]{1,0:T(8,128)(2,1)S(1)} %constant_dynamic-update-slice_fusion.5.refs_0_), channel_id=1, source_target_pairs={{0,1},{1,0},{2,3},{3,2},{4,5},{5,4},{6,7},{7,6},{8,9},{9,8},{10,11... | collective-permute-start | bytes 983048 | tf_op jit(solution)/shard_map/ppermute | solution.py:34
  57.2 1.5 %collective-permute-start.21 = (bf16[24,4096]{1,0:T(8,128)(2,1)S(1)}, bf16[24,4096]{1,0:T(8,128)(2,1)S(1)}, u32[]{:S(2)}, u32[]{:S(2)}) collective-permute-start(bf16[24,4096]{1,0:T(8,128)(2,1)S(1)} %constant_dynamic-update-slice_fusion.10.refs_1_), channel_id=1, source_target_pairs={{0,1},{1,0},{2,3},{3,2},{4,5},{5,4},{6,7},{7,6},{8,9},{9,8},{10,11... | collective-permute-start | bytes 589832 | tf_op jit(solution)/shard_map/ppermute | solution.py:34

commit v5 on v4

--- a/solution.py
+++ b/solution.py
@@ -75,9 +75,7 @@
     far = total(block(2, count), outer).astype(jnp.bfloat16)
     near = total(block(1, 2), inner[rows:]).astype(jnp.bfloat16)
     own = own + inner[:rows].astype(jnp.float32)
-    sums = [
-        swap(far[(slot - 2) * rows : (slot - 1) * rows], 4 * slot, size) for slot in reversed(range(2, count))
-    ]
+    sums = [swap(far[(slot - 2) * rows : (slot - 1) * rows], 4 * slot, size) for slot in range(2, count)]
     sums.append(swap(near, 4, size))
     for value in sums:
         own = own + value.astype(jnp.float32)
@@ -334,7 +332,7 @@
             pltpu.SemaphoreType.DMA,
             pltpu.SemaphoreType.DMA,
         ],
-        compiler_params=params(28 * MIB),
+        compiler_params=params(24 * MIB),
         cost_estimate=cost(10 * tokens * pairs * tile * width, 0),
         name="backward",
     )(*parts, feats, *(in_vmem(array) for array in (feats_t, x_t, near_t, last_t)))
@@ -346,11 +344,11 @@
     scale = 1.0 / math.sqrt(rows * size)
     picked_in, picked_out = pick(row_ids, store_inputs, store_targets)
     held = dec_weight.shape[0] - 1
-    parts, (enc_near, dec_last), (dec_near,) = gather_rows(
+    parts, (enc_near,), (dec_last, dec_near) = gather_rows(
         picked_in,
         size,
-        load([(enc_weight, 0, enc_weight.shape[0]), (dec_weight, held, 1)]),
-        functools.partial(load, [(dec_weight, 0, held)]),
+        load([(enc_weight, 0, enc_weight.shape[0])]),
+        functools.partial(load, [(dec_weight, held, 1), (dec_weight, 0, held)]),
     )
     keep, send, feats, x = forward(parts, enc_near, enc_bias, dec_near, dec_last)
     flipped = turn([dec_near, dec_last])

time: 68.8 us -> 67.9 us (0.987)
  waiting for transfers between devices: 16.8 us -> 15.9 us
    ppermute x22, waiting for transfers between devices: 16.8 us -> 15.9 us  [swap(): lax.ppermute(value, 'feat', [(index, index ^ mask) for index in range(siz...]
where the time goes in v5:
time: 67.9 us; the launch traced here: 67.8 us
  Pallas kernels  26.1 us (38%)
  starting transfers between devices  24.4 us (36%)
  waiting for transfers between devices  15.9 us (23%)
  between operations  1.01 us (1%)
    ppermute x22, starting transfers between devices, swap(): lax.ppermute(value, 'feat', [(index, index ^ mask) for index in range(siz...  24.4 us
    ppermute x22, waiting for transfers between devices, swap(): lax.ppermute(value, 'feat', [(index, index ^ mask) for index in range(siz...  15.9 us
    pallas_call x1, Pallas kernels, backward(): pl.pallas_call(functools.partial(backward_kernel, scale), out_shape=(jax....  9.68 us
    pallas_call x2, Pallas kernels, load(): pl.pallas_call(functools.partial(load_kernel, [(first, count) for _, firs...  8.17 us
    pallas_call x2, Pallas kernels, turn(): pl.pallas_call(turn_kernel, out_shape=[pltpu.VMEM(shape, jnp.bfloat16) fo...  4.09 us
    pallas_call x1, Pallas kernels, forward(): pl.pallas_call(forward_kernel, out_shape=(side, side, jax.ShapeDtypeStruc...  2.95 us
  transfers between devices with their start and end apart: 22, of which 11 were waited for; matrix products, arithmetic and copies ran while one was open for 0% of the time, Pallas kernels for 18%

profile of v5, /device:TPU:0, one launch (start us, length us, event | category | flops | bytes accessed | tf_op | source)
XLA Modules:
  0.0 67.8 jit_solution(14444524319498011093)
XLA Ops:
  0.6 1.2 %pick.1 = (bf16[8,4096]{1,0:T(8,128)(2,1)S(1)}, bf16[8,4096]{1,0:T(8,128)(2,1)S(1)}) custom-call(s32[8]{0:T(128)} %ids_hbm.1, bf16[2,16,2048]{2,1,0:T(8,128)(2,1)} %in_hbm.1, bf16[2,16,2048]{2,1,0:T(8,128)(2,1)} %out_hbm.1), custom_call_target="tpu_custom_call" | custom-call | tf_op jit(solution)/shard_map/pick/pallas_call | solution.py:111
  1.8 3.1 %collective-permute-start.3 = (bf16[8,4096]{1,0:T(8,128)(2,1)S(1)}, bf16[8,4096]{1,0:T(8,128)(2,1)S(1)}, u32[]{:S(2)}, u32[]{:S(2)}) collective-permute-start(bf16[8,4096]{1,0:T(8,128)(2,1)S(1)} %get-tuple-element.28), channel_id=1, source_target_pairs={{0,2},{1,3},{2,0},{3,1},{4,6},{5,7},{6,4},{7,5},{8,10},{9,11},{10,... | collective-permute-start | bytes 196616 | tf_op jit(solution)/shard_map/ppermute | solution.py:34
  4.9 3.6 %collective-permute-start.2 = (bf16[8,4096]{1,0:T(8,128)(2,1)S(1)}, bf16[8,4096]{1,0:T(8,128)(2,1)S(1)}, u32[]{:S(2)}, u32[]{:S(2)}) collective-permute-start(bf16[8,4096]{1,0:T(8,128)(2,1)S(1)} %get-tuple-element.28), channel_id=1, source_target_pairs={{0,12},{1,13},{2,14},{3,15},{4,8},{5,9},{6,10},{7,11},{8,4},{9,5},... | collective-permute-start | bytes 196616 | tf_op jit(solution)/shard_map/ppermute | solution.py:34
  8.5 0.0 collective-permute-start.1
  8.5 0.8 %collective-permute-start = (bf16[8,4096]{1,0:T(8,128)(2,1)S(1)}, bf16[8,4096]{1,0:T(8,128)(2,1)S(1)}, u32[]{:S(2)}, u32[]{:S(2)}) collective-permute-start(bf16[8,4096]{1,0:T(8,128)(2,1)S(1)} %get-tuple-element.28), channel_id=1, source_target_pairs={{0,4},{1,5},{2,6},{3,7},{4,0},{5,1},{6,2},{7,3},{8,12},{9,13},{10,... | collective-permute-start | bytes 196616 | tf_op jit(solution)/shard_map/ppermute | solution.py:34
  9.3 3.5 %load.2.refs_4_ = bf16[2,2048,1024]{2,1,0:T(8,128)(2,1)S(1)} custom-call(bf16[2,2048,1024]{2,1,0:T(8,128)(2,1)} %refs_0_.2), custom_call_target="tpu_custom_call" | custom-call | flops 1677721600 | bytes 16777216 | tf_op jit(solution)/shard_map/load/pallas_call | solution.py:144
  12.8 0.0 collective-permute-done.2
  12.8 1.1 %collective-permute-done.1.refs_2_ = bf16[8,4096]{1,0:T(8,128)(2,1)S(1)} collective-permute-done((bf16[8,4096]{1,0:T(8,128)(2,1)S(1)}, bf16[8,4096]{1,0:T(8,128)(2,1)S(1)}, u32[]{:S(2)}, u32[]{:S(2)}) %collective-permute-start.1) | collective-permute-done | bytes 65568 | tf_op jit(solution)/shard_map/ppermute | solution.py:34
  13.9 0.0 collective-permute-done
  14.0 0.5 collective-permute-start.5
  14.5 0.0 collective-permute-done.3
  14.5 0.0 copy-start
  14.5 0.1 collective-permute-start.6
  14.6 1.7 %collective-permute-start.4 = (bf16[8,4096]{1,0:T(8,128)(2,1)S(1)}, bf16[8,4096]{1,0:T(8,128)(2,1)S(1)}, u32[]{:S(2)}, u32[]{:S(2)}) collective-permute-start(bf16[8,4096]{1,0:T(8,128)(2,1)S(1)} %collective-permute-done), channel_id=1, source_target_pairs={{0,2},{1,3},{2,0},{3,1},{4,6},{5,7},{6,4},{7,5},{8,10},{9,11},{10,... | collective-permute-start | bytes 196616 | tf_op jit(solution)/shard_map/ppermute | solution.py:34
  16.2 4.7 %load.3 = (bf16[1,1024,2048]{2,1,0:T(8,128)(2,1)S(1)}, bf16[2,1024,2048]{2,1,0:T(8,128)(2,1)S(1)}) custom-call(bf16[3,1024,2048]{2,1,0:T(8,128)(2,1)} %refs_1_.1, bf16[3,1024,2048]{2,1,0:T(8,128)(2,1)} %refs_1_.1, bf16[8,4096]{1,0:T(8,128)(2,1)S(1)} %collective-permute-done.1.refs_2_), custom_call_target="tpu_custom_call" | custom-call | flops 2516582400 | bytes 25165824 | tf_op jit(solution)/shard_map/load/pallas_call | solution.py:144
  20.9 0.0 collective-permute-done.4
  21.0 0.0 collective-permute-done.5
  21.0 0.2 collective-permute-start.7
  21.2 1.3 %collective-permute-done.7.refs_3_ = bf16[24,4096]{1,0:T(8,128)(2,1)S(1)} collective-permute-done((bf16[24,4096]{1,0:T(8,128)(2,1)S(1)}, bf16[24,4096]{1,0:T(8,128)(2,1)S(1)}, u32[]{:S(2)}, u32[]{:S(2)}) %collective-permute-start.7) | collective-permute-done | bytes 196640 | tf_op jit(solution)/shard_map/ppermute | solution.py:34
  22.5 0.0 collective-permute-done.6.refs_2_
  22.5 0.0 copy-done
  22.5 3.0 %forward.1 = (bf16[64,4096]{1,0:T(8,128)(2,1)S(1)}, bf16[64,4096]{1,0:T(8,128)(2,1)S(1)}, bf16[2,128,1024]{2,1,0:T(8,128)(2,1)S(1)}, bf16[128,4096]{1,0:T(8,128)(2,1)S(1)}) custom-call(bf16[40,4096]{1,0:T(8,128)(2,1)S(1)} %constant_dynamic-update-slice_fusion.refs_0_, bf16[24,4096]{1,0:T(8,128)(2,1)S(1)} %pad_maximum_fusion.refs_1_, ...), custom_call_target="tpu_custom_call" | custom-call | flops 2684354560 | tf_op jit(solution)/shard_map/forward/pallas_call | solution.py:202
  25.5 0.2 collective-permute-start.8
  25.7 1.8 %collective-permute-done.8 = bf16[64,4096]{1,0:T(8,128)(2,1)S(1)} collective-permute-done((bf16[64,4096]{1,0:T(8,128)(2,1)S(1)}, bf16[64,4096]{1,0:T(8,128)(2,1)S(1)}, u32[]{:S(2)}, u32[]{:S(2)}) %collective-permute-start.8) | collective-permute-done | bytes 524320 | tf_op jit(solution)/shard_map/ppermute | solution.py:34
  27.4 0.1 add_convert_fusion
  27.6 0.5 collective-permute-start.10
  28.1 3.6 %turn.2 = (bf16[2,2048,1024]{2,1,0:T(8,128)(2,1)S(1)}, bf16[1,2048,1024]{2,1,0:T(8,128)(2,1)S(1)}) custom-call(bf16[2,1024,2048]{2,1,0:T(8,128)(2,1)S(1)} %get-tuple-element.35.refs_6_.refs_0_, bf16[1,1024,2048]{2,1,0:T(8,128)(2,1)S(1)} %get-tuple-element.36.refs_7_.refs_1_), custom_call_target="tpu_custom_call" | custom-call | flops 6291456000 | tf_op jit(solution)/shard_map/turn/pallas_call | solution.py:237
  31.7 1.7 %collective-permute-start.9 = (bf16[16,4096]{1,0:T(8,128)(2,1)S(1)}, bf16[16,4096]{1,0:T(8,128)(2,1)S(1)}, u32[]{:S(2)}, u32[]{:S(2)}) collective-permute-start(bf16[16,4096]{1,0:T(8,128)(2,1)S(1)} %get-tuple-element.56), channel_id=1, source_target_pairs={{0,2},{1,3},{2,0},{3,1},{4,6},{5,7},{6,4},{7,5},{8,10},{9,11},{10,... | collective-permute-start | bytes 393224 | tf_op jit(solution)/shard_map/ppermute | solution.py:34
  33.4 0.0 collective-permute-done.10
  33.4 1.8 %collective-permute-start.11 = (bf16[8,4096]{1,0:T(8,128)(2,1)S(1)}, bf16[8,4096]{1,0:T(8,128)(2,1)S(1)}, u32[]{:S(2)}, u32[]{:S(2)}) collective-permute-start(bf16[8,4096]{1,0:T(8,128)(2,1)S(1)} %get-tuple-element.57), channel_id=1, source_target_pairs={{0,8},{1,9},{2,10},{3,11},{4,12},{5,13},{6,14},{7,15},{8,0},{9,1},... | collective-permute-start | bytes 196616 | tf_op jit(solution)/shard_map/ppermute | solution.py:34
  35.3 1.6 %collective-permute-start.12 = (bf16[8,4096]{1,0:T(8,128)(2,1)S(1)}, bf16[8,4096]{1,0:T(8,128)(2,1)S(1)}, u32[]{:S(2)}, u32[]{:S(2)}) collective-permute-start(bf16[8,4096]{1,0:T(8,128)(2,1)S(1)} %get-tuple-element.58), channel_id=1, source_target_pairs={{0,12},{1,13},{2,14},{3,15},{4,8},{5,9},{6,10},{7,11},{8,4},{9,5},... | collective-permute-start | bytes 196616 | tf_op jit(solution)/shard_map/ppermute | solution.py:34
  36.8 0.2 collective-permute-done.9
  37.1 1.1 %collective-permute-start.13 = (bf16[8,4096]{1,0:T(8,128)(2,1)S(1)}, bf16[8,4096]{1,0:T(8,128)(2,1)S(1)}, u32[]{:S(2)}, u32[]{:S(2)}) collective-permute-start(bf16[8,4096]{1,0:T(8,128)(2,1)S(1)} %add_convert_fusion.2), channel_id=1, source_target_pairs={{0,4},{1,5},{2,6},{3,7},{4,0},{5,1},{6,2},{7,3},{8,12},{9,13},{10,... | collective-permute-start | bytes 196616 | tf_op jit(solution)/shard_map/ppermute | solution.py:34
  38.2 2.7 %collective-permute-done.11 = bf16[8,4096]{1,0:T(8,128)(2,1)S(1)} collective-permute-done((bf16[8,4096]{1,0:T(8,128)(2,1)S(1)}, bf16[8,4096]{1,0:T(8,128)(2,1)S(1)}, u32[]{:S(2)}, u32[]{:S(2)}) %collective-permute-start.11) | collective-permute-done | bytes 65568 | tf_op jit(solution)/shard_map/ppermute | solution.py:34
  40.9 0.6 collective-permute-done.12
  41.5 0.6 collective-permute-done.13
  42.1 0.1 constant_dynamic-update-slice_fusion.9
  42.2 2.4 %collective-permute-start.16 = (bf16[8,4096]{1,0:T(8,128)(2,1)S(1)}, bf16[8,4096]{1,0:T(8,128)(2,1)S(1)}, u32[]{:S(2)}, u32[]{:S(2)}) collective-permute-start(bf16[8,4096]{1,0:T(8,128)(2,1)S(1)} %get-tuple-element.54), channel_id=1, source_target_pairs={{0,12},{1,13},{2,14},{3,15},{4,8},{5,9},{6,10},{7,11},{8,4},{9,5},... | collective-permute-start | bytes 196616 | tf_op jit(solution)/shard_map/ppermute | solution.py:34
  44.5 0.0 collective-permute-start.15
  44.5 2.1 %collective-permute-start.14 = (bf16[8,4096]{1,0:T(8,128)(2,1)S(1)}, bf16[8,4096]{1,0:T(8,128)(2,1)S(1)}, u32[]{:S(2)}, u32[]{:S(2)}) collective-permute-start(bf16[8,4096]{1,0:T(8,128)(2,1)S(1)} %get-tuple-element.54), channel_id=1, source_target_pairs={{0,4},{1,5},{2,6},{3,7},{4,0},{5,1},{6,2},{7,3},{8,12},{9,13},{10,... | collective-permute-start | bytes 196616 | tf_op jit(solution)/shard_map/ppermute | solution.py:34
  46.6 0.5 turn.3
  47.1 0.9 %collective-permute-start.17 = (bf16[8,4096]{1,0:T(8,128)(2,1)S(1)}, bf16[8,4096]{1,0:T(8,128)(2,1)S(1)}, u32[]{:S(2)}, u32[]{:S(2)}) collective-permute-start(bf16[8,4096]{1,0:T(8,128)(2,1)S(1)} %get-tuple-element.54), channel_id=1, source_target_pairs={{0,2},{1,3},{2,0},{3,1},{4,6},{5,7},{6,4},{7,5},{8,10},{9,11},{10,... | collective-permute-start | bytes 196616 | tf_op jit(solution)/shard_map/ppermute | solution.py:34
  48.0 0.8 %collective-permute-done.16 = bf16[8,4096]{1,0:T(8,128)(2,1)S(1)} collective-permute-done((bf16[8,4096]{1,0:T(8,128)(2,1)S(1)}, bf16[8,4096]{1,0:T(8,128)(2,1)S(1)}, u32[]{:S(2)}, u32[]{:S(2)}) %collective-permute-start.16) | collective-permute-done | bytes 65568 | tf_op jit(solution)/shard_map/ppermute | solution.py:34
  48.8 1.5 %collective-permute-done.15 = bf16[8,4096]{1,0:T(8,128)(2,1)S(1)} collective-permute-done((bf16[8,4096]{1,0:T(8,128)(2,1)S(1)}, bf16[8,4096]{1,0:T(8,128)(2,1)S(1)}, u32[]{:S(2)}, u32[]{:S(2)}) %collective-permute-start.15) | collective-permute-done | bytes 65568 | tf_op jit(solution)/shard_map/ppermute | solution.py:34
  50.3 0.0 collective-permute-done.14
  50.4 1.4 %collective-permute-start.19 = (bf16[16,4096]{1,0:T(8,128)(2,1)S(1)}, bf16[16,4096]{1,0:T(8,128)(2,1)S(1)}, u32[]{:S(2)}, u32[]{:S(2)}) collective-permute-start(bf16[16,4096]{1,0:T(8,128)(2,1)S(1)} %pad_maximum_fusion.2), channel_id=1, source_target_pairs={{0,2},{1,3},{2,0},{3,1},{4,6},{5,7},{6,4},{7,5},{8,10},{9,11},{10,... | collective-permute-start | bytes 393224 | tf_op jit(solution)/shard_map/ppermute | solution.py:34
  51.8 0.7 collective-permute-start.18
  52.5 0.0 collective-permute-done.17
  52.5 0.1 collective-permute-start.20
  52.6 3.8 %collective-permute-done.18 = bf16[8,4096]{1,0:T(8,128)(2,1)S(1)} collective-permute-done((bf16[8,4096]{1,0:T(8,128)(2,1)S(1)}, bf16[8,4096]{1,0:T(8,128)(2,1)S(1)}, u32[]{:S(2)}, u32[]{:S(2)}) %collective-permute-start.18) | collective-permute-done | bytes 65568 | tf_op jit(solution)/shard_map/ppermute | solution.py:34
  56.4 0.0 collective-permute-done.19
  56.4 0.1 collective-permute-start.21
  56.5 1.4 %collective-permute-done.21.refs_3_ = bf16[24,4096]{1,0:T(8,128)(2,1)S(1)} collective-permute-done((bf16[24,4096]{1,0:T(8,128)(2,1)S(1)}, bf16[24,4096]{1,0:T(8,128)(2,1)S(1)}, u32[]{:S(2)}, u32[]{:S(2)}) %collective-permute-start.21) | collective-permute-done | bytes 196640 | tf_op jit(solution)/shard_map/ppermute | solution.py:34
  57.9 0.0 collective-permute-done.20.refs_2_
  57.9 9.7 %backward.1 = (bf16[2,2048,1024]{2,1,0:T(8,128)(2,1)}, f32[2,1024]{1,0:T(2,128)}, bf16[3,1024,2048]{2,1,0:T(8,128)(2,1)}) custom-call(bf16[40,4096]{1,0:T(8,128)(2,1)S(1)} %constant_dynamic-update-slice_fusion.5.refs_0_, bf16[24,4096]{1,0:T(8,128)(2,1)S(1)} %constant_dynamic-update-slice_fusion.10.refs_1_, ...), custom_call_target="tpu_custom_call" | custom-call | flops 8053063680 | tf_op jit(solution)/shard_map/backward/pallas_call | solution.py:318
  (18 shorter events, 0.2 us)
Async XLA Ops:
  1.8 12.6 %collective-permute-start.3 = (bf16[8,4096]{1,0:T(8,128)(2,1)S(1)}, bf16[8,4096]{1,0:T(8,128)(2,1)S(1)}, u32[]{:S(2)}, u32[]{:S(2)}) collective-permute-start(bf16[8,4096]{1,0:T(8,128)(2,1)S(1)} %get-tuple-element.28), channel_id=1, source_target_pairs={{0,2},{1,3},{2,0},{3,1},{4,6},{5,7},{6,4},{7,5},{8,10},{9,11},{10,... | collective-permute-start | bytes 196616 | tf_op jit(solution)/shard_map/ppermute | solution.py:34
  4.9 7.9 %collective-permute-start.2 = (bf16[8,4096]{1,0:T(8,128)(2,1)S(1)}, bf16[8,4096]{1,0:T(8,128)(2,1)S(1)}, u32[]{:S(2)}, u32[]{:S(2)}) collective-permute-start(bf16[8,4096]{1,0:T(8,128)(2,1)S(1)} %get-tuple-element.28), channel_id=1, source_target_pairs={{0,12},{1,13},{2,14},{3,15},{4,8},{5,9},{6,10},{7,11},{8,4},{9,5},... | collective-permute-start | bytes 196616 | tf_op jit(solution)/shard_map/ppermute | solution.py:34
  8.5 5.4 %collective-permute-start.1 = (bf16[8,4096]{1,0:T(8,128)(2,1)S(1)}, bf16[8,4096]{1,0:T(8,128)(2,1)S(1)}, u32[]{:S(2)}, u32[]{:S(2)}) collective-permute-start(bf16[8,4096]{1,0:T(8,128)(2,1)S(1)} %get-tuple-element.28), channel_id=1, source_target_pairs={{0,8},{1,9},{2,10},{3,11},{4,12},{5,13},{6,14},{7,15},{8,0},{9,1},... | collective-permute-start | bytes 196616 | tf_op jit(solution)/shard_map/ppermute | solution.py:34
  8.5 5.4 %collective-permute-start = (bf16[8,4096]{1,0:T(8,128)(2,1)S(1)}, bf16[8,4096]{1,0:T(8,128)(2,1)S(1)}, u32[]{:S(2)}, u32[]{:S(2)}) collective-permute-start(bf16[8,4096]{1,0:T(8,128)(2,1)S(1)} %get-tuple-element.28), channel_id=1, source_target_pairs={{0,4},{1,5},{2,6},{3,7},{4,0},{5,1},{6,2},{7,3},{8,12},{9,13},{10,... | collective-permute-start | bytes 196616 | tf_op jit(solution)/shard_map/ppermute | solution.py:34
  14.0 7.0 %collective-permute-start.5 = (bf16[16,4096]{1,0:T(8,128)(2,1)S(1)}, bf16[16,4096]{1,0:T(8,128)(2,1)S(1)}, u32[]{:S(2)}, u32[]{:S(2)}) collective-permute-start(bf16[16,4096]{1,0:T(8,128)(2,1)S(1)} %pad_maximum_fusion.1), channel_id=1, source_target_pairs={{0,2},{1,3},{2,0},{3,1},{4,6},{5,7},{6,4},{7,5},{8,10},{9,11},{10,... | collective-permute-start | bytes 393224 | tf_op jit(solution)/shard_map/ppermute | solution.py:34
  14.5 8.0 %copy-start = (f32[2,1024]{1,0:T(2,128)S(1)}, f32[2,1024]{1,0:T(2,128)}, u32[]{:S(2)}) copy-start(f32[2,1024]{1,0:T(2,128)} %refs_5_.1) | copy-start | bytes 24580
  14.5 8.0 %collective-permute-start.6 = (bf16[40,4096]{1,0:T(8,128)(2,1)S(1)}, bf16[40,4096]{1,0:T(8,128)(2,1)S(1)}, u32[]{:S(2)}, u32[]{:S(2)}) collective-permute-start(bf16[40,4096]{1,0:T(8,128)(2,1)S(1)} %constant_dynamic-update-slice_fusion.refs_0_), channel_id=1, source_target_pairs={{0,1},{1,0},{2,3},{3,2},{4,5},{5,4},{6,7},{7,6},{8,9},{9,8},{10,11... | collective-permute-start | bytes 983048 | tf_op jit(solution)/shard_map/ppermute | solution.py:34
  14.6 6.4 %collective-permute-start.4 = (bf16[8,4096]{1,0:T(8,128)(2,1)S(1)}, bf16[8,4096]{1,0:T(8,128)(2,1)S(1)}, u32[]{:S(2)}, u32[]{:S(2)}) collective-permute-start(bf16[8,4096]{1,0:T(8,128)(2,1)S(1)} %collective-permute-done), channel_id=1, source_target_pairs={{0,2},{1,3},{2,0},{3,1},{4,6},{5,7},{6,4},{7,5},{8,10},{9,11},{10,... | collective-permute-start | bytes 196616 | tf_op jit(solution)/shard_map/ppermute | solution.py:34
  21.0 1.5 %collective-permute-start.7 = (bf16[24,4096]{1,0:T(8,128)(2,1)S(1)}, bf16[24,4096]{1,0:T(8,128)(2,1)S(1)}, u32[]{:S(2)}, u32[]{:S(2)}) collective-permute-start(bf16[24,4096]{1,0:T(8,128)(2,1)S(1)} %pad_maximum_fusion.refs_1_), channel_id=1, source_target_pairs={{0,1},{1,0},{2,3},{3,2},{4,5},{5,4},{6,7},{7,6},{8,9},{9,8},{10,11... | collective-permute-start | bytes 589832 | tf_op jit(solution)/shard_map/ppermute | solution.py:34
  25.5 2.0 %collective-permute-start.8 = (bf16[64,4096]{1,0:T(8,128)(2,1)S(1)}, bf16[64,4096]{1,0:T(8,128)(2,1)S(1)}, u32[]{:S(2)}, u32[]{:S(2)}) collective-permute-start(bf16[64,4096]{1,0:T(8,128)(2,1)S(1)} %get-tuple-element.38), channel_id=1, source_target_pairs={{0,1},{1,0},{2,3},{3,2},{4,5},{5,4},{6,7},{7,6},{8,9},{9,8},{10,11... | collective-permute-start | bytes 1572872 | tf_op jit(solution)/shard_map/ppermute | solution.py:34
  27.6 5.8 %collective-permute-start.10 = (bf16[16,4096]{1,0:T(8,128)(2,1)S(1)}, bf16[16,4096]{1,0:T(8,128)(2,1)S(1)}, u32[]{:S(2)}, u32[]{:S(2)}) collective-permute-start(bf16[16,4096]{1,0:T(8,128)(2,1)S(1)} %get-tuple-element.55), channel_id=1, source_target_pairs={{0,2},{1,3},{2,0},{3,1},{4,6},{5,7},{6,4},{7,5},{8,10},{9,11},{10,... | collective-permute-start | bytes 393224 | tf_op jit(solution)/shard_map/ppermute | solution.py:34
  31.7 5.3 %collective-permute-start.9 = (bf16[16,4096]{1,0:T(8,128)(2,1)S(1)}, bf16[16,4096]{1,0:T(8,128)(2,1)S(1)}, u32[]{:S(2)}, u32[]{:S(2)}) collective-permute-start(bf16[16,4096]{1,0:T(8,128)(2,1)S(1)} %get-tuple-element.56), channel_id=1, source_target_pairs={{0,2},{1,3},{2,0},{3,1},{4,6},{5,7},{6,4},{7,5},{8,10},{9,11},{10,... | collective-permute-start | bytes 393224 | tf_op jit(solution)/shard_map/ppermute | solution.py:34
  33.4 7.4 %collective-permute-start.11 = (bf16[8,4096]{1,0:T(8,128)(2,1)S(1)}, bf16[8,4096]{1,0:T(8,128)(2,1)S(1)}, u32[]{:S(2)}, u32[]{:S(2)}) collective-permute-start(bf16[8,4096]{1,0:T(8,128)(2,1)S(1)} %get-tuple-element.57), channel_id=1, source_target_pairs={{0,8},{1,9},{2,10},{3,11},{4,12},{5,13},{6,14},{7,15},{8,0},{9,1},... | collective-permute-start | bytes 196616 | tf_op jit(solution)/shard_map/ppermute | solution.py:34
  35.3 6.3 %collective-permute-start.12 = (bf16[8,4096]{1,0:T(8,128)(2,1)S(1)}, bf16[8,4096]{1,0:T(8,128)(2,1)S(1)}, u32[]{:S(2)}, u32[]{:S(2)}) collective-permute-start(bf16[8,4096]{1,0:T(8,128)(2,1)S(1)} %get-tuple-element.58), channel_id=1, source_target_pairs={{0,12},{1,13},{2,14},{3,15},{4,8},{5,9},{6,10},{7,11},{8,4},{9,5},... | collective-permute-start | bytes 196616 | tf_op jit(solution)/shard_map/ppermute | solution.py:34
  37.1 5.1 %collective-permute-start.13 = (bf16[8,4096]{1,0:T(8,128)(2,1)S(1)}, bf16[8,4096]{1,0:T(8,128)(2,1)S(1)}, u32[]{:S(2)}, u32[]{:S(2)}) collective-permute-start(bf16[8,4096]{1,0:T(8,128)(2,1)S(1)} %add_convert_fusion.2), channel_id=1, source_target_pairs={{0,4},{1,5},{2,6},{3,7},{4,0},{5,1},{6,2},{7,3},{8,12},{9,13},{10,... | collective-permute-start | bytes 196616 | tf_op jit(solution)/shard_map/ppermute | solution.py:34
  42.2 6.6 %collective-permute-start.16 = (bf16[8,4096]{1,0:T(8,128)(2,1)S(1)}, bf16[8,4096]{1,0:T(8,128)(2,1)S(1)}, u32[]{:S(2)}, u32[]{:S(2)}) collective-permute-start(bf16[8,4096]{1,0:T(8,128)(2,1)S(1)} %get-tuple-element.54), channel_id=1, source_target_pairs={{0,12},{1,13},{2,14},{3,15},{4,8},{5,9},{6,10},{7,11},{8,4},{9,5},... | collective-permute-start | bytes 196616 | tf_op jit(solution)/shard_map/ppermute | solution.py:34
  44.5 5.8 %collective-permute-start.15 = (bf16[8,4096]{1,0:T(8,128)(2,1)S(1)}, bf16[8,4096]{1,0:T(8,128)(2,1)S(1)}, u32[]{:S(2)}, u32[]{:S(2)}) collective-permute-start(bf16[8,4096]{1,0:T(8,128)(2,1)S(1)} %get-tuple-element.54), channel_id=1, source_target_pairs={{0,8},{1,9},{2,10},{3,11},{4,12},{5,13},{6,14},{7,15},{8,0},{9,1},... | collective-permute-start | bytes 196616 | tf_op jit(solution)/shard_map/ppermute | solution.py:34
  44.5 5.8 %collective-permute-start.14 = (bf16[8,4096]{1,0:T(8,128)(2,1)S(1)}, bf16[8,4096]{1,0:T(8,128)(2,1)S(1)}, u32[]{:S(2)}, u32[]{:S(2)}) collective-permute-start(bf16[8,4096]{1,0:T(8,128)(2,1)S(1)} %get-tuple-element.54), channel_id=1, source_target_pairs={{0,4},{1,5},{2,6},{3,7},{4,0},{5,1},{6,2},{7,3},{8,12},{9,13},{10,... | collective-permute-start | bytes 196616 | tf_op jit(solution)/shard_map/ppermute | solution.py:34
  47.1 5.4 %collective-permute-start.17 = (bf16[8,4096]{1,0:T(8,128)(2,1)S(1)}, bf16[8,4096]{1,0:T(8,128)(2,1)S(1)}, u32[]{:S(2)}, u32[]{:S(2)}) collective-permute-start(bf16[8,4096]{1,0:T(8,128)(2,1)S(1)} %get-tuple-element.54), channel_id=1, source_target_pairs={{0,2},{1,3},{2,0},{3,1},{4,6},{5,7},{6,4},{7,5},{8,10},{9,11},{10,... | collective-permute-start | bytes 196616 | tf_op jit(solution)/shard_map/ppermute | solution.py:34
  50.4 6.0 %collective-permute-start.19 = (bf16[16,4096]{1,0:T(8,128)(2,1)S(1)}, bf16[16,4096]{1,0:T(8,128)(2,1)S(1)}, u32[]{:S(2)}, u32[]{:S(2)}) collective-permute-start(bf16[16,4096]{1,0:T(8,128)(2,1)S(1)} %pad_maximum_fusion.2), channel_id=1, source_target_pairs={{0,2},{1,3},{2,0},{3,1},{4,6},{5,7},{6,4},{7,5},{8,10},{9,11},{10,... | collective-permute-start | bytes 393224 | tf_op jit(solution)/shard_map/ppermute | solution.py:34
  51.8 4.6 %collective-permute-start.18 = (bf16[8,4096]{1,0:T(8,128)(2,1)S(1)}, bf16[8,4096]{1,0:T(8,128)(2,1)S(1)}, u32[]{:S(2)}, u32[]{:S(2)}) collective-permute-start(bf16[8,4096]{1,0:T(8,128)(2,1)S(1)} %collective-permute-done.14), channel_id=1, source_target_pairs={{0,2},{1,3},{2,0},{3,1},{4,6},{5,7},{6,4},{7,5},{8,10},{9,11},{10,... | collective-permute-start | bytes 196616 | tf_op jit(solution)/shard_map/ppermute | solution.py:34
  52.5 5.5 %collective-permute-start.20 = (bf16[40,4096]{1,0:T(8,128)(2,1)S(1)}, bf16[40,4096]{1,0:T(8,128)(2,1)S(1)}, u32[]{:S(2)}, u32[]{:S(2)}) collective-permute-start(bf16[40,4096]{1,0:T(8,128)(2,1)S(1)} %constant_dynamic-update-slice_fusion.5.refs_0_), channel_id=1, source_target_pairs={{0,1},{1,0},{2,3},{3,2},{4,5},{5,4},{6,7},{7,6},{8,9},{9,8},{10,11... | collective-permute-start | bytes 983048 | tf_op jit(solution)/shard_map/ppermute | solution.py:34
  56.4 1.5 %collective-permute-start.21 = (bf16[24,4096]{1,0:T(8,128)(2,1)S(1)}, bf16[24,4096]{1,0:T(8,128)(2,1)S(1)}, u32[]{:S(2)}, u32[]{:S(2)}) collective-permute-start(bf16[24,4096]{1,0:T(8,128)(2,1)S(1)} %constant_dynamic-update-slice_fusion.10.refs_1_), channel_id=1, source_target_pairs={{0,1},{1,0},{2,3},{3,2},{4,5},{5,4},{6,7},{7,6},{8,9},{9,8},{10,11... | collective-permute-start | bytes 589832 | tf_op jit(solution)/shard_map/ppermute | solution.py:34
